TPU v7x, 256 devices: a whole 4x4x8 slice. The times are simulated.
256 devices in a mesh: gx: 8 (over z), gy: 8 (over y, core), gz: 4 (over x).
Axes of the slice: x: 4, y: 4, z: 8, core: 2. Of those that a mesh axis runs over, the one named last changes fastest.
Arguments:
- acts: bfloat16 [150528, 2048], P(('gx', 'gy', 'gz')), may hold values from -24 to 24
- saved_hidden: bfloat16 [150528, 512], P(('gx', 'gy', 'gz')), as said below
- grad_out: bfloat16 [150528, 2048], P(('gx', 'gy', 'gz')), may hold values from -24 to 24
- master_reduce: float32 [2048, 512], P(('gx', 'gy', 'gz')), may hold values from -60 to 60
- master_expand: float32 [2048, 512], P(('gx', 'gy', 'gz')), may hold values from -60 to 60
- velocity_reduce: float32 [2048, 512], P(('gx', 'gy', 'gz')), may hold values from -6 to 6
- velocity_expand: float32 [2048, 512], P(('gx', 'gy', 'gz')), may hold values from -6 to 6
Outputs:
- grad_in: bfloat16 [150528, 2048], P(('gx', 'gy', 'gz'))
- new_master_reduce: float32 [2048, 512], P(('gx', 'gy', 'gz'))
- new_master_expand: float32 [2048, 512], P(('gx', 'gy', 'gz'))
- new_velocity_reduce: float32 [2048, 512], P(('gx', 'gy', 'gz'))
- new_velocity_expand: float32 [2048, 512], P(('gx', 'gy', 'gz'))
- work_reduce: bfloat16 [2048, 512], replicated
- work_expand: bfloat16 [2048, 512], replicated
Inputs may be any that keep to these rules, and one draw needn't show every extreme that they name: `saved_hidden`: values are zero or positive, zero at about half of the entries.
All inputs are finite; a program needn't handle non-finite values.
Results may differ from a plain program's by a relative error of at most 0.0064.
Values may be sent and summed in bfloat16 or wider, within the bound.
No kernel may reach another device: no remote copies, remote signals or barrier semaphores. Data moves between devices by JAX's collectives and lax.ppermute only.
A program may use at most 64 MiB of HBM per device.

v0:
```python
import jax
import jax.numpy as jnp
from jax import lax
from jax.sharding import Mesh
from jax.sharding import PartitionSpec as P

GX_GY_GZ = ("gx", "gy_0", "gy_1", "gz")


def from_everyone(array, axis):
    peers = lax.axis_size(axis)
    return lax.all_to_all(
        jnp.broadcast_to(array[None], (peers, *array.shape)), axis, 0, 0, tiled=True
    )


def laid_out(parts, dim):
    parts = jnp.moveaxis(parts, 0, dim)
    lengths = parts.shape
    return parts.reshape(*lengths[:dim], lengths[dim] * lengths[dim + 1], *lengths[dim + 2 :])


def whole_of(array, axes, dim):
    far, near = axes
    parts = from_everyone(from_everyone(array, far), near)
    return laid_out(parts.swapaxes(0, 1).reshape(-1, *array.shape), dim)


def split_up(array, dim, peers):
    lengths = array.shape
    parts = array.reshape(*lengths[:dim], peers, lengths[dim] // peers, *lengths[dim + 1 :])
    return jnp.moveaxis(parts, dim, 0)


def summed_on_arrival(array, axis, dim):
    peers = lax.axis_size(axis)
    parts = lax.all_to_all(split_up(array, dim, peers), axis, 0, 0, tiled=True)
    return jnp.sum(parts.astype(jnp.float32), axis=0)


def summed_rows(array, axes, dim):
    far, near = axes
    parts = split_up(array, dim, lax.axis_size(far))
    nearer = summed_on_arrival(parts, near, dim + 1)
    arrived = lax.all_to_all(
        nearer.astype(jnp.bfloat16), far, split_axis=0, concat_axis=0, tiled=True
    )
    return arrived.astype(jnp.float32).sum(axis=0)


def taken_together(array, axis):
    return from_everyone(array, axis).sum(axis=0)


def one_axis_at_a_time(array, axes):
    far, near = axes
    return taken_together(taken_together(array, near), far)


def packed_total(arrays, axis):
    flat, at, outs = (jnp.concatenate([a.reshape(-1) for a in arrays]), 0, [])
    so_far = one_axis_at_a_time(flat, axis)
    for a in arrays:
        outs.append(so_far[at : at + a.size].reshape(a.shape))
        at += a.size
    return tuple(outs)


def sent_together(arrays, axis, dim, along):
    ends, at = ([], 0)
    for a in arrays[:-1]:
        at += a.shape[along]
        ends.append(at)
    both = jnp.concatenate(arrays, axis=along)
    return tuple(jnp.split(lax.all_gather(both, axis, axis=dim, tiled=True), ends, axis=along))


def layer_update(master, grads, velocity, wsquare, gsquare):
    wnorm = jnp.sqrt(wsquare)
    gnorm = jnp.sqrt(gsquare)
    trust = wnorm / (gnorm + 5e-05 * wnorm)
    new_velocity = 0.9 * velocity + trust * (grads + 5e-05 * master)
    new_master = master - 0.1 * new_velocity
    return (new_master, new_velocity)


def shards(
    acts, saved_hidden, grad_out, master_reduce, master_expand, velocity_reduce, velocity_expand
):
    channels = grad_out.shape[1]
    middle = saved_hidden.shape[1]
    inv_c = 1.0 / float(channels) ** 0.5
    inv_m = 1.0 / float(middle) ** 0.5
    cur_reduce = master_reduce.astype(jnp.bfloat16)
    cur_expand = master_expand.astype(jnp.bfloat16)
    columns = grad_out
    summed = jnp.dot(
        columns,
        whole_of(cur_expand, (("gx", "gy_0"), ("gy_1", "gz")), 0),
        preferred_element_type=jnp.float32,
    )
    grad_hidden = jnp.where(saved_hidden > 0, summed * inv_m, 0.0).astype(jnp.bfloat16)
    columns = grad_out
    g_expand = summed_rows(
        (
            lax.dot_general(
                columns, saved_hidden, (((0,), (0,)), ((), ())), preferred_element_type=jnp.float32
            )
            * inv_m
        ).astype(jnp.bfloat16),
        (("gx", "gy_0"), ("gy_1", "gz")),
        0,
    )
    expand_parts = (jnp.sum(master_expand * master_expand), jnp.sum(g_expand * g_expand))
    columns = acts
    g_reduce = summed_rows(
        (
            lax.dot_general(
                columns, grad_hidden, (((0,), (0,)), ((), ())), preferred_element_type=jnp.float32
            )
            * inv_c
        ).astype(jnp.bfloat16),
        (("gx", "gy_0"), ("gy_1", "gz")),
        0,
    )
    back = lax.dot_general(
        grad_hidden,
        whole_of(cur_reduce, (("gx", "gy_0"), ("gy_1", "gz")), 0),
        (((1,), (1,)), ((), ())),
        preferred_element_type=jnp.float32,
    )
    grad_in = (grad_out.astype(jnp.float32) + back * inv_c).astype(jnp.bfloat16)
    reduce_parts = (jnp.sum(master_reduce * master_reduce), jnp.sum(g_reduce * g_reduce))
    totals = packed_total(
        (expand_parts[0], expand_parts[1], reduce_parts[0], reduce_parts[1]),
        (("gx", "gy_0"), ("gy_1", "gz")),
    )
    expand_stats = (totals[0], totals[1])
    reduce_stats = (totals[2], totals[3])
    new_mr, new_vr = layer_update(
        master_reduce, g_reduce, velocity_reduce, reduce_stats[0], reduce_stats[1]
    )
    new_me, new_ve = layer_update(
        master_expand, g_expand, velocity_expand, expand_stats[0], expand_stats[1]
    )
    work_reduce, work_expand = sent_together(
        (new_mr.astype(jnp.bfloat16), new_me.astype(jnp.bfloat16)), GX_GY_GZ, 0, 1
    )
    return (grad_in, new_mr, new_me, new_vr, new_ve, work_reduce, work_expand)


def solution(mesh):
    finer = Mesh(
        mesh.devices.reshape(mesh.shape["gx"], 4, 2, mesh.shape["gz"]), ("gx", "gy_0", "gy_1", "gz")
    )
    return jax.shard_map(
        shards,
        mesh=finer,
        in_specs=(
            P(GX_GY_GZ, None),
            P(GX_GY_GZ, None),
            P(GX_GY_GZ, None),
            P(GX_GY_GZ, None),
            P(GX_GY_GZ, None),
            P(GX_GY_GZ, None),
            P(GX_GY_GZ, None),
        ),
        out_specs=(
            P(GX_GY_GZ, None),
            P(GX_GY_GZ, None),
            P(GX_GY_GZ, None),
            P(GX_GY_GZ, None),
            P(GX_GY_GZ, None),
            P(),
            P(),
        ),
        check_vma=False,
    )
```

profile of v0, /device:TPU:1, one launch (start us, length us, event | category | flops | bytes accessed | tf_op | source)
XLA Modules:
  0.0 311.4 jit_solution(2188358932130534118)
XLA Ops:
  7.2 0.0 copy-start
  7.2 1.5 multiply_reduce_fusion.3
  8.7 23.1 %all_to_all.52 = bf16[32,8,512]{2,1,0:T(8,128)(2,1)S(1)} all-to-all(bf16[32,8,512]{2,1,0:T(8,128)(2,1)S(1)} %broadcast_in_dim.16), channel_id=1, replica_groups=mesh['gx'=8,'gy_0'=4,'gy_1'=2,'gz'=4] {'gx','gy_0'}, dimensions={0} | all-to-all | bytes 524288 | tf_op jit(solution)/shard_map/all_to_all | solution.py:12
  31.8 1.5 broadcast_in_dim.17
  33.3 0.0 copy-start.7
  33.3 6.9 %all-to-all-start.1 = ((bf16[8,32,8,512]{3,2,1,0:T(8,128)(2,1)}), bf16[8,32,8,512]{3,2,1,0:T(8,128)(2,1)}, u32[]{:S(2)}, u32[]{:S(2)}) async-start(bf16[8,32,8,512]{3,2,1,0:T(8,128)(2,1)} %broadcast_in_dim.17), calls=%async_computation.1 | async-start | bytes 4194304 | tf_op jit(solution)/shard_map/all_to_all | solution.py:12
  40.2 0.0 copy-done.7
  40.2 3.5 %multiply_convert_fusion.1 = bf16[2048,512]{1,0:T(8,128)(2,1)S(1)} fusion(bf16[588,2048]{1,0:T(8,128)(2,1)} %param.9, bf16[588,512]{1,0:T(8,128)(2,1)S(1)} %copy-done.7), kind=kOutput, calls=%fused_computation.2 | convolution fusion | flops 1235222528 | bytes 5107712 | tf_op jit(solution)/shard_map/dot_general | solution.py:106
  43.7 1.5 copy.39
  45.3 21.2 %all-to-all-done.1 = bf16[8,32,8,512]{3,2,1,0:T(8,128)(2,1)} async-done(((bf16[8,32,8,512]{3,2,1,0:T(8,128)(2,1)}), bf16[8,32,8,512]{3,2,1,0:T(8,128)(2,1)}, u32[]{:S(2)}, u32[]{:S(2)}) %all-to-all-start.1) | async-done | bytes 2097184 | tf_op jit(solution)/shard_map/all_to_all | solution.py:12
  66.5 4.5 %all-to-all-start.4 = ((bf16[8,32,8,512]{3,2,1,0:T(8,128)(2,1)}), bf16[8,32,8,512]{3,2,1,0:T(8,128)(2,1)}, u32[]{:S(2)}, u32[]{:S(2)}) async-start(bf16[8,32,8,512]{3,2,1,0:T(8,128)(2,1)} %bitcast.31), calls=%async_computation.4 | async-start | bytes 4194304 | tf_op jit(solution)/shard_map/all_to_all | solution.py:37
  71.0 0.0 copy-start.5
  71.0 2.0 copy.25
  73.1 0.3 copy-done.5
  73.4 1.4 fusion.2
  74.8 0.0 copy-start.8
  74.8 0.8 copy-done.8
  75.6 0.0 copy-done
  75.6 3.1 %fusion = bf16[2048,512]{0,1:T(8,128)(2,1)} fusion(bf16[588,512]{1,0:T(8,128)(2,1)S(1)} %fusion.2, bf16[588,2048]{1,0:T(8,128)(2,1)S(1)} %copy-done), kind=kOutput, calls=%fused_computation.3 | convolution fusion | flops 1235222528 | bytes 5107712 | tf_op jit(solution)/shard_map/dot_general | solution.py:118
  78.8 3.9 %copy.28 = bf16[2048,512]{1,0:T(8,128)(2,1)} copy(bf16[2048,512]{0,1:T(8,128)(2,1)} %fusion) | data formatting | bytes 4194304 | tf_op jit(solution)/shard_map/convert_element_type | solution.py:122
  82.7 3.1 copy.29
  85.8 11.5 %all-to-all-done.4 = bf16[8,32,8,512]{3,2,1,0:T(8,128)(2,1)} async-done(((bf16[8,32,8,512]{3,2,1,0:T(8,128)(2,1)}), bf16[8,32,8,512]{3,2,1,0:T(8,128)(2,1)}, u32[]{:S(2)}, u32[]{:S(2)}) %all-to-all-start.4) | async-done | bytes 2097184 | tf_op jit(solution)/shard_map/all_to_all | solution.py:37
  97.4 4.6 %all-to-all-start.6 = ((bf16[8,32,8,512]{3,2,1,0:T(8,128)(2,1)}), bf16[8,32,8,512]{3,2,1,0:T(8,128)(2,1)}, u32[]{:S(2)}, u32[]{:S(2)}) async-start(bf16[8,32,8,512]{3,2,1,0:T(8,128)(2,1)} %copy.29), calls=%async_computation.6 | async-start | bytes 4194304 | tf_op jit(solution)/shard_map/all_to_all | solution.py:37
  101.9 2.7 reduce_sum.97
  104.6 0.0 copy-start.2
  104.6 0.0 copy-start.1
  104.6 0.0 copy-start.3
  104.6 0.0 copy-start.4
  104.6 23.6 %all-to-all-done.6 = bf16[8,32,8,512]{3,2,1,0:T(8,128)(2,1)} async-done(((bf16[8,32,8,512]{3,2,1,0:T(8,128)(2,1)}), bf16[8,32,8,512]{3,2,1,0:T(8,128)(2,1)}, u32[]{:S(2)}, u32[]{:S(2)}) %all-to-all-start.6) | async-done | bytes 2097184 | tf_op jit(solution)/shard_map/all_to_all | solution.py:37
  128.2 3.9 %all-to-all-start.5 = ((bf16[32,8,512]{2,1,0:T(8,128)(2,1)}), bf16[32,8,512]{2,1,0:T(8,128)(2,1)S(1)}, u32[]{:S(2)}, u32[]{:S(2)}) async-start(bf16[32,8,512]{2,1,0:T(8,128)(2,1)} %reduce_sum.97), calls=%async_computation.5 | async-start | bytes 524288 | tf_op jit(solution)/shard_map/all_to_all | solution.py:45
  132.1 2.7 reduce_sum.101
  134.8 9.1 %all-to-all-done.5 = bf16[32,8,512]{2,1,0:T(8,128)(2,1)S(1)} async-done(((bf16[32,8,512]{2,1,0:T(8,128)(2,1)}), bf16[32,8,512]{2,1,0:T(8,128)(2,1)S(1)}, u32[]{:S(2)}, u32[]{:S(2)}) %all-to-all-start.5) | async-done | bytes 262176 | tf_op jit(solution)/shard_map/all_to_all | solution.py:45
  143.8 4.4 %all-to-all-start.7 = ((bf16[32,8,512]{2,1,0:T(8,128)(2,1)}), bf16[32,8,512]{2,1,0:T(8,128)(2,1)S(1)}, u32[]{:S(2)}, u32[]{:S(2)}) async-start(bf16[32,8,512]{2,1,0:T(8,128)(2,1)} %reduce_sum.101), calls=%async_computation.7 | async-start | bytes 524288 | tf_op jit(solution)/shard_map/all_to_all | solution.py:45
  148.2 0.0 all-gather.2.cloned.1.call-start
  148.3 0.0 copy-done.2
  148.3 0.6 multiply_reduce_fusion.1
  148.9 0.6 multiply_reduce_fusion.2
  149.5 9.1 %all-to-all-done.7 = bf16[32,8,512]{2,1,0:T(8,128)(2,1)S(1)} async-done(((bf16[32,8,512]{2,1,0:T(8,128)(2,1)}), bf16[32,8,512]{2,1,0:T(8,128)(2,1)S(1)}, u32[]{:S(2)}, u32[]{:S(2)}) %all-to-all-start.7) | async-done | bytes 262176 | tf_op jit(solution)/shard_map/all_to_all | solution.py:45
  158.7 0.6 multiply_reduce_fusion
  159.3 2.7 pad_maximum_fusion.1
  162.0 10.5 %all_to_all.53 = f32[8,1,4]{2,1,0:T(1,128)S(1)} all-to-all(f32[8,1,4]{2,1,0:T(1,128)S(1)} %broadcast_in_dim.21), channel_id=1, replica_groups=mesh['gx'=8,'gy_0'=4,'gy_1'=2,'gz'=4] {'gy_1','gz'}, dimensions={0} | all-to-all | bytes 256 | tf_op jit(solution)/shard_map/all_to_all | solution.py:12
  172.5 11.9 %all_to_all.54 = f32[32,1,4]{2,1,0:T(1,128)S(1)} all-to-all(f32[32,1,4]{2,1,0:T(1,128)S(1)} %broadcast_in_dim.22), channel_id=1, replica_groups=mesh['gx'=8,'gy_0'=4,'gy_1'=2,'gz'=4] {'gx','gy_0'}, dimensions={0} | all-to-all | bytes 1024 | tf_op jit(solution)/shard_map/all_to_all | solution.py:12
  184.4 0.1 reduce_sum.105
  184.4 0.6 fusion.6
  187.9 0.0 copy-done.1
  187.9 0.0 copy-done.3
  187.9 0.6 fusion.4
  188.5 0.0 copy-done.4
  188.5 0.6 fusion.3
  189.1 0.6 pad_maximum_fusion
  189.7 0.0 all-gather.2.cloned.1.call-update
  189.8 13.6 %all_to_all.55 = bf16[32,8,512]{2,1,0:T(8,128)(2,1)S(1)} all-to-all(bf16[32,8,512]{2,1,0:T(8,128)(2,1)S(1)} %broadcast_in_dim.19), channel_id=1, replica_groups=mesh['gx'=8,'gy_0'=4,'gy_1'=2,'gz'=4] {'gx','gy_0'}, dimensions={0} | all-to-all | bytes 524288 | tf_op jit(solution)/shard_map/all_to_all | solution.py:12
  203.3 0.2 broadcast_in_dim.20
  203.5 32.2 %all_to_all.56 = bf16[8,32,8,512]{3,2,1,0:T(8,128)(2,1)S(1)} all-to-all(bf16[8,32,8,512]{3,2,1,0:T(8,128)(2,1)S(1)} %broadcast_in_dim.20), channel_id=1, replica_groups=mesh['gx'=8,'gy_0'=4,'gy_1'=2,'gz'=4] {'gy_1','gz'}, dimensions={0} | all-to-all | bytes 4194304 | tf_op jit(solution)/shard_map/all_to_all | solution.py:12
  235.8 0.0 copy-start.6
  235.8 0.0 copy-start.9
  235.8 0.3 copy.26
  236.0 1.4 copy-done.6
  237.4 0.1 copy-done.9
  237.6 2.9 add_convert_fusion
  240.4 59.6 %all-gather.2.cloned.1.call-done = bf16[2048,1024]{1,0:T(8,128)(2,1)} async-done(((bf16[8,1024]{1,0:T(8,128)(2,1)}), bf16[2048,1024]{1,0:T(8,128)(2,1)}) %all-gather.2.cloned.1.call-update) | async-done | bytes 4194320 | tf_op jit(solution)/shard_map/all_gather | solution.py:75
  300.1 4.5 %fusion.5 = (bf16[2048,512]{1,0:T(8,128)(2,1)}, bf16[2048,512]{1,0:T(8,128)(2,1)}) fusion(bf16[2048,1024]{1,0:T(8,128)(2,1)} %all-gather.2.cloned.1.call-done), kind=kLoop, calls=%fused_computation.22 | loop fusion | bytes 8388608 | tf_op jit(solution)/shard_map/split | solution.py:75
  (7 shorter events, 0.2 us)
Async XLA Ops:
  7.2 68.5 %copy-start = (bf16[588,2048]{1,0:T(8,128)(2,1)S(1)}, bf16[588,2048]{1,0:T(8,128)(2,1)}, u32[]{:S(2)}) copy-start(bf16[588,2048]{1,0:T(8,128)(2,1)} %param.7) | copy-start | bytes 7225348
  33.3 6.9 %copy-start.7 = (bf16[588,512]{1,0:T(8,128)(2,1)S(1)}, bf16[588,512]{1,0:T(8,128)(2,1)}, u32[]{:S(2)}) copy-start(bf16[588,512]{1,0:T(8,128)(2,1)} %param.8) | copy-start | bytes 1806340
  33.3 33.2 %all-to-all-start.1 = ((bf16[8,32,8,512]{3,2,1,0:T(8,128)(2,1)}), bf16[8,32,8,512]{3,2,1,0:T(8,128)(2,1)}, u32[]{:S(2)}, u32[]{:S(2)}) async-start(bf16[8,32,8,512]{3,2,1,0:T(8,128)(2,1)} %broadcast_in_dim.17), calls=%async_computation.1 | async-start | bytes 4194304 | tf_op jit(solution)/shard_map/all_to_all | solution.py:12
  66.5 30.8 %all-to-all-start.4 = ((bf16[8,32,8,512]{3,2,1,0:T(8,128)(2,1)}), bf16[8,32,8,512]{3,2,1,0:T(8,128)(2,1)}, u32[]{:S(2)}, u32[]{:S(2)}) async-start(bf16[8,32,8,512]{3,2,1,0:T(8,128)(2,1)} %bitcast.31), calls=%async_computation.4 | async-start | bytes 4194304 | tf_op jit(solution)/shard_map/all_to_all | solution.py:37
  71.0 2.3 copy-start.5
  74.8 0.8 copy-start.8
  97.4 30.9 %all-to-all-start.6 = ((bf16[8,32,8,512]{3,2,1,0:T(8,128)(2,1)}), bf16[8,32,8,512]{3,2,1,0:T(8,128)(2,1)}, u32[]{:S(2)}, u32[]{:S(2)}) async-start(bf16[8,32,8,512]{3,2,1,0:T(8,128)(2,1)} %copy.29), calls=%async_computation.6 | async-start | bytes 4194304 | tf_op jit(solution)/shard_map/all_to_all | solution.py:37
  104.6 43.7 %copy-start.2 = (f32[8,512]{1,0:T(8,128)S(1)}, f32[8,512]{1,0:T(8,128)}, u32[]{:S(2)}) copy-start(f32[8,512]{1,0:T(8,128)} %param.10) | copy-start | bytes 49156
  104.6 83.3 %copy-start.1 = (f32[8,512]{1,0:T(8,128)S(1)}, f32[8,512]{1,0:T(8,128)}, u32[]{:S(2)}) copy-start(f32[8,512]{1,0:T(8,128)} %param.11) | copy-start | bytes 49156
  104.6 83.3 %copy-start.3 = (f32[8,512]{1,0:T(8,128)S(1)}, f32[8,512]{1,0:T(8,128)}, u32[]{:S(2)}) copy-start(f32[8,512]{1,0:T(8,128)} %param.13) | copy-start | bytes 49156
  104.6 83.9 %copy-start.4 = (f32[8,512]{1,0:T(8,128)S(1)}, f32[8,512]{1,0:T(8,128)}, u32[]{:S(2)}) copy-start(f32[8,512]{1,0:T(8,128)} %param.12) | copy-start | bytes 49156
  128.2 15.6 %all-to-all-start.5 = ((bf16[32,8,512]{2,1,0:T(8,128)(2,1)}), bf16[32,8,512]{2,1,0:T(8,128)(2,1)S(1)}, u32[]{:S(2)}, u32[]{:S(2)}) async-start(bf16[32,8,512]{2,1,0:T(8,128)(2,1)} %reduce_sum.97), calls=%async_computation.5 | async-start | bytes 524288 | tf_op jit(solution)/shard_map/all_to_all | solution.py:45
  143.8 14.8 %all-to-all-start.7 = ((bf16[32,8,512]{2,1,0:T(8,128)(2,1)}), bf16[32,8,512]{2,1,0:T(8,128)(2,1)S(1)}, u32[]{:S(2)}, u32[]{:S(2)}) async-start(bf16[32,8,512]{2,1,0:T(8,128)(2,1)} %reduce_sum.101), calls=%async_computation.7 | async-start | bytes 524288 | tf_op jit(solution)/shard_map/all_to_all | solution.py:45
  148.2 151.9 %all-gather.2.cloned.1.call-start = ((), (), s32[]{:S(2)}) async-start(), calls=%async_computation.10 | async-start | bytes 4210688 | tf_op jit(solution)/shard_map/all_gather | solution.py:75
  235.8 1.7 copy-start.6
  235.8 1.8 copy-start.9
Sparse Core Ops, SparseCore 0:
  189.9 110.1 all-gather.1
where the time goes:
time: 312 us; the launch traced here: 311 us
  waiting for transfers between devices  134 us (43%)
  blocking collectives  91.3 us (29%)
  starting transfers between devices  24.2 us (8%)
  local copies, waits for them, and re-layouts  20.3 us (7%)
  between operations  17 us (5%)
  other arithmetic  13.3 us (4%)
  matrix products  11 us (4%)
    all_to_all x5, blocking collectives, from_everyone(): lax.all_to_all(jnp.broadcast_to(array[None], (peers, *array.shape)), axis...  91.3 us
    all_gather x1, waiting for transfers between devices, sent_together(): lax.all_gather(both, axis, axis=dim, tiled=True)  59.6 us
    all_to_all x2, waiting for transfers between devices, summed_on_arrival(): parts = lax.all_to_all(split_up(array, dim, peers), axis, 0, 0, tiled=True)  35.2 us
    all_to_all x1, waiting for transfers between devices, from_everyone(): lax.all_to_all(jnp.broadcast_to(array[None], (peers, *array.shape)), axis...  21.2 us
    all_to_all x2, waiting for transfers between devices, summed_rows(): lax.all_to_all(nearer.astype(jnp.bfloat16), far, split_axis=0, concat_axi...  18.2 us
    all_to_all x2, starting transfers between devices, summed_on_arrival(): parts = lax.all_to_all(split_up(array, dim, peers), axis, 0, 0, tiled=True)  9.1 us
    all_to_all x2, starting transfers between devices, summed_rows(): lax.all_to_all(nearer.astype(jnp.bfloat16), far, split_axis=0, concat_axi...  8.22 us
    all_to_all x1, starting transfers between devices, from_everyone(): lax.all_to_all(jnp.broadcast_to(array[None], (peers, *array.shape)), axis...  6.89 us
  transfers between devices with their start and end apart: 6, of which 6 were waited for; matrix products, arithmetic and copies ran while one was open for 9% of the time, Pallas kernels for 0%

commit v1 on v0

v1 whole, which is shorter than its diff:
```python
import jax
import jax.numpy as jnp
from jax import lax
from jax.sharding import Mesh
from jax.sharding import PartitionSpec as P

ROWS_OVER = ("z", "y", "c", "x")
BF = jnp.bfloat16
F32 = jnp.float32


def exchange(parts, axes):
    return lax.all_to_all(parts, axes, 0, 0, tiled=True)


def everywhere(block, axes):
    peers = lax.axis_size(axes)
    return exchange(jnp.broadcast_to(block[None], (peers, *block.shape)), axes)


def from_other_core(block):
    return lax.ppermute(block, "c", [(0, 1), (1, 0)])


def both_cores(block):
    core = lax.axis_index("c")
    other = from_other_core(block)
    first = jnp.where(core == 0, block, other)
    second = jnp.where(core == 0, other, block)
    return jnp.stack([first, second])


def whole_rows(parts, rest):
    c, yx, z, r, n = parts.shape
    parts = parts.reshape(c, 4, 4, z, r, n)
    return parts.transpose(3, 1, 0, 2, 4, 5).reshape(c * yx * z * r, n)


def core_half(terms):
    rows, n = terms.shape
    parts = terms.astype(BF).reshape(8, 4, 2, 4, rows // 256, n)
    core = lax.axis_index("c")
    mine = lax.dynamic_index_in_dim(parts, core, 2, keepdims=False)
    others = lax.dynamic_index_in_dim(parts, 1 - core, 2, keepdims=False)
    got = from_other_core(others)
    both = mine.astype(F32) + got.astype(F32)
    return both.astype(BF).transpose(1, 2, 0, 3, 4).reshape(16, 8, rows // 256, n)


def layer_update(master, grads, velocity, wsquare, gsquare):
    wnorm = jnp.sqrt(wsquare)
    gnorm = jnp.sqrt(gsquare)
    trust = wnorm / (gnorm + 5e-05 * wnorm)
    new_velocity = 0.9 * velocity + trust * (grads + 5e-05 * master)
    new_master = master - 0.1 * new_velocity
    return (new_master, new_velocity)


def shards(
    acts, saved_hidden, grad_out, master_reduce, master_expand, velocity_reduce, velocity_expand
):
    channels = grad_out.shape[1]
    middle = saved_hidden.shape[1]
    inv_c = 1.0 / float(channels) ** 0.5
    inv_m = 1.0 / float(middle) ** 0.5
    cur = jnp.stack([master_expand.astype(BF), master_reduce.astype(BF)])
    along_z = everywhere(cur, "z")
    expand_parts = everywhere(along_z[:, 0], ("y", "x"))
    cur_expand = whole_rows(both_cores(expand_parts), middle)
    reduce_parts = everywhere(along_z[:, 1], ("y", "x"))
    g_expand_half = core_half(
        lax.dot_general(
            grad_out, saved_hidden, (((0,), (0,)), ((), ())), preferred_element_type=F32
        )
        * inv_m
    )
    summed = jnp.dot(grad_out, cur_expand, preferred_element_type=F32)
    grad_hidden = jnp.where(saved_hidden > 0, summed * inv_m, 0.0).astype(BF)
    g_reduce_half = core_half(
        lax.dot_general(acts, grad_hidden, (((0,), (0,)), ((), ())), preferred_element_type=F32)
        * inv_c
    )
    halves = jnp.stack([g_expand_half, g_reduce_half], axis=1)
    arrived = exchange(halves, ("y", "x"))
    over_plane = jnp.sum(arrived.astype(F32), axis=0).astype(BF)
    arrived = exchange(over_plane.transpose(1, 0, 2, 3), "z")
    grads = jnp.sum(arrived.astype(F32), axis=0)
    g_expand, g_reduce = grads[0], grads[1]

    cur_reduce = whole_rows(both_cores(reduce_parts), middle)
    back = lax.dot_general(
        grad_hidden, cur_reduce, (((1,), (1,)), ((), ())), preferred_element_type=F32
    )
    grad_in = (grad_out.astype(F32) + back * inv_c).astype(BF)

    squares = jnp.stack(
        [
            jnp.sum(master_expand * master_expand),
            jnp.sum(g_expand * g_expand),
            jnp.sum(master_reduce * master_reduce),
            jnp.sum(g_reduce * g_reduce),
        ]
    )
    squares = everywhere(squares[None], ("z", "y")).sum(axis=0)
    squares = everywhere(squares, ("c", "x")).sum(axis=0)[0]
    new_mr, new_vr = layer_update(master_reduce, g_reduce, velocity_reduce, squares[2], squares[3])
    new_me, new_ve = layer_update(master_expand, g_expand, velocity_expand, squares[0], squares[1])
    work = jnp.stack([new_me.astype(BF), new_mr.astype(BF)])
    along_z = everywhere(work, "z")
    parts = both_cores(everywhere(along_z, ("y", "x")))
    work_expand = whole_rows(parts[:, :, :, 0], middle)
    work_reduce = whole_rows(parts[:, :, :, 1], middle)
    return (grad_in, new_mr, new_me, new_vr, new_ve, work_reduce, work_expand)


def solution(mesh):
    finer = Mesh(mesh.devices.reshape(8, 4, 2, 4), ROWS_OVER)
    split = P(ROWS_OVER, None)
    return jax.shard_map(
        shards,
        mesh=finer,
        in_specs=(split,) * 7,
        out_specs=(split,) * 5 + (P(), P()),
        check_vma=False,
    )
```

time: 312 us -> 217 us (0.70)
  waiting for transfers between devices: 134 us -> 11.9 us
  blocking collectives: 91.3 us -> 141 us
  between operations: 17 us -> 3.75 us
  starting transfers between devices: 24.2 us -> 15.3 us
    all_to_all x5 -> x1, waiting for transfers between devices: 74.6 us -> 9.22 us  [exchange(): return lax.all_to_all(parts, axes, 0, 0, tiled=True)]
    all_gather x1 -> x0, waiting for transfers between devices: 59.6 us -> none  [sent_together(): lax.all_gather(both, axis, axis=dim, tiled=True)]
    all_to_all x5 -> x8, blocking collectives: 91.3 us -> 141 us  [exchange(): return lax.all_to_all(parts, axes, 0, 0, tiled=True)]
    all_to_all x5 -> x1, starting transfers between devices: 24.2 us -> 3.66 us  [exchange(): return lax.all_to_all(parts, axes, 0, 0, tiled=True)]
    ppermute x0 -> x5, starting transfers between devices: none -> 11.7 us  [from_other_core(): return lax.ppermute(block, 'c', [(0, 1), (1, 0)])]
    reduce_sum x8 -> x4, other arithmetic: 7.59 us -> 0.39 us  [the longest x1 0.29 us: shards(): over_plane = jnp.sum(arrived.astype(F32), axis=0).astype(BF)]
    another operation x0 -> x9, other arithmetic: none -> 6.23 us  [the longest x4 2.69 us: both_cores(): return jnp.stack([first, second])]
    split x1 -> x0, local copies, waits for them, and re-layouts: 4.5 us -> none  [sent_together(): jnp.split(lax.all_gather(both, axis, axis=dim, tiled=True), ends, axis=al...]
  transfers between devices with their start and end apart: 6 -> 6, of which waited for: 6 -> 3; matrix products, arithmetic and copies ran while one was open for 9% -> 11% of each run, Pallas kernels for 0% -> 0%
where the time goes in v1:
time: 217 us; the launch traced here: 216 us
  blocking collectives  141 us (65%)
  local copies, waits for them, and re-layouts  17.4 us (8%)
  starting transfers between devices  15.3 us (7%)
  other arithmetic  13.8 us (6%)
  matrix products  12.4 us (6%)
  waiting for transfers between devices  11.9 us (5%)
  between operations  3.75 us (2%)
    all_to_all x8, blocking collectives, exchange(): return lax.all_to_all(parts, axes, 0, 0, tiled=True)  141 us
    ppermute x5, starting transfers between devices, from_other_core(): return lax.ppermute(block, 'c', [(0, 1), (1, 0)])  11.7 us
    all_to_all x1, waiting for transfers between devices, exchange(): return lax.all_to_all(parts, axes, 0, 0, tiled=True)  9.22 us
    dot_general x1, matrix products, shards(): lax.dot_general(grad_out, saved_hidden, (((0,), (0,)), ((), ())), preferr...  4.95 us
    unnamed x22, local copies, waits for them, and re-layouts  4.81 us
  transfers between devices with their start and end apart: 6, of which 3 were waited for; matrix products, arithmetic and copies ran while one was open for 11% of the time, Pallas kernels for 0%

profile of v1, /device:TPU:1, one launch (start us, length us, event | category | flops | bytes accessed | tf_op | source)
XLA Modules:
  0.0 215.7 jit_solution(10105225635768505424)
XLA Ops:
  0.6 0.0 copy-start
  0.6 1.5 multiply_reduce_fusion.1
  2.2 16.6 %all_to_all.45 = bf16[8,2,8,512]{3,2,1,0:T(8,128)(2,1)S(1)} all-to-all(bf16[8,2,8,512]{3,2,1,0:T(8,128)(2,1)S(1)} %broadcast_in_dim.22), channel_id=1, replica_groups=mesh['z'=8,'y'=4,'c'=2,'x'=4] {'z'}, dimensions={0} | all-to-all | bytes 262144 | tf_op jit(solution)/shard_map/all_to_all | solution.py:13
  18.8 0.1 broadcast_in_dim.24
  18.9 21.5 %all_to_all.46 = bf16[16,8,8,512]{3,2,1,0:T(8,128)(2,1)S(1)} all-to-all(bf16[16,8,8,512]{3,2,1,0:T(8,128)(2,1)S(1)} %broadcast_in_dim.24), channel_id=1, replica_groups=mesh['z'=8,'y'=4,'c'=2,'x'=4] {'y','x'}, dimensions={0} | all-to-all | bytes 2097152 | tf_op jit(solution)/shard_map/all_to_all | solution.py:13
  40.4 3.3 %collective-permute-start = (bf16[16,8,8,512]{3,2,1,0:T(8,128)(2,1)S(1)}, bf16[16,8,8,512]{3,2,1,0:T(8,128)(2,1)}, u32[]{:S(2)}, u32[]{:S(2)}) collective-permute-start(bf16[16,8,8,512]{3,2,1,0:T(8,128)(2,1)S(1)} %all_to_all.46), channel_id=1, source_target_pairs={{0,4},{4,0},{1,5},{5,1},{2,6},{6,2},{3,7},{7,3},{8,12},{12,8},{9,1... | collective-permute-start | bytes 3145736 | tf_op jit(solution)/shard_map/ppermute | solution.py:22
  43.6 5.0 %multiply_convert_fusion.1 = bf16[2048,512]{1,0:T(8,128)(2,1)} fusion(bf16[588,2048]{1,0:T(8,128)(2,1)} %param.9, bf16[588,512]{1,0:T(8,128)(2,1)} %param.8), kind=kOutput, calls=%fused_computation.4 | convolution fusion | flops 1235222528 | bytes 5107712 | tf_op jit(solution)/shard_map/dot_general | solution.py:72
  48.6 2.3 %dynamic-slice_bitcast_fusion.1 = bf16[8,4,4,8,512]{4,3,2,1,0:T(8,128)(2,1)} fusion(bf16[8,4,2,4,8,512]{5,4,3,2,1,0:T(8,128)(2,1)} %bitcast.14, s32[]{:T(128)S(6)} %select_n.52), kind=kLoop, calls=%fused_computation.23 | loop fusion | bytes 2097156 | tf_op jit(solution)/shard_map/jit(dynamic_index_in_dim)/squeeze | solution.py:44
  50.9 0.0 collective-permute-start.2
  50.9 0.0 collective-permute-done
  50.9 1.4 broadcast_select_fusion.3
  52.3 0.1 copy.65
  52.4 0.1 copy.66
  52.5 0.0 copy-start.6
  52.5 0.0 copy-start.8
  52.5 0.2 pad_maximum_fusion.1
  52.7 1.5 copy-done.6
  54.2 0.1 copy-done.8
  54.3 1.4 fusion.6
  55.7 0.8 copy-done.9
  56.6 3.1 %fusion = bf16[2048,512]{0,1:T(8,128)(2,1)} fusion(bf16[588,512]{1,0:T(8,128)(2,1)S(1)} %fusion.6, bf16[588,2048]{1,0:T(8,128)(2,1)S(1)} %copy-done), kind=kOutput, calls=%fused_computation.5 | convolution fusion | flops 1235222528 | bytes 5107712 | tf_op jit(solution)/shard_map/dot_general | solution.py:80
  59.7 2.9 %copy.70 = bf16[2048,512]{1,0:T(8,128)(2,1)S(1)} copy(bf16[2048,512]{0,1:T(8,128)(2,1)} %fusion) | data formatting | bytes 4194304 | tf_op jit(solution)/shard_map/convert_element_type | solution.py:41
  62.6 0.1 dynamic-slice_bitcast_fusion
  62.7 0.6 collective-permute-start.3
  63.3 0.0 collective-permute-done.2
  63.3 1.9 fusion.7
  65.2 0.1 copy.69
  65.3 0.4 collective-permute-done.3
  65.7 1.6 fusion.2
  67.3 0.2 pad_maximum_fusion.3
  67.5 30.2 %all_to_all.47 = bf16[16,2,8,8,512]{4,3,2,1,0:T(8,128)(2,1)S(1)} all-to-all(bf16[16,2,8,8,512]{4,3,2,1,0:T(8,128)(2,1)S(1)} %pad_maximum_fusion.3), channel_id=1, replica_groups=mesh['z'=8,'y'=4,'c'=2,'x'=4] {'y','x'}, dimensions={0} | all-to-all | bytes 4194304 | tf_op jit(solution)/shard_map/all_to_all | solution.py:13
  97.8 0.3 reduce_sum.78
  98.1 10.3 %all_to_all.48 = bf16[8,2,8,512]{3,2,1,0:T(8,128)(2,1)S(1)} all-to-all(bf16[8,2,8,512]{3,2,1,0:T(8,128)(2,1)S(1)} %copy.72), channel_id=1, replica_groups=mesh['z'=8,'y'=4,'c'=2,'x'=4] {'z'}, dimensions={0} | all-to-all | bytes 262144 | tf_op jit(solution)/shard_map/all_to_all | solution.py:13
  108.5 0.6 multiply_reduce_fusion.2
  109.1 2.7 %pad_maximum_fusion.6 = f32[4]{0:T(128)S(1)} fusion(f32[1]{0:T(128)} %bitcast.30, f32[1]{0:T(128)} %bitcast.28, f32[1]{0:T(128)} %bitcast.27, f32[1]{0:T(128)} %bitcast.13), kind=kLoop, calls=%fused_computation.47 | loop fusion | flops 12 | bytes 32 | tf_op jit(solution)/shard_map/stack | solution.py:96
  111.7 11.6 %all_to_all.49 = f32[32,1,4]{2,1,0:T(1,128)S(1)} all-to-all(f32[32,1,4]{2,1,0:T(1,128)S(1)} %broadcast_in_dim.53), channel_id=1, replica_groups=mesh['z'=8,'y'=4,'c'=2,'x'=4] {'z','y'}, dimensions={0} | all-to-all | bytes 1024 | tf_op jit(solution)/shard_map/all_to_all | solution.py:13
  123.3 0.1 reduce_sum.83
  123.4 11.0 %all_to_all.50 = f32[8,1,4]{2,1,0:T(1,128)S(1)} all-to-all(f32[8,1,4]{2,1,0:T(1,128)S(1)} %broadcast_in_dim.54), channel_id=1, replica_groups=mesh['z'=8,'y'=4,'c'=2,'x'=4] {'c','x'}, dimensions={0} | all-to-all | bytes 256 | tf_op jit(solution)/shard_map/all_to_all | solution.py:13
  134.4 0.6 fusion.8
  137.9 0.6 convert_bitcast_fusion.1
  138.5 10.2 %all_to_all.51 = bf16[8,2,8,512]{3,2,1,0:T(8,128)(2,1)S(1)} all-to-all(bf16[8,2,8,512]{3,2,1,0:T(8,128)(2,1)S(1)} %broadcast_in_dim.55), channel_id=1, replica_groups=mesh['z'=8,'y'=4,'c'=2,'x'=4] {'z'}, dimensions={0} | all-to-all | bytes 262144 | tf_op jit(solution)/shard_map/all_to_all | solution.py:13
  148.8 0.2 broadcast_in_dim.56
  149.0 29.8 %all_to_all.52 = bf16[16,8,2,8,512]{4,3,1,2,0:T(8,128)(2,1)S(1)} all-to-all(bf16[16,8,2,8,512]{4,3,1,2,0:T(8,128)(2,1)S(1)} %broadcast_in_dim.56), channel_id=1, replica_groups=mesh['z'=8,'y'=4,'c'=2,'x'=4] {'y','x'}, dimensions={0} | all-to-all | bytes 4194304 | tf_op jit(solution)/shard_map/all_to_all | solution.py:13
  178.8 1.1 broadcast_in_dim.52
  179.8 3.7 %all-to-all-start.2 = ((bf16[16,8,8,512]{3,2,1,0:T(8,128)(2,1)}), bf16[16,8,8,512]{3,2,1,0:T(8,128)(2,1)S(1)}, u32[]{:S(2)}, u32[]{:S(2)}) async-start(bf16[16,8,8,512]{3,2,1,0:T(8,128)(2,1)} %broadcast_in_dim.52), calls=%async_computation.2 | async-start | bytes 2097152 | tf_op jit(solution)/shard_map/all_to_all | solution.py:13
  183.5 1.5 copy.77
  185.0 3.3 %collective-permute-start.4 = (bf16[16,8,2,8,512]{4,3,1,0,2:T(8,128)(2,1)}, bf16[16,8,2,8,512]{4,3,1,0,2:T(8,128)(2,1)}, u32[]{:S(2)}, u32[]{:S(2)}) collective-permute-start(bf16[16,8,2,8,512]{4,3,1,0,2:T(8,128)(2,1)} %copy.77), channel_id=1, source_target_pairs={{0,4},{4,0},{1,5},{5,1},{2,6},{6,2},{3,7},{7,3},{8,12},{12,8},{9,1... | collective-permute-start | bytes 6291464 | tf_op jit(solution)/shard_map/ppermute | solution.py:22
  188.3 9.2 %all-to-all-done.2 = bf16[16,8,8,512]{3,2,1,0:T(8,128)(2,1)S(1)} async-done(((bf16[16,8,8,512]{3,2,1,0:T(8,128)(2,1)}), bf16[16,8,8,512]{3,2,1,0:T(8,128)(2,1)S(1)}, u32[]{:S(2)}, u32[]{:S(2)}) %all-to-all-start.2) | async-done | bytes 1048608 | tf_op jit(solution)/shard_map/all_to_all | solution.py:13
  197.5 4.5 %collective-permute-start.1 = (bf16[16,8,8,512]{3,2,1,0:T(8,128)(2,1)S(1)}, bf16[16,8,8,512]{3,2,1,0:T(8,128)(2,1)S(1)}, u32[]{:S(2)}, u32[]{:S(2)}) collective-permute-start(bf16[16,8,8,512]{3,2,1,0:T(8,128)(2,1)S(1)} %all-to-all-done.2), channel_id=1, source_target_pairs={{0,4},{4,0},{1,5},{5,1},{2,6},{6,2},{3,7},{7,3},{8,12},{12,8},{9,1... | collective-permute-start | bytes 3145736 | tf_op jit(solution)/shard_map/ppermute | solution.py:22
  202.0 2.3 %collective-permute-done.1 = bf16[16,8,8,512]{3,2,1,0:T(8,128)(2,1)S(1)} collective-permute-done((bf16[16,8,8,512]{3,2,1,0:T(8,128)(2,1)S(1)}, bf16[16,8,8,512]{3,2,1,0:T(8,128)(2,1)S(1)}, u32[]{:S(2)}, u32[]{:S(2)}) %collective-permute-start.1) | collective-permute-done | bytes 1048608 | tf_op jit(solution)/shard_map/ppermute | solution.py:22
  204.3 0.1 broadcast_select_fusion.1
  204.4 0.1 copy.68
  204.5 0.1 copy.67
  204.6 0.0 copy-start.7
  204.7 0.2 pad_maximum_fusion.2
  204.9 1.5 copy-done.7
  206.3 0.1 copy-done.10
  206.5 2.9 %add_convert_fusion = bf16[588,2048]{1,0:T(8,128)(2,1)} fusion(bf16[588,2048]{1,0:T(8,128)(2,1)S(1)} %copy-done.7, bf16[588,512]{1,0:T(8,128)(2,1)S(1)} %copy-done.10, bf16[2048,512]{1,0:T(8,128)(2,1)S(1)} %bitcast.106), kind=kOutput, calls=%fused_computation | convolution fusion | flops 1237942272 | bytes 7516160 | tf_op jit(solution)/shard_map/dot_general | solution.py:91
  209.3 0.0 collective-permute-done.4
  209.3 1.9 select_bitcast_fusion
  211.2 0.4 pad_maximum_fusion
  211.6 1.6 copy.80
  213.3 1.6 copy.81
  214.9 0.8 copy-done.1
  (23 shorter events, 0.2 us)
Async XLA Ops:
  0.6 55.9 %copy-start = (bf16[588,2048]{1,0:T(8,128)(2,1)S(1)}, bf16[588,2048]{1,0:T(8,128)(2,1)}, u32[]{:S(2)}) copy-start(bf16[588,2048]{1,0:T(8,128)(2,1)} %param.7) | copy-start | bytes 7225348
  40.4 10.6 %collective-permute-start = (bf16[16,8,8,512]{3,2,1,0:T(8,128)(2,1)S(1)}, bf16[16,8,8,512]{3,2,1,0:T(8,128)(2,1)}, u32[]{:S(2)}, u32[]{:S(2)}) collective-permute-start(bf16[16,8,8,512]{3,2,1,0:T(8,128)(2,1)S(1)} %all_to_all.46), channel_id=1, source_target_pairs={{0,4},{4,0},{1,5},{5,1},{2,6},{6,2},{3,7},{7,3},{8,12},{12,8},{9,1... | collective-permute-start | bytes 3145736 | tf_op jit(solution)/shard_map/ppermute | solution.py:22
  50.9 12.4 %collective-permute-start.2 = (bf16[8,4,4,8,512]{4,3,2,1,0:T(8,128)(2,1)}, bf16[8,4,4,8,512]{4,3,2,1,0:T(8,128)(2,1)}, u32[]{:S(2)}, u32[]{:S(2)}) collective-permute-start(bf16[8,4,4,8,512]{4,3,2,1,0:T(8,128)(2,1)} %dynamic-slice_bitcast_fusion.1), channel_id=1, source_target_pairs={{0,4},{4,0},{1,5},{5,1},{2,6},{6,2},{3,7},{7,3},{8,12},{12,8},{9,1... | collective-permute-start | bytes 3145736 | tf_op jit(solution)/shard_map/ppermute | solution.py:22
  52.5 1.7 copy-start.6
  52.5 1.8 copy-start.8
  55.7 0.8 copy-start.9
  62.7 3.0 %collective-permute-start.3 = (bf16[8,4,4,8,512]{4,3,2,1,0:T(8,128)(2,1)S(1)}, bf16[8,4,4,8,512]{4,3,2,1,0:T(8,128)(2,1)}, u32[]{:S(2)}, u32[]{:S(2)}) collective-permute-start(bf16[8,4,4,8,512]{4,3,2,1,0:T(8,128)(2,1)S(1)} %dynamic-slice_bitcast_fusion), channel_id=1, source_target_pairs={{0,4},{4,0},{1,5},{5,1},{2,6},{6,2},{3,7},{7,3},{8,12},{12,8},{9,1... | collective-permute-start | bytes 3145736 | tf_op jit(solution)/shard_map/ppermute | solution.py:22
  97.8 40.1 %copy-start.2 = (f32[8,512]{1,0:T(8,128)S(1)}, f32[8,512]{1,0:T(8,128)}, u32[]{:S(2)}) copy-start(f32[8,512]{1,0:T(8,128)} %param.10) | copy-start | bytes 49156
  97.8 40.1 %copy-start.3 = (f32[8,512]{1,0:T(8,128)S(1)}, f32[8,512]{1,0:T(8,128)}, u32[]{:S(2)}) copy-start(f32[8,512]{1,0:T(8,128)} %param.11) | copy-start | bytes 49156
  97.8 40.1 %copy-start.4 = (f32[8,512]{1,0:T(8,128)S(1)}, f32[8,512]{1,0:T(8,128)}, u32[]{:S(2)}) copy-start(f32[8,512]{1,0:T(8,128)} %param.13) | copy-start | bytes 49156
  97.8 40.1 %copy-start.5 = (f32[8,512]{1,0:T(8,128)S(1)}, f32[8,512]{1,0:T(8,128)}, u32[]{:S(2)}) copy-start(f32[8,512]{1,0:T(8,128)} %param.12) | copy-start | bytes 49156
  179.8 17.7 %all-to-all-start.2 = ((bf16[16,8,8,512]{3,2,1,0:T(8,128)(2,1)}), bf16[16,8,8,512]{3,2,1,0:T(8,128)(2,1)S(1)}, u32[]{:S(2)}, u32[]{:S(2)}) async-start(bf16[16,8,8,512]{3,2,1,0:T(8,128)(2,1)} %broadcast_in_dim.52), calls=%async_computation.2 | async-start | bytes 2097152 | tf_op jit(solution)/shard_map/all_to_all | solution.py:13
  185.0 24.3 %collective-permute-start.4 = (bf16[16,8,2,8,512]{4,3,1,0,2:T(8,128)(2,1)}, bf16[16,8,2,8,512]{4,3,1,0,2:T(8,128)(2,1)}, u32[]{:S(2)}, u32[]{:S(2)}) collective-permute-start(bf16[16,8,2,8,512]{4,3,1,0,2:T(8,128)(2,1)} %copy.77), channel_id=1, source_target_pairs={{0,4},{4,0},{1,5},{5,1},{2,6},{6,2},{3,7},{7,3},{8,12},{12,8},{9,1... | collective-permute-start | bytes 6291464 | tf_op jit(solution)/shard_map/ppermute | solution.py:22
  197.5 6.8 %collective-permute-start.1 = (bf16[16,8,8,512]{3,2,1,0:T(8,128)(2,1)S(1)}, bf16[16,8,8,512]{3,2,1,0:T(8,128)(2,1)S(1)}, u32[]{:S(2)}, u32[]{:S(2)}) collective-permute-start(bf16[16,8,8,512]{3,2,1,0:T(8,128)(2,1)S(1)} %all-to-all-done.2), channel_id=1, source_target_pairs={{0,4},{4,0},{1,5},{5,1},{2,6},{6,2},{3,7},{7,3},{8,12},{12,8},{9,1... | collective-permute-start | bytes 3145736 | tf_op jit(solution)/shard_map/ppermute | solution.py:22
  204.6 1.7 copy-start.7
  204.7 1.8 copy-start.10
  213.3 2.4 %copy-start.1 = (bf16[588,2048]{1,0:T(8,128)(2,1)S(1)}, bf16[588,2048]{1,0:T(8,128)(2,1)}, u32[]{:S(2)}) copy-start(bf16[588,2048]{1,0:T(8,128)(2,1)} %param.7) | copy-start | bytes 7225348

commit v2 on v1

--- a/solution.py
+++ b/solution.py
@@ -3,6 +3,7 @@
 from jax import lax
 from jax.sharding import Mesh
 from jax.sharding import PartitionSpec as P
+
 
 ROWS_OVER = ("z", "y", "c", "x")
 BF = jnp.bfloat16
@@ -30,7 +31,7 @@
     return jnp.stack([first, second])
 
 
-def whole_rows(parts, rest):
+def whole_rows(parts):
     c, yx, z, r, n = parts.shape
     parts = parts.reshape(c, 4, 4, z, r, n)
     return parts.transpose(3, 1, 0, 2, 4, 5).reshape(c * yx * z * r, n)
@@ -38,7 +39,7 @@
 
 def core_half(terms):
     rows, n = terms.shape
-    parts = terms.astype(BF).reshape(8, 4, 2, 4, rows // 256, n)
+    parts = terms.reshape(8, 4, 2, 4, rows // 256, n)
     core = lax.axis_index("c")
     mine = lax.dynamic_index_in_dim(parts, core, 2, keepdims=False)
     others = lax.dynamic_index_in_dim(parts, 1 - core, 2, keepdims=False)
@@ -56,7 +57,7 @@
     return (new_master, new_velocity)
 
 
-def shards(
+def step(
     acts, saved_hidden, grad_out, master_reduce, master_expand, velocity_reduce, velocity_expand
 ):
     channels = grad_out.shape[1]
@@ -66,28 +67,33 @@
     cur = jnp.stack([master_expand.astype(BF), master_reduce.astype(BF)])
     along_z = everywhere(cur, "z")
     expand_parts = everywhere(along_z[:, 0], ("y", "x"))
-    cur_expand = whole_rows(both_cores(expand_parts), middle)
+    cur_expand = whole_rows(both_cores(expand_parts))
     reduce_parts = everywhere(along_z[:, 1], ("y", "x"))
-    g_expand_half = core_half(
+    expand_terms = (
         lax.dot_general(
             grad_out, saved_hidden, (((0,), (0,)), ((), ())), preferred_element_type=F32
         )
         * inv_m
-    )
+    ).astype(BF)
+    g_expand_half = core_half(expand_terms)
     summed = jnp.dot(grad_out, cur_expand, preferred_element_type=F32)
     grad_hidden = jnp.where(saved_hidden > 0, summed * inv_m, 0.0).astype(BF)
-    g_reduce_half = core_half(
-        lax.dot_general(acts, grad_hidden, (((0,), (0,)), ((), ())), preferred_element_type=F32)
+    reduce_terms = (
+        lax.dot_general(
+            acts, grad_hidden, (((0,), (0,)), ((), ())), preferred_element_type=F32
+        )
         * inv_c
-    )
+    ).astype(BF)
+    g_reduce_half = core_half(reduce_terms)
     halves = jnp.stack([g_expand_half, g_reduce_half], axis=1)
+    halves, reduce_parts = lax.optimization_barrier((halves, reduce_parts))
     arrived = exchange(halves, ("y", "x"))
     over_plane = jnp.sum(arrived.astype(F32), axis=0).astype(BF)
     arrived = exchange(over_plane.transpose(1, 0, 2, 3), "z")
     grads = jnp.sum(arrived.astype(F32), axis=0)
     g_expand, g_reduce = grads[0], grads[1]
 
-    cur_reduce = whole_rows(both_cores(reduce_parts), middle)
+    cur_reduce = whole_rows(both_cores(reduce_parts))
     back = lax.dot_general(
         grad_hidden, cur_reduce, (((1,), (1,)), ((), ())), preferred_element_type=F32
     )
@@ -108,8 +114,8 @@
     work = jnp.stack([new_me.astype(BF), new_mr.astype(BF)])
     along_z = everywhere(work, "z")
     parts = both_cores(everywhere(along_z, ("y", "x")))
-    work_expand = whole_rows(parts[:, :, :, 0], middle)
-    work_reduce = whole_rows(parts[:, :, :, 1], middle)
+    work_expand = whole_rows(parts[:, :, :, 0])
+    work_reduce = whole_rows(parts[:, :, :, 1])
     return (grad_in, new_mr, new_me, new_vr, new_ve, work_reduce, work_expand)
 
 
@@ -117,7 +123,7 @@
     finer = Mesh(mesh.devices.reshape(8, 4, 2, 4), ROWS_OVER)
     split = P(ROWS_OVER, None)
     return jax.shard_map(
-        shards,
+        step,
         mesh=finer,
         in_specs=(split,) * 7,
         out_specs=(split,) * 5 + (P(), P()),

time: 217 us -> 221 us (1.018)
  waiting for transfers between devices: 11.9 us -> 19.9 us
  starting transfers between devices: 15.3 us -> 11.1 us
    all_to_all x1, waiting for transfers between devices: 9.22 us -> 14.9 us  [exchange(): return lax.all_to_all(parts, axes, 0, 0, tiled=True)]
    ppermute x5, starting transfers between devices: 11.7 us -> 7.46 us  [from_other_core(): return lax.ppermute(block, 'c', [(0, 1), (1, 0)])]
    ppermute x5, waiting for transfers between devices: 2.67 us -> 5.02 us  [from_other_core(): return lax.ppermute(block, 'c', [(0, 1), (1, 0)])]
  transfers between devices with their start and end apart: 6 -> 6, of which waited for: 3 -> 2; matrix products, arithmetic and copies ran while one was open for 11% -> 12% of each run, Pallas kernels for 0% -> 0%
where the time goes in v2:
time: 221 us; the launch traced here: 220 us
  blocking collectives  142 us (64%)
  waiting for transfers between devices  19.9 us (9%)
  local copies, waits for them, and re-layouts  17 us (8%)
  other arithmetic  13.9 us (6%)
  matrix products  12.4 us (6%)
  starting transfers between devices  11.1 us (5%)
  between operations  3.76 us (2%)
    all_to_all x8, blocking collectives, exchange(): return lax.all_to_all(parts, axes, 0, 0, tiled=True)  142 us
    all_to_all x1, waiting for transfers between devices, exchange(): return lax.all_to_all(parts, axes, 0, 0, tiled=True)  14.9 us
    ppermute x5, starting transfers between devices, from_other_core(): return lax.ppermute(block, 'c', [(0, 1), (1, 0)])  7.46 us
    ppermute x5, waiting for transfers between devices, from_other_core(): return lax.ppermute(block, 'c', [(0, 1), (1, 0)])  5.02 us
    dot_general x1, matrix products, step(): lax.dot_general(grad_out, saved_hidden, (((0,), (0,)), ((), ())), preferr...  4.95 us
    unnamed x22, local copies, waits for them, and re-layouts  4.8 us
  transfers between devices with their start and end apart: 6, of which 2 were waited for; matrix products, arithmetic and copies ran while one was open for 12% of the time, Pallas kernels for 0%

profile of v2, /device:TPU:1, one launch (start us, length us, event | category | flops | bytes accessed | tf_op | source)
XLA Modules:
  0.0 219.9 jit_solution(12470851511103781035)
XLA Ops:
  0.6 0.0 copy-start
  0.6 1.5 multiply_reduce_fusion.1
  2.2 16.6 %all_to_all.45 = bf16[8,2,8,512]{3,2,1,0:T(8,128)(2,1)S(1)} all-to-all(bf16[8,2,8,512]{3,2,1,0:T(8,128)(2,1)S(1)} %broadcast_in_dim.22), channel_id=1, replica_groups=mesh['z'=8,'y'=4,'c'=2,'x'=4] {'z'}, dimensions={0} | all-to-all | bytes 262144 | tf_op jit(solution)/shard_map/all_to_all | solution.py:14
  18.8 0.1 broadcast_in_dim.24
  18.9 21.5 %all_to_all.46 = bf16[16,8,8,512]{3,2,1,0:T(8,128)(2,1)S(1)} all-to-all(bf16[16,8,8,512]{3,2,1,0:T(8,128)(2,1)S(1)} %broadcast_in_dim.24), channel_id=1, replica_groups=mesh['z'=8,'y'=4,'c'=2,'x'=4] {'y','x'}, dimensions={0} | all-to-all | bytes 2097152 | tf_op jit(solution)/shard_map/all_to_all | solution.py:14
  40.4 3.3 %collective-permute-start = (bf16[16,8,8,512]{3,2,1,0:T(8,128)(2,1)S(1)}, bf16[16,8,8,512]{3,2,1,0:T(8,128)(2,1)}, u32[]{:S(2)}, u32[]{:S(2)}) collective-permute-start(bf16[16,8,8,512]{3,2,1,0:T(8,128)(2,1)S(1)} %all_to_all.46), channel_id=1, source_target_pairs={{0,4},{4,0},{1,5},{5,1},{2,6},{6,2},{3,7},{7,3},{8,12},{12,8},{9,1... | collective-permute-start | bytes 3145736 | tf_op jit(solution)/shard_map/ppermute | solution.py:23
  43.6 5.0 %multiply_convert_fusion.1 = bf16[2048,512]{1,0:T(8,128)(2,1)} fusion(bf16[588,2048]{1,0:T(8,128)(2,1)} %param.9, bf16[588,512]{1,0:T(8,128)(2,1)} %param.8), kind=kOutput, calls=%fused_computation.4 | convolution fusion | flops 1235222528 | bytes 5107712 | tf_op jit(solution)/shard_map/dot_general | solution.py:73
  48.6 2.3 %dynamic-slice_bitcast_fusion.1 = bf16[8,4,4,8,512]{4,3,2,1,0:T(8,128)(2,1)} fusion(bf16[8,4,2,4,8,512]{5,4,3,2,1,0:T(8,128)(2,1)} %bitcast.8, s32[]{:T(128)S(6)} %select_n.50), kind=kLoop, calls=%fused_computation.23 | loop fusion | bytes 2097156 | tf_op jit(solution)/shard_map/jit(dynamic_index_in_dim)/squeeze | solution.py:45
  50.9 0.0 collective-permute-start.1
  50.9 0.0 collective-permute-done
  50.9 1.4 broadcast_select_fusion.3
  52.3 0.1 copy.65
  52.4 0.1 copy.66
  52.5 0.0 copy-start.6
  52.5 0.0 copy-start.8
  52.5 0.2 pad_maximum_fusion.1
  52.7 1.5 copy-done.6
  54.2 0.1 copy-done.8
  54.3 1.4 fusion.6
  55.7 0.8 copy-done.9
  56.6 3.1 %fusion = bf16[2048,512]{0,1:T(8,128)(2,1)} fusion(bf16[588,512]{1,0:T(8,128)(2,1)S(1)} %fusion.6, bf16[588,2048]{1,0:T(8,128)(2,1)S(1)} %copy-done), kind=kOutput, calls=%fused_computation.5 | convolution fusion | flops 1235222528 | bytes 5107712 | tf_op jit(solution)/shard_map/dot_general | solution.py:82
  59.7 2.9 %copy.68 = bf16[2048,512]{1,0:T(8,128)(2,1)S(1)} copy(bf16[2048,512]{0,1:T(8,128)(2,1)} %fusion) | data formatting | bytes 4194304 | tf_op jit(solution)/shard_map/convert_element_type | solution.py:86
  62.6 1.1 dynamic-slice_bitcast_fusion
  63.7 0.5 collective-permute-start.2
  64.2 1.1 broadcast_in_dim.52
  65.3 3.7 %all-to-all-start.2 = ((bf16[16,8,8,512]{3,2,1,0:T(8,128)(2,1)}), bf16[16,8,8,512]{3,2,1,0:T(8,128)(2,1)S(1)}, u32[]{:S(2)}, u32[]{:S(2)}) async-start(bf16[16,8,8,512]{3,2,1,0:T(8,128)(2,1)} %broadcast_in_dim.52), calls=%async_computation.2 | async-start | bytes 2097152 | tf_op jit(solution)/shard_map/all_to_all | solution.py:14
  68.9 0.0 collective-permute-done.1
  68.9 1.9 fusion.7
  70.9 0.1 copy.67
  71.0 0.0 collective-permute-done.2
  71.0 1.6 fusion.2
  72.7 0.2 pad_maximum_fusion.2
  72.9 14.9 %all-to-all-done.2 = bf16[16,8,8,512]{3,2,1,0:T(8,128)(2,1)S(1)} async-done(((bf16[16,8,8,512]{3,2,1,0:T(8,128)(2,1)}), bf16[16,8,8,512]{3,2,1,0:T(8,128)(2,1)S(1)}, u32[]{:S(2)}, u32[]{:S(2)}) %all-to-all-start.2) | async-done | bytes 1048608 | tf_op jit(solution)/shard_map/all_to_all | solution.py:14
  87.7 30.7 %all_to_all.47 = bf16[16,2,8,8,512]{4,3,2,1,0:T(8,128)(2,1)} all-to-all(bf16[16,2,8,8,512]{4,3,2,1,0:T(8,128)(2,1)S(1)} %pad_maximum_fusion.2), channel_id=1, replica_groups=mesh['z'=8,'y'=4,'c'=2,'x'=4] {'y','x'}, dimensions={0} | all-to-all | bytes 4194304 | tf_op jit(solution)/shard_map/all_to_all | solution.py:14
  118.4 1.9 reduce_sum.78
  120.4 10.4 %all_to_all.48 = bf16[8,2,8,512]{3,2,1,0:T(8,128)(2,1)S(1)} all-to-all(bf16[8,2,8,512]{3,2,1,0:T(8,128)(2,1)S(1)} %copy.72), channel_id=1, replica_groups=mesh['z'=8,'y'=4,'c'=2,'x'=4] {'z'}, dimensions={0} | all-to-all | bytes 262144 | tf_op jit(solution)/shard_map/all_to_all | solution.py:14
  130.8 0.6 multiply_reduce_fusion.2
  131.4 2.7 %pad_maximum_fusion.6 = f32[4]{0:T(128)S(1)} fusion(f32[1]{0:T(128)} %bitcast.30, f32[1]{0:T(128)} %bitcast.28, f32[1]{0:T(128)} %bitcast.27, f32[1]{0:T(128)} %bitcast.24), kind=kLoop, calls=%fused_computation.47 | loop fusion | flops 12 | bytes 32 | tf_op jit(solution)/shard_map/stack | solution.py:102
  134.1 11.6 %all_to_all.49 = f32[32,1,4]{2,1,0:T(1,128)S(1)} all-to-all(f32[32,1,4]{2,1,0:T(1,128)S(1)} %broadcast_in_dim.53), channel_id=1, replica_groups=mesh['z'=8,'y'=4,'c'=2,'x'=4] {'z','y'}, dimensions={0} | all-to-all | bytes 1024 | tf_op jit(solution)/shard_map/all_to_all | solution.py:14
  145.7 0.1 reduce_sum.83
  145.8 11.1 %all_to_all.50 = f32[8,1,4]{2,1,0:T(1,128)S(1)} all-to-all(f32[8,1,4]{2,1,0:T(1,128)S(1)} %broadcast_in_dim.54), channel_id=1, replica_groups=mesh['z'=8,'y'=4,'c'=2,'x'=4] {'c','x'}, dimensions={0} | all-to-all | bytes 256 | tf_op jit(solution)/shard_map/all_to_all | solution.py:14
  156.9 0.6 fusion.8
  160.4 0.6 convert_bitcast_fusion.1
  161.0 10.2 %all_to_all.51 = bf16[8,2,8,512]{3,2,1,0:T(8,128)(2,1)S(1)} all-to-all(bf16[8,2,8,512]{3,2,1,0:T(8,128)(2,1)S(1)} %broadcast_in_dim.55), channel_id=1, replica_groups=mesh['z'=8,'y'=4,'c'=2,'x'=4] {'z'}, dimensions={0} | all-to-all | bytes 262144 | tf_op jit(solution)/shard_map/all_to_all | solution.py:14
  171.3 0.2 broadcast_in_dim.56
  171.5 29.8 %all_to_all.52 = bf16[16,8,2,8,512]{4,3,1,2,0:T(8,128)(2,1)S(1)} all-to-all(bf16[16,8,2,8,512]{4,3,1,2,0:T(8,128)(2,1)S(1)} %broadcast_in_dim.56), channel_id=1, replica_groups=mesh['z'=8,'y'=4,'c'=2,'x'=4] {'y','x'}, dimensions={0} | all-to-all | bytes 4194304 | tf_op jit(solution)/shard_map/all_to_all | solution.py:14
  201.3 0.2 copy.77
  201.4 3.4 %collective-permute-start.4 = (bf16[16,8,2,8,512]{4,3,1,0,2:T(8,128)(2,1)S(1)}, bf16[16,8,2,8,512]{4,3,1,0,2:T(8,128)(2,1)S(1)}, u32[]{:S(2)}, u32[]{:S(2)}) collective-permute-start(bf16[16,8,2,8,512]{4,3,1,0,2:T(8,128)(2,1)S(1)} %copy.77), channel_id=1, source_target_pairs={{0,4},{4,0},{1,5},{5,1},{2,6},{6,2},{3,7},{7,3},{8,12},{12,8},{9,1... | collective-permute-start | bytes 6291464 | tf_op jit(solution)/shard_map/ppermute | solution.py:23
  204.8 0.3 collective-permute-start.3
  205.1 5.0 %collective-permute-done.3 = bf16[16,8,8,512]{3,2,1,0:T(8,128)(2,1)S(1)} collective-permute-done((bf16[16,8,8,512]{3,2,1,0:T(8,128)(2,1)S(1)}, bf16[16,8,8,512]{3,2,1,0:T(8,128)(2,1)S(1)}, u32[]{:S(2)}, u32[]{:S(2)}) %collective-permute-start.3) | collective-permute-done | bytes 1048608 | tf_op jit(solution)/shard_map/ppermute | solution.py:23
  210.1 0.1 broadcast_select_fusion.1
  210.2 0.1 copy.70
  210.3 0.1 copy.71
  210.4 0.0 copy-start.7
  210.5 0.2 pad_maximum_fusion.3
  210.7 1.5 copy-done.7
  212.1 0.1 copy-done.10
  212.2 2.9 %add_convert_fusion = bf16[588,2048]{1,0:T(8,128)(2,1)} fusion(bf16[588,2048]{1,0:T(8,128)(2,1)S(1)} %copy-done.7, bf16[588,512]{1,0:T(8,128)(2,1)S(1)} %copy-done.10, bf16[2048,512]{1,0:T(8,128)(2,1)S(1)} %bitcast.106), kind=kOutput, calls=%fused_computation | convolution fusion | flops 1237942272 | bytes 7516160 | tf_op jit(solution)/shard_map/dot_general | solution.py:97
  215.1 0.0 collective-permute-done.4
  215.1 0.3 select_bitcast_fusion
  215.4 0.4 pad_maximum_fusion
  215.8 1.6 copy.80
  217.5 1.6 copy.81
  219.1 0.8 copy-done.1
  (23 shorter events, 0.2 us)
Async XLA Ops:
  0.6 55.9 %copy-start = (bf16[588,2048]{1,0:T(8,128)(2,1)S(1)}, bf16[588,2048]{1,0:T(8,128)(2,1)}, u32[]{:S(2)}) copy-start(bf16[588,2048]{1,0:T(8,128)(2,1)} %param.7) | copy-start | bytes 7225348
  40.4 10.6 %collective-permute-start = (bf16[16,8,8,512]{3,2,1,0:T(8,128)(2,1)S(1)}, bf16[16,8,8,512]{3,2,1,0:T(8,128)(2,1)}, u32[]{:S(2)}, u32[]{:S(2)}) collective-permute-start(bf16[16,8,8,512]{3,2,1,0:T(8,128)(2,1)S(1)} %all_to_all.46), channel_id=1, source_target_pairs={{0,4},{4,0},{1,5},{5,1},{2,6},{6,2},{3,7},{7,3},{8,12},{12,8},{9,1... | collective-permute-start | bytes 3145736 | tf_op jit(solution)/shard_map/ppermute | solution.py:23
  50.9 18.0 %collective-permute-start.1 = (bf16[8,4,4,8,512]{4,3,2,1,0:T(8,128)(2,1)}, bf16[8,4,4,8,512]{4,3,2,1,0:T(8,128)(2,1)}, u32[]{:S(2)}, u32[]{:S(2)}) collective-permute-start(bf16[8,4,4,8,512]{4,3,2,1,0:T(8,128)(2,1)} %dynamic-slice_bitcast_fusion.1), channel_id=1, source_target_pairs={{0,4},{4,0},{1,5},{5,1},{2,6},{6,2},{3,7},{7,3},{8,12},{12,8},{9,1... | collective-permute-start | bytes 3145736 | tf_op jit(solution)/shard_map/ppermute | solution.py:23
  52.5 1.7 copy-start.6
  52.5 1.8 copy-start.8
  55.7 0.8 copy-start.9
  63.7 7.3 %collective-permute-start.2 = (bf16[8,4,4,8,512]{4,3,2,1,0:T(8,128)(2,1)}, bf16[8,4,4,8,512]{4,3,2,1,0:T(8,128)(2,1)}, u32[]{:S(2)}, u32[]{:S(2)}) collective-permute-start(bf16[8,4,4,8,512]{4,3,2,1,0:T(8,128)(2,1)} %dynamic-slice_bitcast_fusion), channel_id=1, source_target_pairs={{0,4},{4,0},{1,5},{5,1},{2,6},{6,2},{3,7},{7,3},{8,12},{12,8},{9,1... | collective-permute-start | bytes 3145736 | tf_op jit(solution)/shard_map/ppermute | solution.py:23
  65.3 22.5 %all-to-all-start.2 = ((bf16[16,8,8,512]{3,2,1,0:T(8,128)(2,1)}), bf16[16,8,8,512]{3,2,1,0:T(8,128)(2,1)S(1)}, u32[]{:S(2)}, u32[]{:S(2)}) async-start(bf16[16,8,8,512]{3,2,1,0:T(8,128)(2,1)} %broadcast_in_dim.52), calls=%async_computation.2 | async-start | bytes 2097152 | tf_op jit(solution)/shard_map/all_to_all | solution.py:14
  118.4 41.9 %copy-start.2 = (f32[8,512]{1,0:T(8,128)S(1)}, f32[8,512]{1,0:T(8,128)}, u32[]{:S(2)}) copy-start(f32[8,512]{1,0:T(8,128)} %param.10) | copy-start | bytes 49156
  118.4 41.9 %copy-start.3 = (f32[8,512]{1,0:T(8,128)S(1)}, f32[8,512]{1,0:T(8,128)}, u32[]{:S(2)}) copy-start(f32[8,512]{1,0:T(8,128)} %param.11) | copy-start | bytes 49156
  118.4 41.9 %copy-start.4 = (f32[8,512]{1,0:T(8,128)S(1)}, f32[8,512]{1,0:T(8,128)}, u32[]{:S(2)}) copy-start(f32[8,512]{1,0:T(8,128)} %param.13) | copy-start | bytes 49156
  118.4 41.9 %copy-start.5 = (f32[8,512]{1,0:T(8,128)S(1)}, f32[8,512]{1,0:T(8,128)}, u32[]{:S(2)}) copy-start(f32[8,512]{1,0:T(8,128)} %param.12) | copy-start | bytes 49156
  201.4 13.7 %collective-permute-start.4 = (bf16[16,8,2,8,512]{4,3,1,0,2:T(8,128)(2,1)S(1)}, bf16[16,8,2,8,512]{4,3,1,0,2:T(8,128)(2,1)S(1)}, u32[]{:S(2)}, u32[]{:S(2)}) collective-permute-start(bf16[16,8,2,8,512]{4,3,1,0,2:T(8,128)(2,1)S(1)} %copy.77), channel_id=1, source_target_pairs={{0,4},{4,0},{1,5},{5,1},{2,6},{6,2},{3,7},{7,3},{8,12},{12,8},{9,1... | collective-permute-start | bytes 6291464 | tf_op jit(solution)/shard_map/ppermute | solution.py:23
  204.8 5.3 %collective-permute-start.3 = (bf16[16,8,8,512]{3,2,1,0:T(8,128)(2,1)S(1)}, bf16[16,8,8,512]{3,2,1,0:T(8,128)(2,1)S(1)}, u32[]{:S(2)}, u32[]{:S(2)}) collective-permute-start(bf16[16,8,8,512]{3,2,1,0:T(8,128)(2,1)S(1)} %all-to-all-done.2), channel_id=1, source_target_pairs={{0,4},{4,0},{1,5},{5,1},{2,6},{6,2},{3,7},{7,3},{8,12},{12,8},{9,1... | collective-permute-start | bytes 3145736 | tf_op jit(solution)/shard_map/ppermute | solution.py:23
  210.4 1.7 copy-start.7
  210.5 1.8 copy-start.10
  217.5 2.4 %copy-start.1 = (bf16[588,2048]{1,0:T(8,128)(2,1)S(1)}, bf16[588,2048]{1,0:T(8,128)(2,1)}, u32[]{:S(2)}) copy-start(bf16[588,2048]{1,0:T(8,128)(2,1)} %param.7) | copy-start | bytes 7225348

commit v3 on v2

v3 whole, which is shorter than its diff:
```python
import functools

import jax
import jax.numpy as jnp
from jax import lax
from jax.experimental import pallas as pl
from jax.experimental.pallas import tpu as pltpu
from jax.sharding import Mesh
from jax.sharding import PartitionSpec as P


ROWS_OVER = ("z", "y", "c", "x")
BF = jnp.bfloat16
F32 = jnp.float32


def exchange(parts, axes):
    return lax.all_to_all(parts, axes, 0, 0, tiled=True)


def everywhere(block, axes):
    peers = lax.axis_size(axes)
    return exchange(jnp.broadcast_to(block[None], (peers, *block.shape)), axes)


def from_other_core(block):
    return lax.ppermute(block, "c", [(0, 1), (1, 0)])


def both_cores(block):
    core = lax.axis_index("c")
    other = from_other_core(block)
    first = jnp.where(core == 0, block, other)
    second = jnp.where(core == 0, other, block)
    return jnp.stack([first, second])


def whole_rows(parts):
    c, yx, z, r, n = parts.shape
    parts = parts.reshape(c, 4, 4, z, r, n)
    return parts.transpose(3, 1, 0, 2, 4, 5).reshape(c * yx * z * r, n)


def fill_weights(core, mine_ref, other_ref, whole_ref):
    for z in range(8):
        tiles = []
        for y in range(4):
            mine = [mine_ref[y * 4 + x, z].astype(F32) for x in range(4)]
            other = [other_ref[y * 4 + x, z].astype(F32) for x in range(4)]
            tiles += [jnp.where(core == 0, m, o) for m, o in zip(mine, other)]
            tiles += [jnp.where(core == 0, o, m) for m, o in zip(mine, other)]
        rows = jnp.concatenate(tiles, axis=0).astype(BF)
        whole_ref[pl.ds(z * 256, 256), :] = rows


def terms_to_halves(core, left_ref, right, scale, keep_ref, send_ref):
    for z in range(8):
        left = left_ref[:, pl.ds(z * 256, 256)]
        part = lax.dot_general(left, right, (((0,), (0,)), ((), ())), preferred_element_type=F32)
        part = (part * scale).reshape(4, 2, 4, 8, right.shape[1])
        for y in range(4):
            first, second = part[y, 0], part[y, 1]
            keep_ref[pl.ds(y * 4, 4), z] = jnp.where(core == 0, first, second).astype(BF)
            send_ref[pl.ds(y * 4, 4), z] = jnp.where(core == 0, second, first).astype(BF)


def expand_kernel(scale, core_ref, grad_ref, hidden_ref, keep_ref, send_ref):
    terms_to_halves(core_ref[0], grad_ref, hidden_ref[...], scale, keep_ref, send_ref)


def hidden_kernel(
    inv_m,
    inv_c,
    core_ref,
    saved_ref,
    mine_ref,
    other_ref,
    grad_hbm,
    acts_hbm,
    out_ref,
    keep_ref,
    send_ref,
    whole_ref,
    grad_ref,
    acts_ref,
    sems,
):
    core = core_ref[0]
    grad_copy = pltpu.make_async_copy(grad_hbm, grad_ref, sems.at[0])
    acts_copy = pltpu.make_async_copy(acts_hbm, acts_ref, sems.at[1])
    grad_copy.start()
    acts_copy.start()
    fill_weights(core, mine_ref, other_ref, whole_ref)
    grad_copy.wait()
    summed = jnp.dot(grad_ref[...], whole_ref[...], preferred_element_type=F32)
    saved = saved_ref[...].astype(F32)
    out_ref[...] = jnp.where(saved > 0, summed * inv_m, 0.0).astype(BF)
    acts_copy.wait()
    terms_to_halves(core, acts_ref, out_ref[...], inv_c, keep_ref, send_ref)


def chip_sum_kernel(keep_e_ref, got_e_ref, keep_r_ref, got_r_ref, out_ref):
    for at, (keep_ref, got_ref) in enumerate(((keep_e_ref, got_e_ref), (keep_r_ref, got_r_ref))):
        total = keep_ref[...].astype(F32) + got_ref[...].astype(F32)
        out_ref[:, at] = total.astype(BF)


def chip_sum(*parts):
    peers, *rest = parts[0].shape
    whole = pl.BlockSpec(memory_space=pltpu.VMEM)
    moved = 3 * parts[0].size * 4
    return pl.pallas_call(
        chip_sum_kernel,
        out_shape=jax.ShapeDtypeStruct((peers, 2, *rest), BF),
        in_specs=[whole] * 4,
        out_specs=whole,
        compiler_params=pltpu.CompilerParams(vmem_limit_bytes=16 * 1024 * 1024),
        cost_estimate=pl.CostEstimate(
            flops=2 * parts[0].size, bytes_accessed=moved, transcendentals=0
        ),
    )(*parts)


def back_kernel(inv_c, core_ref, grad_ref, hidden_ref, mine_ref, other_ref, out_ref, whole_ref):
    fill_weights(core_ref[0], mine_ref, other_ref, whole_ref)
    for z in range(8):
        columns = pl.ds(z * 256, 256)
        back = lax.dot_general(
            hidden_ref[...],
            whole_ref[columns, :],
            (((1,), (1,)), ((), ())),
            preferred_element_type=F32,
        )
        out_ref[:, columns] = (grad_ref[:, columns].astype(F32) + back * inv_c).astype(BF)


def local_call(kernel, operands, outs, scratch, flops, streamed=()):
    whole = pl.BlockSpec(memory_space=pltpu.VMEM)
    core = lax.axis_index("c").astype(jnp.int32).reshape(1)
    moved = sum(x.size * x.dtype.itemsize for x in (*operands, *streamed, *outs))
    scratch = scratch + [pltpu.VMEM(x.shape, x.dtype) for x in streamed]
    if streamed:
        scratch = scratch + [pltpu.SemaphoreType.DMA((len(streamed),))]
    return pl.pallas_call(
        kernel,
        out_shape=outs,
        in_specs=[pl.BlockSpec(memory_space=pltpu.SMEM)] + [whole] * len(operands)
        + [pl.BlockSpec(memory_space=pltpu.HBM)] * len(streamed),
        out_specs=[whole] * len(outs),
        scratch_shapes=scratch,
        compiler_params=pltpu.CompilerParams(vmem_limit_bytes=50 * 1024 * 1024),
        cost_estimate=pl.CostEstimate(flops=flops, bytes_accessed=moved, transcendentals=0),
    )(core, *operands, *streamed)


def layer_update(master, grads, velocity, wsquare, gsquare):
    wnorm = jnp.sqrt(wsquare)
    gnorm = jnp.sqrt(gsquare)
    trust = wnorm / (gnorm + 5e-05 * wnorm)
    new_velocity = 0.9 * velocity + trust * (grads + 5e-05 * master)
    new_master = master - 0.1 * new_velocity
    return (new_master, new_velocity)


def step(
    acts, saved_hidden, grad_out, master_reduce, master_expand, velocity_reduce, velocity_expand
):
    channels = grad_out.shape[1]
    middle = saved_hidden.shape[1]
    inv_c = 1.0 / float(channels) ** 0.5
    inv_m = 1.0 / float(middle) ** 0.5
    half = jax.ShapeDtypeStruct((16, 8, channels // 256, middle), BF)
    whole = pltpu.VMEM((channels, middle), BF)
    flops = 2 * grad_out.size * middle

    cur = jnp.stack([master_expand.astype(BF), master_reduce.astype(BF)])
    along_z = everywhere(cur, "z")
    mine = everywhere(along_z[:, 0], ("y", "x"))
    keep_e, send_e = local_call(
        functools.partial(expand_kernel, inv_m), (grad_out, saved_hidden), (half, half), [], flops
    )
    other = from_other_core(mine)
    mine_reduce = everywhere(along_z[:, 1], ("y", "x"))
    grad_hidden, keep_r, send_r = local_call(
        functools.partial(hidden_kernel, inv_m, inv_c),
        (saved_hidden, mine, other),
        (jax.ShapeDtypeStruct(saved_hidden.shape, BF), half, half),
        [whole],
        2 * flops,
        (grad_out, acts),
    )
    halves = chip_sum(keep_e, from_other_core(send_e), keep_r, from_other_core(send_r))
    halves, mine_reduce = lax.optimization_barrier((halves, mine_reduce))
    arrived = exchange(halves, ("y", "x"))
    over_plane = jnp.sum(arrived.astype(F32), axis=0).astype(BF)
    arrived = exchange(over_plane.transpose(1, 0, 2, 3), "z")
    grads = jnp.sum(arrived.astype(F32), axis=0)
    g_expand, g_reduce = grads[0], grads[1]

    other_reduce = from_other_core(mine_reduce)
    (grad_in,) = local_call(
        functools.partial(back_kernel, inv_c),
        (grad_out, grad_hidden, mine_reduce, other_reduce),
        (jax.ShapeDtypeStruct(grad_out.shape, BF),),
        [whole],
        flops,
    )

    squares = jnp.stack(
        [
            jnp.sum(master_expand * master_expand),
            jnp.sum(g_expand * g_expand),
            jnp.sum(master_reduce * master_reduce),
            jnp.sum(g_reduce * g_reduce),
        ]
    )
    squares = everywhere(squares[None], ("z", "y")).sum(axis=0)
    squares = everywhere(squares, ("c", "x")).sum(axis=0)[0]
    new_mr, new_vr = layer_update(master_reduce, g_reduce, velocity_reduce, squares[2], squares[3])
    new_me, new_ve = layer_update(master_expand, g_expand, velocity_expand, squares[0], squares[1])
    work = jnp.stack([new_me.astype(BF), new_mr.astype(BF)])
    along_z = everywhere(work, "z")
    mine = everywhere(along_z, ("y", "x"))
    parts = both_cores(mine)
    work_expand = whole_rows(parts[:, :, :, 0])
    work_reduce = whole_rows(parts[:, :, :, 1])
    return (grad_in, new_mr, new_me, new_vr, new_ve, work_reduce, work_expand)


def solution(mesh):
    finer = Mesh(mesh.devices.reshape(8, 4, 2, 4), ROWS_OVER)
    split = P(ROWS_OVER, None)
    return jax.shard_map(
        step,
        mesh=finer,
        in_specs=(split,) * 7,
        out_specs=(split,) * 5 + (P(), P()),
        check_vma=False,
    )
```

time: 221 us -> 217 us (0.982)
  Pallas kernels: 0 us -> 17.3 us
  matrix products: 12.4 us -> 0 us
  waiting for transfers between devices: 19.9 us -> 15 us
  other arithmetic: 13.9 us -> 9.68 us
    pallas_call x0 -> x4, Pallas kernels: none -> 17.3 us  [the longest x3 16.8 us: local_call(): pl.pallas_call(kernel, out_shape=outs, in_specs=[pl.BlockSpec(memory_spac...]
    dot_general x4 -> x0, matrix products: 12.4 us -> none  [the longest x1 4.95 us: step(): lax.dot_general(grad_out, saved_hidden, (((0,), (0,)), ((), ())), preferr...]
    all_to_all x1, waiting for transfers between devices: 14.9 us -> 9.47 us  [exchange(): return lax.all_to_all(parts, axes, 0, 0, tiled=True)]
    unnamed x22 -> x36, local copies, waits for them, and re-layouts: 4.8 us -> 10.1 us
    squeeze x2 -> x0, local copies, waits for them, and re-layouts: 3.44 us -> none  [core_half(): others = lax.dynamic_index_in_dim(parts, 1 - core, 2, keepdims=False)]
    convert_element_type x1 -> x0, local copies, waits for them, and re-layouts: 2.86 us -> none  [step(): reduce_terms = (lax.dot_general(acts, grad_hidden, (((0,), (0,)), ((), ()...]
  transfers between devices with their start and end apart: 6 -> 6, of which waited for: 2 -> 2; matrix products, arithmetic and copies ran while one was open for 12% -> 0% of each run, Pallas kernels for 0% -> 8%
where the time goes in v3:
time: 217 us; the launch traced here: 216 us
  blocking collectives  143 us (66%)
  Pallas kernels  17.3 us (8%)
  local copies, waits for them, and re-layouts  17 us (8%)
  waiting for transfers between devices  15 us (7%)
  starting transfers between devices  10.7 us (5%)
  other arithmetic  9.68 us (4%)
  between operations  3.64 us (2%)
    all_to_all x8, blocking collectives, exchange(): return lax.all_to_all(parts, axes, 0, 0, tiled=True)  143 us
    pallas_call x3, Pallas kernels, local_call(): pl.pallas_call(kernel, out_shape=outs, in_specs=[pl.BlockSpec(memory_spac...  16.8 us
    unnamed x36, local copies, waits for them, and re-layouts  10.1 us
    all_to_all x1, waiting for transfers between devices, exchange(): return lax.all_to_all(parts, axes, 0, 0, tiled=True)  9.47 us
    ppermute x5, starting transfers between devices, from_other_core(): return lax.ppermute(block, 'c', [(0, 1), (1, 0)])  7.09 us
    ppermute x5, waiting for transfers between devices, from_other_core(): return lax.ppermute(block, 'c', [(0, 1), (1, 0)])  5.5 us
  transfers between devices with their start and end apart: 6, of which 2 were waited for; matrix products, arithmetic and copies ran while one was open for 0% of the time, Pallas kernels for 8%

profile of v3, /device:TPU:1, one launch (start us, length us, event | category | flops | bytes accessed | tf_op | source)
XLA Modules:
  0.0 216.0 jit_solution(17126354405172220130)
XLA Ops:
  0.6 0.0 copy-start.10
  0.6 1.4 multiply_reduce_fusion.1
  2.1 16.6 %all_to_all.45 = bf16[8,2,8,512]{3,2,1,0:T(8,128)(2,1)S(1)} all-to-all(bf16[8,2,8,512]{3,2,1,0:T(8,128)(2,1)S(1)} %broadcast_in_dim.18), channel_id=1, replica_groups=mesh['z'=8,'y'=4,'c'=2,'x'=4] {'z'}, dimensions={0} | all-to-all | bytes 262144 | tf_op jit(solution)/shard_map/all_to_all | solution.py:18
  18.7 0.1 broadcast_in_dim.20
  18.8 21.5 %all_to_all.46.mine_ref = bf16[16,8,8,512]{3,2,1,0:T(8,128)(2,1)S(1)} all-to-all(bf16[16,8,8,512]{3,2,1,0:T(8,128)(2,1)S(1)} %broadcast_in_dim.20), channel_id=1, replica_groups=mesh['z'=8,'y'=4,'c'=2,'x'=4] {'y','x'}, dimensions={0} | all-to-all | bytes 2097152 | tf_op jit(solution)/shard_map/all_to_all | solution.py:18
  40.3 0.0 copy-start.13
  40.3 3.3 %collective-permute-start = (bf16[16,8,8,512]{3,2,1,0:T(8,128)(2,1)S(1)}, bf16[16,8,8,512]{3,2,1,0:T(8,128)(2,1)}, u32[]{:S(2)}, u32[]{:S(2)}) collective-permute-start(bf16[16,8,8,512]{3,2,1,0:T(8,128)(2,1)S(1)} %all_to_all.46.mine_ref), channel_id=1, source_target_pairs={{0,4},{4,0},{1,5},{5,1},{2,6},{6,2},{3,7},{7,3},{8,12},{12,8},{9,1... | collective-permute-start | bytes 3145736 | tf_op jit(solution)/shard_map/ppermute | solution.py:27
  43.5 0.0 copy-done.10
  43.6 4.5 %shard_map.127 = (bf16[16,8,8,512]{3,2,1,0:T(8,128)(2,1)S(1)}, bf16[16,8,8,512]{3,2,1,0:T(8,128)(2,1)}) custom-call(s32[1]{0:T(128)} %bitcast.core_ref, bf16[588,2048]{1,0:T(8,128)(2,1)} %grad_ref.3, bf16[588,512]{1,0:T(8,128)(2,1)S(1)} %copy-done.10), custom_call_target="tpu_custom_call" | custom-call | flops 1233125376 | bytes 5107712 | tf_op jit(solution)/shard_map/pallas_call | solution.py:144
  48.0 0.0 copy-done.13
  48.0 0.0 copy-start
  48.0 1.0 copy-done
  49.0 0.4 collective-permute-start.1
  49.4 0.0 collective-permute-done.other_ref
  49.4 7.5 %shard_map.126 = (bf16[588,512]{1,0:T(8,128)(2,1)S(1)}, bf16[16,8,8,512]{3,2,1,0:T(8,128)(2,1)S(1)}, bf16[16,8,8,512]{3,2,1,0:T(8,128)(2,1)}) custom-call(s32[1]{0:T(128)} %bitcast.core_ref, bf16[588,512]{1,0:T(8,128)(2,1)S(1)} %copy-done.10, bf16[16,8,8,512]{3,2,1,0:T(8,128)(2,1)} %copy-done.13, bf16[16,8,8,512]{3,2,1,0:T(8,128)(2,1)} %collective-permute-done.other_ref, ...), custom_call_target="tpu_custom_call" | custom-call | flops 2466250752 | bytes 10215424 | tf_op jit(solution)/shard_map/pallas_call | solution.py:144
  56.9 0.0 copy-start.4
  56.9 1.0 copy-done.4
  57.9 0.0 copy-start.8
  57.9 0.8 copy-done.8
  58.8 0.1 collective-permute-start.2
  58.9 1.1 broadcast_in_dim.22
  60.0 3.7 %all-to-all-start.2 = ((bf16[16,8,8,512]{3,2,1,0:T(8,128)(2,1)}), bf16[16,8,8,512]{3,2,1,0:T(8,128)(2,1)S(1)}, u32[]{:S(2)}, u32[]{:S(2)}) async-start(bf16[16,8,8,512]{3,2,1,0:T(8,128)(2,1)} %broadcast_in_dim.22), calls=%async_computation.2 | async-start | bytes 2097152 | tf_op jit(solution)/shard_map/all_to_all | solution.py:18
  63.6 0.0 collective-permute-done.1.got_e_ref
  63.6 0.0 copy-start.2
  63.6 1.0 copy-done.2
  64.6 0.0 collective-permute-done.2.got_r_ref
  64.6 0.0 copy-start.6
  64.6 1.0 copy-done.6
  65.6 1.2 copy-done.1
  66.8 1.2 copy-done.3
  68.0 1.2 copy-done.5
  69.3 1.2 copy-done.7
  70.5 0.5 shard_map.128
  71.0 9.5 %all-to-all-done.2.mine_ref = bf16[16,8,8,512]{3,2,1,0:T(8,128)(2,1)S(1)} async-done(((bf16[16,8,8,512]{3,2,1,0:T(8,128)(2,1)}), bf16[16,8,8,512]{3,2,1,0:T(8,128)(2,1)S(1)}, u32[]{:S(2)}, u32[]{:S(2)}) %all-to-all-start.2) | async-done | bytes 1048608 | tf_op jit(solution)/shard_map/all_to_all | solution.py:18
  80.4 31.4 %all_to_all.47 = bf16[16,2,8,8,512]{4,3,2,1,0:T(8,128)(2,1)} all-to-all(bf16[16,2,8,8,512]{4,3,2,1,0:T(8,128)(2,1)S(1)} %shard_map.128), channel_id=1, replica_groups=mesh['z'=8,'y'=4,'c'=2,'x'=4] {'y','x'}, dimensions={0} | all-to-all | bytes 4194304 | tf_op jit(solution)/shard_map/all_to_all | solution.py:18
  111.9 1.9 reduce_sum.78
  113.8 10.4 %all_to_all.48 = bf16[8,2,8,512]{3,2,1,0:T(8,128)(2,1)S(1)} all-to-all(bf16[8,2,8,512]{3,2,1,0:T(8,128)(2,1)S(1)} %copy.41), channel_id=1, replica_groups=mesh['z'=8,'y'=4,'c'=2,'x'=4] {'z'}, dimensions={0} | all-to-all | bytes 262144 | tf_op jit(solution)/shard_map/all_to_all | solution.py:18
  124.3 0.6 multiply_reduce_fusion.2
  124.9 2.7 %pad_maximum_fusion.3 = f32[4]{0:T(128)S(1)} fusion(f32[1]{0:T(128)} %bitcast.11, f32[1]{0:T(128)} %bitcast.9, f32[1]{0:T(128)} %bitcast.8, f32[1]{0:T(128)} %bitcast.5), kind=kLoop, calls=%fused_computation.25 | loop fusion | flops 12 | bytes 32 | tf_op jit(solution)/shard_map/stack | solution.py:209
  127.5 11.6 %all_to_all.49 = f32[32,1,4]{2,1,0:T(1,128)S(1)} all-to-all(f32[32,1,4]{2,1,0:T(1,128)S(1)} %broadcast_in_dim.23), channel_id=1, replica_groups=mesh['z'=8,'y'=4,'c'=2,'x'=4] {'z','y'}, dimensions={0} | all-to-all | bytes 1024 | tf_op jit(solution)/shard_map/all_to_all | solution.py:18
  139.1 0.1 reduce_sum.83
  139.2 11.2 %all_to_all.50 = f32[8,1,4]{2,1,0:T(1,128)S(1)} all-to-all(f32[8,1,4]{2,1,0:T(1,128)S(1)} %broadcast_in_dim.24), channel_id=1, replica_groups=mesh['z'=8,'y'=4,'c'=2,'x'=4] {'c','x'}, dimensions={0} | all-to-all | bytes 256 | tf_op jit(solution)/shard_map/all_to_all | solution.py:18
  150.4 0.6 fusion.1
  153.9 0.0 copy-done.14
  153.9 0.0 copy-done.15
  153.9 0.0 copy-done.16
  153.9 0.0 copy-done.17
  153.9 0.6 convert_bitcast_fusion.1
  154.6 10.2 %all_to_all.51 = bf16[8,2,8,512]{3,2,1,0:T(8,128)(2,1)S(1)} all-to-all(bf16[8,2,8,512]{3,2,1,0:T(8,128)(2,1)S(1)} %broadcast_in_dim.50), channel_id=1, replica_groups=mesh['z'=8,'y'=4,'c'=2,'x'=4] {'z'}, dimensions={0} | all-to-all | bytes 262144 | tf_op jit(solution)/shard_map/all_to_all | solution.py:18
  164.8 0.2 broadcast_in_dim.51
  165.0 29.8 %all_to_all.52 = bf16[16,8,2,8,512]{4,3,1,2,0:T(8,128)(2,1)S(1)} all-to-all(bf16[16,8,2,8,512]{4,3,1,2,0:T(8,128)(2,1)S(1)} %broadcast_in_dim.51), channel_id=1, replica_groups=mesh['z'=8,'y'=4,'c'=2,'x'=4] {'y','x'}, dimensions={0} | all-to-all | bytes 4194304 | tf_op jit(solution)/shard_map/all_to_all | solution.py:18
  194.8 1.5 copy.46
  196.3 0.5 copy-done.11
  196.8 3.3 %collective-permute-start.4 = (bf16[16,8,2,8,512]{4,3,1,0,2:T(8,128)(2,1)}, bf16[16,8,2,8,512]{4,3,1,0,2:T(8,128)(2,1)}, u32[]{:S(2)}, u32[]{:S(2)}) collective-permute-start(bf16[16,8,2,8,512]{4,3,1,0,2:T(8,128)(2,1)} %copy.46), channel_id=1, source_target_pairs={{0,4},{4,0},{1,5},{5,1},{2,6},{6,2},{3,7},{7,3},{8,12},{12,8},{9,1... | collective-permute-start | bytes 6291464 | tf_op jit(solution)/shard_map/ppermute | solution.py:27
  200.1 0.0 collective-permute-start.3
  200.1 5.5 %collective-permute-done.3.other_ref = bf16[16,8,8,512]{3,2,1,0:T(8,128)(2,1)S(1)} collective-permute-done((bf16[16,8,8,512]{3,2,1,0:T(8,128)(2,1)S(1)}, bf16[16,8,8,512]{3,2,1,0:T(8,128)(2,1)S(1)}, u32[]{:S(2)}, u32[]{:S(2)}) %collective-permute-start.3) | collective-permute-done | bytes 1048608 | tf_op jit(solution)/shard_map/ppermute | solution.py:27
  205.6 0.0 copy-done.9
  205.6 4.8 %shard_map.129 = bf16[588,2048]{1,0:T(8,128)(2,1)} custom-call(s32[1]{0:T(128)} %bitcast.core_ref, bf16[588,2048]{1,0:T(8,128)(2,1)} %grad_ref.3, bf16[588,512]{1,0:T(8,128)(2,1)S(1)} %copy-done.9, bf16[16,8,8,512]{3,2,1,0:T(8,128)(2,1)S(1)} %all-to-all-done.2.mine_ref, bf16[16,8,8,512]{3,2,1,0:T(8,128)(2,1)S(1)} %collective-permute-done.3.other_ref), custom_call_target="tpu_custom_call" | custom-call | flops 1233125376 | bytes 7516160 | tf_op jit(solution)/shard_map/pallas_call | solution.py:144
  210.4 0.0 collective-permute-done.4
  210.4 0.0 copy-done.12
  210.4 1.9 select_bitcast_fusion
  212.3 0.4 pad_maximum_fusion
  212.7 1.6 copy.49
  214.4 1.6 copy.50
  (22 shorter events, 0.1 us)
Async XLA Ops:
  0.6 42.9 %copy-start.10 = (bf16[588,512]{1,0:T(8,128)(2,1)S(1)}, bf16[588,512]{1,0:T(8,128)(2,1)}, u32[]{:S(2)}) copy-start(bf16[588,512]{1,0:T(8,128)(2,1)} %hidden_ref.1) | copy-start | bytes 1806340
  40.3 7.8 %copy-start.13 = (bf16[16,8,8,512]{3,2,1,0:T(8,128)(2,1)}, bf16[16,8,8,512]{3,2,1,0:T(8,128)(2,1)S(1)}, u32[]{:S(2)}) copy-start(bf16[16,8,8,512]{3,2,1,0:T(8,128)(2,1)S(1)} %all_to_all.46.mine_ref) | copy-start | bytes 3145732
  40.3 9.1 %collective-permute-start = (bf16[16,8,8,512]{3,2,1,0:T(8,128)(2,1)S(1)}, bf16[16,8,8,512]{3,2,1,0:T(8,128)(2,1)}, u32[]{:S(2)}, u32[]{:S(2)}) collective-permute-start(bf16[16,8,8,512]{3,2,1,0:T(8,128)(2,1)S(1)} %all_to_all.46.mine_ref), channel_id=1, source_target_pairs={{0,4},{4,0},{1,5},{5,1},{2,6},{6,2},{3,7},{7,3},{8,12},{12,8},{9,1... | collective-permute-start | bytes 3145736 | tf_op jit(solution)/shard_map/ppermute | solution.py:27
  48.0 1.0 copy-start
  49.0 14.6 %collective-permute-start.1 = (bf16[16,8,8,512]{3,2,1,0:T(8,128)(2,1)}, bf16[16,8,8,512]{3,2,1,0:T(8,128)(2,1)S(1)}, u32[]{:S(2)}, u32[]{:S(2)}) collective-permute-start(bf16[16,8,8,512]{3,2,1,0:T(8,128)(2,1)} %get-tuple-element.16), channel_id=1, source_target_pairs={{0,4},{4,0},{1,5},{5,1},{2,6},{6,2},{3,7},{7,3},{8,12},{12,8},{9,1... | collective-permute-start | bytes 3145736 | tf_op jit(solution)/shard_map/ppermute | solution.py:27
  56.9 1.0 copy-start.4
  57.9 0.8 copy-start.8
  58.8 5.8 %collective-permute-start.2 = (bf16[16,8,8,512]{3,2,1,0:T(8,128)(2,1)}, bf16[16,8,8,512]{3,2,1,0:T(8,128)(2,1)S(1)}, u32[]{:S(2)}, u32[]{:S(2)}) collective-permute-start(bf16[16,8,8,512]{3,2,1,0:T(8,128)(2,1)} %get-tuple-element.18), channel_id=1, source_target_pairs={{0,4},{4,0},{1,5},{5,1},{2,6},{6,2},{3,7},{7,3},{8,12},{12,8},{9,1... | collective-permute-start | bytes 3145736 | tf_op jit(solution)/shard_map/ppermute | solution.py:27
  60.0 20.5 %all-to-all-start.2 = ((bf16[16,8,8,512]{3,2,1,0:T(8,128)(2,1)}), bf16[16,8,8,512]{3,2,1,0:T(8,128)(2,1)S(1)}, u32[]{:S(2)}, u32[]{:S(2)}) async-start(bf16[16,8,8,512]{3,2,1,0:T(8,128)(2,1)} %broadcast_in_dim.22), calls=%async_computation.2 | async-start | bytes 2097152 | tf_op jit(solution)/shard_map/all_to_all | solution.py:18
  63.6 1.0 copy-start.2
  64.6 1.0 copy-start.6
  65.6 1.2 copy-start.1
  66.8 1.2 copy-start.3
  68.0 1.2 copy-start.5
  69.3 1.2 copy-start.7
  111.8 42.0 %copy-start.14 = (f32[8,512]{1,0:T(8,128)S(1)}, f32[8,512]{1,0:T(8,128)}, u32[]{:S(2)}) copy-start(f32[8,512]{1,0:T(8,128)} %param.10) | copy-start | bytes 49156
  111.8 42.0 %copy-start.15 = (f32[8,512]{1,0:T(8,128)S(1)}, f32[8,512]{1,0:T(8,128)}, u32[]{:S(2)}) copy-start(f32[8,512]{1,0:T(8,128)} %param.11) | copy-start | bytes 49156
  111.9 42.0 %copy-start.16 = (f32[8,512]{1,0:T(8,128)S(1)}, f32[8,512]{1,0:T(8,128)}, u32[]{:S(2)}) copy-start(f32[8,512]{1,0:T(8,128)} %param.13) | copy-start | bytes 49156
  111.9 42.0 %copy-start.17 = (f32[8,512]{1,0:T(8,128)S(1)}, f32[8,512]{1,0:T(8,128)}, u32[]{:S(2)}) copy-start(f32[8,512]{1,0:T(8,128)} %param.12) | copy-start | bytes 49156
  194.8 2.0 copy-start.11
  194.8 10.8 %copy-start.9 = (bf16[588,512]{1,0:T(8,128)(2,1)S(1)}, bf16[588,512]{1,0:T(8,128)(2,1)}, u32[]{:S(2)}) copy-start(bf16[588,512]{1,0:T(8,128)(2,1)} %copy-done.8) | copy-start | bytes 1806340
  196.8 13.6 %collective-permute-start.4 = (bf16[16,8,2,8,512]{4,3,1,0,2:T(8,128)(2,1)}, bf16[16,8,2,8,512]{4,3,1,0,2:T(8,128)(2,1)}, u32[]{:S(2)}, u32[]{:S(2)}) collective-permute-start(bf16[16,8,2,8,512]{4,3,1,0,2:T(8,128)(2,1)} %copy.46), channel_id=1, source_target_pairs={{0,4},{4,0},{1,5},{5,1},{2,6},{6,2},{3,7},{7,3},{8,12},{12,8},{9,1... | collective-permute-start | bytes 6291464 | tf_op jit(solution)/shard_map/ppermute | solution.py:27
  200.1 5.5 %collective-permute-start.3 = (bf16[16,8,8,512]{3,2,1,0:T(8,128)(2,1)S(1)}, bf16[16,8,8,512]{3,2,1,0:T(8,128)(2,1)S(1)}, u32[]{:S(2)}, u32[]{:S(2)}) collective-permute-start(bf16[16,8,8,512]{3,2,1,0:T(8,128)(2,1)S(1)} %all-to-all-done.2.mine_ref), channel_id=1, source_target_pairs={{0,4},{4,0},{1,5},{5,1},{2,6},{6,2},{3,7},{7,3},{8,12},{12,8},{9,1... | collective-permute-start | bytes 3145736 | tf_op jit(solution)/shard_map/ppermute | solution.py:27
  205.6 4.8 %copy-start.12 = (bf16[16,8,2,8,512]{4,3,1,2,0:T(8,128)(2,1)S(1)}, bf16[16,8,2,8,512]{4,3,1,2,0:T(8,128)(2,1)}, u32[]{:S(2)}) copy-start(bf16[16,8,2,8,512]{4,3,1,2,0:T(8,128)(2,1)} %copy-done.11) | copy-start | bytes 6291460

commit v4 on v3

--- a/solution.py
+++ b/solution.py
@@ -25,20 +25,6 @@
 
 def from_other_core(block):
     return lax.ppermute(block, "c", [(0, 1), (1, 0)])
-
-
-def both_cores(block):
-    core = lax.axis_index("c")
-    other = from_other_core(block)
-    first = jnp.where(core == 0, block, other)
-    second = jnp.where(core == 0, other, block)
-    return jnp.stack([first, second])
-
-
-def whole_rows(parts):
-    c, yx, z, r, n = parts.shape
-    parts = parts.reshape(c, 4, 4, z, r, n)
-    return parts.transpose(3, 1, 0, 2, 4, 5).reshape(c * yx * z * r, n)
 
 
 def fill_weights(core, mine_ref, other_ref, whole_ref):
@@ -153,13 +139,134 @@
     )(core, *operands, *streamed)
 
 
-def layer_update(master, grads, velocity, wsquare, gsquare):
-    wnorm = jnp.sqrt(wsquare)
-    gnorm = jnp.sqrt(gsquare)
-    trust = wnorm / (gnorm + 5e-05 * wnorm)
-    new_velocity = 0.9 * velocity + trust * (grads + 5e-05 * master)
-    new_master = master - 0.1 * new_velocity
-    return (new_master, new_velocity)
+def total_of(terms):
+    return jnp.sum(jnp.sum(terms, axis=1, keepdims=True), axis=0, keepdims=True)
+
+
+def owner_kernel(arrived_ref, me_ref, mr_ref, ve_ref, vr_ref, grads_ref, out_ref):
+    tiles, squares = [], []
+    moved = []
+    for layer, (m_ref, v_ref) in enumerate(((me_ref, ve_ref), (mr_ref, vr_ref))):
+        grads = arrived_ref[0, layer].astype(F32)
+        for z in range(1, 8):
+            grads = grads + arrived_ref[z, layer].astype(F32)
+        grads_ref[layer] = grads
+        master = m_ref[...]
+        tiles.append((grads + 5e-05 * master).astype(BF))
+        moved.append((master - 0.1 * (0.9 * v_ref[...])).astype(BF))
+        squares += [total_of(master * master), total_of(grads * grads)]
+    tiles += moved
+    rows = lax.broadcasted_iota(jnp.int32, (8, 128), 0)
+    left = jnp.zeros((8, 128), F32)
+    for at, square in enumerate(squares):
+        left = jnp.where(rows == at, square, left)
+    parts = []
+    for _ in range(3):
+        part = left.astype(BF)
+        left = left - part.astype(F32)
+        parts.append(part)
+    tiles.append(jnp.concatenate(parts + [jnp.zeros((8, 128), BF)], axis=1))
+    for z in range(8):
+        for at, tile in enumerate(tiles):
+            out_ref[z, at] = tile
+
+
+def ring_squares_kernel(ring_ref, out_ref):
+    total = jnp.zeros((8, 128), F32)
+    for z in range(8):
+        packed = ring_ref[z, 4].astype(F32)
+        total = total + ((packed[:, :128] + packed[:, 128:256]) + packed[:, 256:384])
+    out_ref[...] = jnp.broadcast_to(total[None], out_ref.shape)
+
+
+def update_kernel(
+    squares_ref,
+    ring_ref,
+    grads_ref,
+    me_ref,
+    mr_ref,
+    ve_ref,
+    vr_ref,
+    new_me_ref,
+    new_mr_ref,
+    new_ve_ref,
+    new_vr_ref,
+    work_ref,
+):
+    squares = squares_ref[0]
+    for peer in range(1, squares_ref.shape[0]):
+        squares = squares + squares_ref[peer]
+    norms = jnp.sqrt(squares)
+    layers = (
+        (me_ref, ve_ref, new_me_ref, new_ve_ref),
+        (mr_ref, vr_ref, new_mr_ref, new_vr_ref),
+    )
+    for layer, (m_ref, v_ref, new_m_ref, new_v_ref) in enumerate(layers):
+        wnorm = norms[2 * layer : 2 * layer + 1, :1]
+        gnorm = norms[2 * layer + 1 : 2 * layer + 2, :1]
+        trust = wnorm / (gnorm + 5e-05 * wnorm)
+        master = m_ref[...]
+        new_velocity = 0.9 * v_ref[...] + trust * (grads_ref[layer] + 5e-05 * master)
+        new_v_ref[...] = new_velocity
+        new_m_ref[...] = master - 0.1 * new_velocity
+        for z in range(8):
+            step = 0.1 * (trust * ring_ref[z, layer].astype(F32))
+            work_ref[z, layer] = (ring_ref[z, 2 + layer].astype(F32) - step).astype(BF)
+
+
+def small_call(kernel, operands, outs):
+    whole = pl.BlockSpec(memory_space=pltpu.VMEM)
+    moved = sum(x.size * x.dtype.itemsize for x in (*operands, *outs))
+    return pl.pallas_call(
+        kernel,
+        out_shape=outs,
+        in_specs=[whole] * len(operands),
+        out_specs=[whole] * len(outs),
+        compiler_params=pltpu.CompilerParams(vmem_limit_bytes=16 * 1024 * 1024),
+        cost_estimate=pl.CostEstimate(flops=moved, bytes_accessed=moved, transcendentals=0),
+    )(*operands)
+
+
+def place_kernel(core_ref, parts_ref, *refs):
+    expand_ref, reduce_ref, sems = refs[-3:]
+    core = core_ref[0]
+    copies = []
+    for y in range(4):
+        for x in range(4):
+            for layer, out_ref in enumerate((expand_ref, reduce_ref)):
+                copies.append(
+                    pltpu.make_async_copy(
+                        parts_ref.at[y * 4 + x, :, layer],
+                        out_ref.at[:, y, core, x],
+                        sems.at[len(copies)],
+                    )
+                )
+    for copy in copies:
+        copy.start()
+    for copy in copies:
+        copy.wait()
+
+
+def place(core, parts, into):
+    _, z, _, r, n = parts.shape
+    whole = jax.ShapeDtypeStruct((z, 4, 2, 4, r, n), BF)
+    hbm = pl.BlockSpec(memory_space=pl.ANY)
+    return pl.pallas_call(
+        place_kernel,
+        out_shape=(whole, whole),
+        in_specs=[
+            pl.BlockSpec(memory_space=pltpu.SMEM),
+            pl.BlockSpec(memory_space=pltpu.VMEM),
+        ]
+        + [hbm] * len(into),
+        out_specs=(hbm, hbm),
+        scratch_shapes=[pltpu.SemaphoreType.DMA((32,))],
+        input_output_aliases={2 + at: at for at in range(len(into))},
+        compiler_params=pltpu.CompilerParams(vmem_limit_bytes=8 * 1024 * 1024),
+        cost_estimate=pl.CostEstimate(
+            flops=parts.size, bytes_accessed=4 * parts.size, transcendentals=0
+        ),
+    )(core.astype(jnp.int32).reshape(1), parts, *into)
 
 
 def step(
@@ -194,9 +301,6 @@
     arrived = exchange(halves, ("y", "x"))
     over_plane = jnp.sum(arrived.astype(F32), axis=0).astype(BF)
     arrived = exchange(over_plane.transpose(1, 0, 2, 3), "z")
-    grads = jnp.sum(arrived.astype(F32), axis=0)
-    g_expand, g_reduce = grads[0], grads[1]
-
     other_reduce = from_other_core(mine_reduce)
     (grad_in,) = local_call(
         functools.partial(back_kernel, inv_c),
@@ -206,24 +310,32 @@
         flops,
     )
 
-    squares = jnp.stack(
-        [
-            jnp.sum(master_expand * master_expand),
-            jnp.sum(g_expand * g_expand),
-            jnp.sum(master_reduce * master_reduce),
-            jnp.sum(g_reduce * g_reduce),
-        ]
-    )
-    squares = everywhere(squares[None], ("z", "y")).sum(axis=0)
-    squares = everywhere(squares, ("c", "x")).sum(axis=0)[0]
-    new_mr, new_vr = layer_update(master_reduce, g_reduce, velocity_reduce, squares[2], squares[3])
-    new_me, new_ve = layer_update(master_expand, g_expand, velocity_expand, squares[0], squares[1])
-    work = jnp.stack([new_me.astype(BF), new_mr.astype(BF)])
-    along_z = everywhere(work, "z")
-    mine = everywhere(along_z, ("y", "x"))
-    parts = both_cores(mine)
-    work_expand = whole_rows(parts[:, :, :, 0])
-    work_reduce = whole_rows(parts[:, :, :, 1])
+    state = (master_expand, master_reduce, velocity_expand, velocity_reduce)
+    own = jax.ShapeDtypeStruct(master_expand.shape, F32)
+    grads, rows = small_call(
+        owner_kernel,
+        (arrived, *state),
+        (
+            jax.ShapeDtypeStruct((2, *own.shape), F32),
+            jax.ShapeDtypeStruct((8, 5, *own.shape), BF),
+        ),
+    )
+    ring = exchange(rows, "z")
+    (squares,) = small_call(
+        ring_squares_kernel, (ring,), (jax.ShapeDtypeStruct((32, 8, 128), F32),)
+    )
+    squares = exchange(squares, ("y", "c", "x"))
+    new_me, new_mr, new_ve, new_vr, work = small_call(
+        update_kernel,
+        (squares, ring, grads, *state),
+        (own, own, own, own, jax.ShapeDtypeStruct((8, 2, *own.shape), BF)),
+    )
+    mine = everywhere(work, ("y", "x"))
+    core = lax.axis_index("c")
+    other = from_other_core(mine)
+    placed = place(core, mine, ())
+    placed = place(1 - core, other, placed)
+    work_expand, work_reduce = (p.reshape(channels, middle) for p in placed)
     return (grad_in, new_mr, new_me, new_vr, new_ve, work_reduce, work_expand)
 
 

time: 217 us -> 201 us (0.926)
  other arithmetic: 9.68 us -> 2.76 us
  Pallas kernels: 17.3 us -> 23 us
  blocking collectives: 143 us -> 138 us
  local copies, waits for them, and re-layouts: 17 us -> 12.2 us
  between operations: 3.64 us -> 0.77 us
    pallas_call x0 -> x5, Pallas kernels: none -> 5.61 us  [the longest x2 4.73 us: place(): pl.pallas_call(place_kernel, out_shape=(whole, whole), in_specs=[pl.Block...]
    another operation x5 -> x0, other arithmetic: 5.58 us -> none  [the longest x1 2.66 us: step(): jnp.stack([jnp.sum(master_expand * master_expand), jnp.sum(g_expand * g_e...]
    all_to_all x8 -> x7, blocking collectives: 143 us -> 138 us  [exchange(): return lax.all_to_all(parts, axes, 0, 0, tiled=True)]
    transpose x3 -> x0, local copies, waits for them, and re-layouts: 3.27 us -> none  [the longest x2 3.26 us: whole_rows(): return parts.transpose(3, 1, 0, 2, 4, 5).reshape(c * yx * z * r, n)]
    unnamed x36 -> x32, local copies, waits for them, and re-layouts: 10.1 us -> 10.7 us
  transfers between devices with their start and end apart: 6 -> 6, of which waited for: 2 -> 2; matrix products, arithmetic and copies ran while one was open for 0% -> 1% of each run, Pallas kernels for 8% -> 9%
where the time goes in v4:
time: 201 us
  blocking collectives  138 us (69%)
  Pallas kernels  23 us (11%)
  waiting for transfers between devices  14.9 us (7%)
  local copies, waits for them, and re-layouts  12.2 us (6%)
  starting transfers between devices  9.42 us (5%)
  other arithmetic  2.76 us (1%)
    all_to_all x7, blocking collectives, exchange(): return lax.all_to_all(parts, axes, 0, 0, tiled=True)  138 us
    pallas_call x3, Pallas kernels, local_call(): pl.pallas_call(kernel, out_shape=outs, in_specs=[pl.BlockSpec(memory_spac...  16.9 us
    unnamed x32, local copies, waits for them, and re-layouts  10.7 us
    all_to_all x1, waiting for transfers between devices, exchange(): return lax.all_to_all(parts, axes, 0, 0, tiled=True)  9.47 us
    ppermute x5, starting transfers between devices, from_other_core(): return lax.ppermute(block, 'c', [(0, 1), (1, 0)])  5.76 us
    ppermute x5, waiting for transfers between devices, from_other_core(): return lax.ppermute(block, 'c', [(0, 1), (1, 0)])  5.42 us
    pallas_call x2, Pallas kernels, place(): pl.pallas_call(place_kernel, out_shape=(whole, whole), in_specs=[pl.Block...  4.73 us
  transfers between devices with their start and end apart: 6, of which 2 were waited for; matrix products, arithmetic and copies ran while one was open for 1% of the time, Pallas kernels for 9%

profile of v4, /device:TPU:1, one launch (start us, length us, event | category | flops | bytes accessed | tf_op | source)
XLA Modules:
  0.0 200.6 jit_solution(10094871732406675094)
XLA Ops:
  0.6 0.0 copy-start.14
  0.6 0.8 convert_bitcast_fusion
  1.5 16.6 %all_to_all.40 = bf16[8,2,8,512]{3,2,1,0:T(8,128)(2,1)S(1)} all-to-all(bf16[8,2,8,512]{3,2,1,0:T(8,128)(2,1)S(1)} %broadcast_in_dim.12), channel_id=1, replica_groups=mesh['z'=8,'y'=4,'c'=2,'x'=4] {'z'}, dimensions={0} | all-to-all | bytes 262144 | tf_op jit(solution)/shard_map/all_to_all | solution.py:18
  18.0 0.1 broadcast_in_dim.28
  18.1 21.5 %all_to_all.41.mine_ref = bf16[16,8,8,512]{3,2,1,0:T(8,128)(2,1)S(1)} all-to-all(bf16[16,8,8,512]{3,2,1,0:T(8,128)(2,1)S(1)} %broadcast_in_dim.28), channel_id=1, replica_groups=mesh['z'=8,'y'=4,'c'=2,'x'=4] {'y','x'}, dimensions={0} | all-to-all | bytes 2097152 | tf_op jit(solution)/shard_map/all_to_all | solution.py:18
  39.6 0.0 copy-start.15
  39.6 3.3 %collective-permute-start = (bf16[16,8,8,512]{3,2,1,0:T(8,128)(2,1)S(1)}, bf16[16,8,8,512]{3,2,1,0:T(8,128)(2,1)}, u32[]{:S(2)}, u32[]{:S(2)}) collective-permute-start(bf16[16,8,8,512]{3,2,1,0:T(8,128)(2,1)S(1)} %all_to_all.41.mine_ref), channel_id=1, source_target_pairs={{0,4},{4,0},{1,5},{5,1},{2,6},{6,2},{3,7},{7,3},{8,12},{12,8},{9,1... | collective-permute-start | bytes 3145736 | tf_op jit(solution)/shard_map/ppermute | solution.py:27
  42.9 0.0 copy-done.14
  42.9 4.5 %shard_map.127 = (bf16[16,8,8,512]{3,2,1,0:T(8,128)(2,1)S(1)}, bf16[16,8,8,512]{3,2,1,0:T(8,128)(2,1)}) custom-call(s32[1]{0:T(128)} %bitcast.core_ref, bf16[588,2048]{1,0:T(8,128)(2,1)} %grad_ref.3, bf16[588,512]{1,0:T(8,128)(2,1)S(1)} %copy-done.14), custom_call_target="tpu_custom_call" | custom-call | flops 1233125376 | bytes 5107712 | tf_op jit(solution)/shard_map/pallas_call | solution.py:130
  47.4 0.0 copy-done.15
  47.4 0.0 copy-start
  47.4 1.0 copy-done
  48.4 0.4 collective-permute-start.1
  48.8 0.0 collective-permute-done.other_ref
  48.8 7.5 %shard_map.126 = (bf16[588,512]{1,0:T(8,128)(2,1)S(1)}, bf16[16,8,8,512]{3,2,1,0:T(8,128)(2,1)S(1)}, bf16[16,8,8,512]{3,2,1,0:T(8,128)(2,1)}) custom-call(s32[1]{0:T(128)} %bitcast.core_ref, bf16[588,512]{1,0:T(8,128)(2,1)S(1)} %copy-done.14, bf16[16,8,8,512]{3,2,1,0:T(8,128)(2,1)} %copy-done.15, bf16[16,8,8,512]{3,2,1,0:T(8,128)(2,1)} %collective-permute-done.other_ref, ...), custom_call_target="tpu_custom_call" | custom-call | flops 2466250752 | bytes 10215424 | tf_op jit(solution)/shard_map/pallas_call | solution.py:130
  56.3 0.0 copy-start.4
  56.3 0.9 copy-done.4
  57.3 0.0 copy-start.8
  57.3 0.8 copy-done.8
  58.1 0.1 collective-permute-start.2
  58.2 1.1 broadcast_in_dim.30
  59.3 3.7 %all-to-all-start.2 = ((bf16[16,8,8,512]{3,2,1,0:T(8,128)(2,1)}), bf16[16,8,8,512]{3,2,1,0:T(8,128)(2,1)S(1)}, u32[]{:S(2)}, u32[]{:S(2)}) async-start(bf16[16,8,8,512]{3,2,1,0:T(8,128)(2,1)} %broadcast_in_dim.30), calls=%async_computation.2 | async-start | bytes 2097152 | tf_op jit(solution)/shard_map/all_to_all | solution.py:18
  63.0 0.0 collective-permute-done.1.got_e_ref
  63.0 0.0 copy-start.2
  63.0 1.0 copy-done.2
  63.9 0.0 collective-permute-done.2.got_r_ref
  63.9 0.0 copy-start.6
  63.9 1.0 copy-done.6
  64.9 0.0 copy-start.1
  64.9 1.2 copy-done.1
  66.1 0.0 copy-start.3
  66.1 1.2 copy-done.3
  67.4 0.0 copy-start.5
  67.4 1.2 copy-done.5
  68.6 0.0 copy-start.7
  68.6 1.2 copy-done.7
  69.8 0.5 shard_map.128
  70.3 9.5 %all-to-all-done.2.mine_ref = bf16[16,8,8,512]{3,2,1,0:T(8,128)(2,1)S(1)} async-done(((bf16[16,8,8,512]{3,2,1,0:T(8,128)(2,1)}), bf16[16,8,8,512]{3,2,1,0:T(8,128)(2,1)S(1)}, u32[]{:S(2)}, u32[]{:S(2)}) %all-to-all-start.2) | async-done | bytes 1048608 | tf_op jit(solution)/shard_map/all_to_all | solution.py:18
  79.8 31.5 %all_to_all.42 = bf16[16,2,8,8,512]{4,3,2,1,0:T(8,128)(2,1)} all-to-all(bf16[16,2,8,8,512]{4,3,2,1,0:T(8,128)(2,1)S(1)} %shard_map.128), channel_id=1, replica_groups=mesh['z'=8,'y'=4,'c'=2,'x'=4] {'y','x'}, dimensions={0} | all-to-all | bytes 4194304 | tf_op jit(solution)/shard_map/all_to_all | solution.py:18
  111.2 0.0 copy-start.10
  111.2 0.0 copy-start.11
  111.2 0.0 copy-start.12
  111.3 0.0 copy-start.13
  111.3 1.9 reduce_sum.12
  113.2 10.4 %all_to_all.43.arrived_ref = bf16[8,2,8,512]{3,2,1,0:T(8,128)(2,1)S(1)} all-to-all(bf16[8,2,8,512]{3,2,1,0:T(8,128)(2,1)S(1)} %bitcast.17), channel_id=1, replica_groups=mesh['z'=8,'y'=4,'c'=2,'x'=4] {'z'}, dimensions={0} | all-to-all | bytes 262144 | tf_op jit(solution)/shard_map/all_to_all | solution.py:18
  123.6 0.0 copy-done.10
  123.6 0.0 copy-done.11
  123.6 0.0 copy-done.12
  123.6 0.0 copy-done.13
  123.7 0.1 shard_map.130
  123.8 12.4 %all_to_all.44.ring_ref = bf16[8,5,8,512]{3,2,1,0:T(8,128)(2,1)S(1)} all-to-all(bf16[8,5,8,512]{3,2,1,0:T(8,128)(2,1)S(1)} %get-tuple-element.32), channel_id=1, replica_groups=mesh['z'=8,'y'=4,'c'=2,'x'=4] {'z'}, dimensions={0} | all-to-all | bytes 655360 | tf_op jit(solution)/shard_map/all_to_all | solution.py:18
  136.2 15.2 %all_to_all.45.squares_ref = f32[32,8,128]{2,1,0:T(8,128)S(1)} all-to-all(f32[32,8,128]{2,1,0:T(8,128)S(1)} %shard_map.131), channel_id=1, replica_groups=mesh['z'=8,'y'=4,'c'=2,'x'=4] {'y','c','x'}, dimensions={0} | all-to-all | bytes 262144 | tf_op jit(solution)/shard_map/all_to_all | solution.py:18
  151.4 0.7 shard_map.132
  152.1 0.2 broadcast_in_dim.31
  152.4 30.0 %all_to_all.46.parts_ref = bf16[16,8,2,8,512]{4,3,2,1,0:T(8,128)(2,1)S(1)} all-to-all(bf16[16,8,2,8,512]{4,3,2,1,0:T(8,128)(2,1)S(1)} %broadcast_in_dim.31), channel_id=1, replica_groups=mesh['z'=8,'y'=4,'c'=2,'x'=4] {'y','x'}, dimensions={0} | all-to-all | bytes 4194304 | tf_op jit(solution)/shard_map/all_to_all | solution.py:18
  182.4 2.0 collective-permute-start.4
  184.4 0.0 collective-permute-start.3
  184.4 5.4 %collective-permute-done.3.other_ref = bf16[16,8,8,512]{3,2,1,0:T(8,128)(2,1)} collective-permute-done((bf16[16,8,8,512]{3,2,1,0:T(8,128)(2,1)S(1)}, bf16[16,8,8,512]{3,2,1,0:T(8,128)(2,1)}, u32[]{:S(2)}, u32[]{:S(2)}) %collective-permute-start.3) | collective-permute-done | bytes 1048608 | tf_op jit(solution)/shard_map/ppermute | solution.py:27
  189.8 0.0 copy-start.9
  189.8 1.1 copy-done.9
  190.9 5.0 %shard_map.129 = bf16[588,2048]{1,0:T(8,128)(2,1)} custom-call(s32[1]{0:T(128)} %bitcast.core_ref, bf16[588,2048]{1,0:T(8,128)(2,1)} %grad_ref.3, bf16[588,512]{1,0:T(8,128)(2,1)S(1)} %copy-done.9, bf16[16,8,8,512]{3,2,1,0:T(8,128)(2,1)S(1)} %all-to-all-done.2.mine_ref, bf16[16,8,8,512]{3,2,1,0:T(8,128)(2,1)} %collective-permute-done.3.other_ref), custom_call_target="tpu_custom_call" | custom-call | flops 1233125376 | bytes 7516160 | tf_op jit(solution)/shard_map/pallas_call | solution.py:130
  195.8 1.6 shard_map.133
  197.4 0.0 collective-permute-done.4.parts_ref
  197.4 3.2 %shard_map.134 = (bf16[8,4,2,4,8,512]{5,4,3,2,1,0:T(8,128)(2,1)}, bf16[8,4,2,4,8,512]{5,4,3,2,1,0:T(8,128)(2,1)}) custom-call(s32[1]{0:T(128)} %bitcast.6.core_ref, bf16[16,8,2,8,512]{4,3,2,1,0:T(8,128)(2,1)} %collective-permute-done.4.parts_ref, ...), custom_call_target="tpu_custom_call", output_to_operand_aliasing={{0}: (2, {}), {1}: (3, {})} | custom-call | flops 1048576 | bytes 4194304 | tf_op jit(solution)/shard_map/pallas_call | solution.py:254
  (5 shorter events, 0.1 us)
Async XLA Ops:
  0.6 42.3 %copy-start.14 = (bf16[588,512]{1,0:T(8,128)(2,1)S(1)}, bf16[588,512]{1,0:T(8,128)(2,1)}, u32[]{:S(2)}) copy-start(bf16[588,512]{1,0:T(8,128)(2,1)} %hidden_ref.1) | copy-start | bytes 1806340
  39.6 7.8 %copy-start.15 = (bf16[16,8,8,512]{3,2,1,0:T(8,128)(2,1)}, bf16[16,8,8,512]{3,2,1,0:T(8,128)(2,1)S(1)}, u32[]{:S(2)}) copy-start(bf16[16,8,8,512]{3,2,1,0:T(8,128)(2,1)S(1)} %all_to_all.41.mine_ref) | copy-start | bytes 3145732
  39.6 9.2 %collective-permute-start = (bf16[16,8,8,512]{3,2,1,0:T(8,128)(2,1)S(1)}, bf16[16,8,8,512]{3,2,1,0:T(8,128)(2,1)}, u32[]{:S(2)}, u32[]{:S(2)}) collective-permute-start(bf16[16,8,8,512]{3,2,1,0:T(8,128)(2,1)S(1)} %all_to_all.41.mine_ref), channel_id=1, source_target_pairs={{0,4},{4,0},{1,5},{5,1},{2,6},{6,2},{3,7},{7,3},{8,12},{12,8},{9,1... | collective-permute-start | bytes 3145736 | tf_op jit(solution)/shard_map/ppermute | solution.py:27
  47.4 1.0 copy-start
  48.4 14.5 %collective-permute-start.1 = (bf16[16,8,8,512]{3,2,1,0:T(8,128)(2,1)}, bf16[16,8,8,512]{3,2,1,0:T(8,128)(2,1)S(1)}, u32[]{:S(2)}, u32[]{:S(2)}) collective-permute-start(bf16[16,8,8,512]{3,2,1,0:T(8,128)(2,1)} %get-tuple-element.27), channel_id=1, source_target_pairs={{0,4},{4,0},{1,5},{5,1},{2,6},{6,2},{3,7},{7,3},{8,12},{12,8},{9,1... | collective-permute-start | bytes 3145736 | tf_op jit(solution)/shard_map/ppermute | solution.py:27
  56.3 1.0 copy-start.4
  57.3 0.8 copy-start.8
  58.1 5.8 %collective-permute-start.2 = (bf16[16,8,8,512]{3,2,1,0:T(8,128)(2,1)}, bf16[16,8,8,512]{3,2,1,0:T(8,128)(2,1)S(1)}, u32[]{:S(2)}, u32[]{:S(2)}) collective-permute-start(bf16[16,8,8,512]{3,2,1,0:T(8,128)(2,1)} %get-tuple-element.29), channel_id=1, source_target_pairs={{0,4},{4,0},{1,5},{5,1},{2,6},{6,2},{3,7},{7,3},{8,12},{12,8},{9,1... | collective-permute-start | bytes 3145736 | tf_op jit(solution)/shard_map/ppermute | solution.py:27
  59.3 20.5 %all-to-all-start.2 = ((bf16[16,8,8,512]{3,2,1,0:T(8,128)(2,1)}), bf16[16,8,8,512]{3,2,1,0:T(8,128)(2,1)S(1)}, u32[]{:S(2)}, u32[]{:S(2)}) async-start(bf16[16,8,8,512]{3,2,1,0:T(8,128)(2,1)} %broadcast_in_dim.30), calls=%async_computation.2 | async-start | bytes 2097152 | tf_op jit(solution)/shard_map/all_to_all | solution.py:18
  63.0 1.0 copy-start.2
  63.9 1.0 copy-start.6
  64.9 1.2 copy-start.1
  66.1 1.2 copy-start.3
  67.4 1.2 copy-start.5
  68.6 1.2 copy-start.7
  111.2 12.4 %copy-start.10 = (f32[8,512]{1,0:T(8,128)S(1)}, f32[8,512]{1,0:T(8,128)}, u32[]{:S(2)}) copy-start(f32[8,512]{1,0:T(8,128)} %mr_ref.3) | copy-start | bytes 49156
  111.2 12.4 %copy-start.11 = (f32[8,512]{1,0:T(8,128)S(1)}, f32[8,512]{1,0:T(8,128)}, u32[]{:S(2)}) copy-start(f32[8,512]{1,0:T(8,128)} %me_ref.3) | copy-start | bytes 49156
  111.2 12.4 %copy-start.12 = (f32[8,512]{1,0:T(8,128)S(1)}, f32[8,512]{1,0:T(8,128)}, u32[]{:S(2)}) copy-start(f32[8,512]{1,0:T(8,128)} %ve_ref.3) | copy-start | bytes 49156
  111.3 12.4 %copy-start.13 = (f32[8,512]{1,0:T(8,128)S(1)}, f32[8,512]{1,0:T(8,128)}, u32[]{:S(2)}) copy-start(f32[8,512]{1,0:T(8,128)} %vr_ref.3) | copy-start | bytes 49156
  182.4 15.0 %collective-permute-start.4 = (bf16[16,8,2,8,512]{4,3,2,1,0:T(8,128)(2,1)S(1)}, bf16[16,8,2,8,512]{4,3,2,1,0:T(8,128)(2,1)}, u32[]{:S(2)}, u32[]{:S(2)}) collective-permute-start(bf16[16,8,2,8,512]{4,3,2,1,0:T(8,128)(2,1)S(1)} %all_to_all.46.parts_ref), channel_id=1, source_target_pairs={{0,4},{4,0},{1,5},{5,1},{2,6},{6,2},{3,7},{7,3},{8,12},{12,8},{9,1... | collective-permute-start | bytes 6291464 | tf_op jit(solution)/shard_map/ppermute | solution.py:27
  184.4 5.4 %collective-permute-start.3 = (bf16[16,8,8,512]{3,2,1,0:T(8,128)(2,1)S(1)}, bf16[16,8,8,512]{3,2,1,0:T(8,128)(2,1)}, u32[]{:S(2)}, u32[]{:S(2)}) collective-permute-start(bf16[16,8,8,512]{3,2,1,0:T(8,128)(2,1)S(1)} %all-to-all-done.2.mine_ref), channel_id=1, source_target_pairs={{0,4},{4,0},{1,5},{5,1},{2,6},{6,2},{3,7},{7,3},{8,12},{12,8},{9,1... | collective-permute-start | bytes 3145736 | tf_op jit(solution)/shard_map/ppermute | solution.py:27
  189.8 1.1 copy-start.9

commit v5 on v4

--- a/solution.py
+++ b/solution.py
@@ -23,16 +23,24 @@
     return exchange(jnp.broadcast_to(block[None], (peers, *block.shape)), axes)
 
 
+def shifted(block, axis):
+    pieces = [block]
+    for s in range(1, 4):
+        pieces.append(lax.ppermute(block, axis, [(i, (i + s) % 4) for i in range(4)]))
+    return jnp.stack(pieces)
+
+
 def from_other_core(block):
     return lax.ppermute(block, "c", [(0, 1), (1, 0)])
 
 
-def fill_weights(core, mine_ref, other_ref, whole_ref):
+def fill_weights(core, piece, mine_ref, other_ref, whole_ref):
     for z in range(8):
         tiles = []
         for y in range(4):
-            mine = [mine_ref[y * 4 + x, z].astype(F32) for x in range(4)]
-            other = [other_ref[y * 4 + x, z].astype(F32) for x in range(4)]
+            at = [piece(y, x) for x in range(4)]
+            mine = [mine_ref[i, z].astype(F32) for i in at]
+            other = [other_ref[i, z].astype(F32) for i in at]
             tiles += [jnp.where(core == 0, m, o) for m, o in zip(mine, other)]
             tiles += [jnp.where(core == 0, o, m) for m, o in zip(mine, other)]
         rows = jnp.concatenate(tiles, axis=0).astype(BF)
@@ -50,14 +58,14 @@
             send_ref[pl.ds(y * 4, 4), z] = jnp.where(core == 0, second, first).astype(BF)
 
 
-def expand_kernel(scale, core_ref, grad_ref, hidden_ref, keep_ref, send_ref):
-    terms_to_halves(core_ref[0], grad_ref, hidden_ref[...], scale, keep_ref, send_ref)
+def expand_kernel(scale, place_ref, grad_ref, hidden_ref, keep_ref, send_ref):
+    terms_to_halves(place_ref[0], grad_ref, hidden_ref[...], scale, keep_ref, send_ref)
 
 
 def hidden_kernel(
     inv_m,
     inv_c,
-    core_ref,
+    place_ref,
     saved_ref,
     mine_ref,
     other_ref,
@@ -71,12 +79,12 @@
     acts_ref,
     sems,
 ):
-    core = core_ref[0]
+    core = place_ref[0]
     grad_copy = pltpu.make_async_copy(grad_hbm, grad_ref, sems.at[0])
     acts_copy = pltpu.make_async_copy(acts_hbm, acts_ref, sems.at[1])
     grad_copy.start()
     acts_copy.start()
-    fill_weights(core, mine_ref, other_ref, whole_ref)
+    fill_weights(core, lambda y, x: y * 4 + x, mine_ref, other_ref, whole_ref)
     grad_copy.wait()
     summed = jnp.dot(grad_ref[...], whole_ref[...], preferred_element_type=F32)
     saved = saved_ref[...].astype(F32)
@@ -85,30 +93,26 @@
     terms_to_halves(core, acts_ref, out_ref[...], inv_c, keep_ref, send_ref)
 
 
-def chip_sum_kernel(keep_e_ref, got_e_ref, keep_r_ref, got_r_ref, out_ref):
-    for at, (keep_ref, got_ref) in enumerate(((keep_e_ref, got_e_ref), (keep_r_ref, got_r_ref))):
-        total = keep_ref[...].astype(F32) + got_ref[...].astype(F32)
-        out_ref[:, at] = total.astype(BF)
-
-
-def chip_sum(*parts):
-    peers, *rest = parts[0].shape
-    whole = pl.BlockSpec(memory_space=pltpu.VMEM)
-    moved = 3 * parts[0].size * 4
-    return pl.pallas_call(
-        chip_sum_kernel,
-        out_shape=jax.ShapeDtypeStruct((peers, 2, *rest), BF),
-        in_specs=[whole] * 4,
-        out_specs=whole,
-        compiler_params=pltpu.CompilerParams(vmem_limit_bytes=16 * 1024 * 1024),
-        cost_estimate=pl.CostEstimate(
-            flops=2 * parts[0].size, bytes_accessed=moved, transcendentals=0
-        ),
-    )(*parts)
-
-
-def back_kernel(inv_c, core_ref, grad_ref, hidden_ref, mine_ref, other_ref, out_ref, whole_ref):
-    fill_weights(core_ref[0], mine_ref, other_ref, whole_ref)
+def chip_sum_kernel(keep_ref, got_ref, out_ref):
+    out_ref[...] = (keep_ref[...].astype(F32) + got_ref[...].astype(F32)).astype(BF)
+
+
+def plane_sum_kernel(expand_ref, reduce_ref, out_ref):
+    for z in range(8):
+        out_ref[z, 0] = expand_ref[z]
+        total = reduce_ref[0, z].astype(F32)
+        for peer in range(1, reduce_ref.shape[0]):
+            total = total + reduce_ref[peer, z].astype(F32)
+        out_ref[z, 1] = total.astype(BF)
+
+
+def back_kernel(inv_c, place_ref, grad_ref, hidden_ref, mine_ref, other_ref, out_ref, whole_ref):
+    core, my_y, my_x = place_ref[0], place_ref[1], place_ref[2]
+
+    def piece(y, x):
+        return lax.rem(my_y - y + 4, 4) * 4 + lax.rem(my_x - x + 4, 4)
+
+    fill_weights(core, piece, mine_ref, other_ref, whole_ref)
     for z in range(8):
         columns = pl.ds(z * 256, 256)
         back = lax.dot_general(
@@ -122,7 +126,7 @@
 
 def local_call(kernel, operands, outs, scratch, flops, streamed=()):
     whole = pl.BlockSpec(memory_space=pltpu.VMEM)
-    core = lax.axis_index("c").astype(jnp.int32).reshape(1)
+    at = jnp.stack([lax.axis_index(axis).astype(jnp.int32) for axis in ("c", "y", "x")])
     moved = sum(x.size * x.dtype.itemsize for x in (*operands, *streamed, *outs))
     scratch = scratch + [pltpu.VMEM(x.shape, x.dtype) for x in streamed]
     if streamed:
@@ -136,7 +140,7 @@
         scratch_shapes=scratch,
         compiler_params=pltpu.CompilerParams(vmem_limit_bytes=50 * 1024 * 1024),
         cost_estimate=pl.CostEstimate(flops=flops, bytes_accessed=moved, transcendentals=0),
-    )(core, *operands, *streamed)
+    )(at, *operands, *streamed)
 
 
 def total_of(terms):
@@ -286,8 +290,9 @@
     keep_e, send_e = local_call(
         functools.partial(expand_kernel, inv_m), (grad_out, saved_hidden), (half, half), [], flops
     )
+    (sent_e,) = small_call(chip_sum_kernel, (keep_e, from_other_core(send_e)), (half,))
     other = from_other_core(mine)
-    mine_reduce = everywhere(along_z[:, 1], ("y", "x"))
+    arrived_e = exchange(sent_e, ("y", "x"))
     grad_hidden, keep_r, send_r = local_call(
         functools.partial(hidden_kernel, inv_m, inv_c),
         (saved_hidden, mine, other),
@@ -296,11 +301,17 @@
         2 * flops,
         (grad_out, acts),
     )
-    halves = chip_sum(keep_e, from_other_core(send_e), keep_r, from_other_core(send_r))
-    halves, mine_reduce = lax.optimization_barrier((halves, mine_reduce))
-    arrived = exchange(halves, ("y", "x"))
-    over_plane = jnp.sum(arrived.astype(F32), axis=0).astype(BF)
-    arrived = exchange(over_plane.transpose(1, 0, 2, 3), "z")
+    (sent_r,) = small_call(chip_sum_kernel, (keep_r, from_other_core(send_r)), (half,))
+    arrived_r = exchange(sent_r, ("y", "x"))
+    row = shifted(along_z[:, 1], "x")
+    plane_e = jnp.sum(arrived_e.astype(F32), axis=0).astype(BF)
+    (over_plane,) = small_call(
+        plane_sum_kernel,
+        (plane_e, arrived_r),
+        (jax.ShapeDtypeStruct((8, 2, channels // 256, middle), BF),),
+    )
+    arrived = exchange(over_plane, "z")
+    mine_reduce = shifted(row, "y").reshape(half.shape)
     other_reduce = from_other_core(mine_reduce)
     (grad_in,) = local_call(
         functools.partial(back_kernel, inv_c),

time: 201 us -> 206 us (1.025)
  waiting for transfers between devices: 14.9 us -> 48.3 us
  blocking collectives: 138 us -> 107 us
  starting transfers between devices: 9.42 us -> 21.1 us
  local copies, waits for them, and re-layouts: 12.2 us -> 2.28 us
    all_to_all x7 -> x6, blocking collectives: 138 us -> 107 us  [exchange(): return lax.all_to_all(parts, axes, 0, 0, tiled=True)]
    all_to_all x1 -> x2, waiting for transfers between devices: 9.47 us -> 30.3 us  [exchange(): return lax.all_to_all(parts, axes, 0, 0, tiled=True)]
    ppermute x0 -> x6, waiting for transfers between devices: none -> 15.6 us  [shifted(): lax.ppermute(block, axis, [(i, (i + s) % 4) for i in range(4)])]
    unnamed x32 -> x16, local copies, waits for them, and re-layouts: 10.7 us -> 1.91 us
    ppermute x0 -> x6, starting transfers between devices: none -> 5.4 us  [shifted(): lax.ppermute(block, axis, [(i, (i + s) % 4) for i in range(4)])]
    all_to_all x1 -> x2, starting transfers between devices: 3.66 us -> 8.24 us  [exchange(): return lax.all_to_all(parts, axes, 0, 0, tiled=True)]
    ppermute x5, waiting for transfers between devices: 5.42 us -> 2.43 us  [from_other_core(): return lax.ppermute(block, 'c', [(0, 1), (1, 0)])]
    pallas_call x3 -> x6, Pallas kernels: 0.88 us -> 3.44 us  [small_call(): pl.pallas_call(kernel, out_shape=outs, in_specs=[whole] * len(operands),...]
  transfers between devices with their start and end apart: 6 -> 13, of which waited for: 2 -> 9; matrix products, arithmetic and copies ran while one was open for 1% -> 1% of each run, Pallas kernels for 9% -> 9%
where the time goes in v5:
time: 206 us; the launch traced here: 205 us
  blocking collectives  107 us (52%)
  waiting for transfers between devices  48.3 us (23%)
  Pallas kernels  23.3 us (11%)
  starting transfers between devices  21.1 us (10%)
  other arithmetic  2.44 us (1%)
  local copies, waits for them, and re-layouts  2.28 us (1%)
    all_to_all x6, blocking collectives, exchange(): return lax.all_to_all(parts, axes, 0, 0, tiled=True)  107 us
    all_to_all x2, waiting for transfers between devices, exchange(): return lax.all_to_all(parts, axes, 0, 0, tiled=True)  30.3 us
    ppermute x6, waiting for transfers between devices, shifted(): lax.ppermute(block, axis, [(i, (i + s) % 4) for i in range(4)])  15.6 us
    pallas_call x3, Pallas kernels, local_call(): pl.pallas_call(kernel, out_shape=outs, in_specs=[pl.BlockSpec(memory_spac...  15.2 us
    all_to_all x2, starting transfers between devices, exchange(): return lax.all_to_all(parts, axes, 0, 0, tiled=True)  8.24 us
    ppermute x5, starting transfers between devices, from_other_core(): return lax.ppermute(block, 'c', [(0, 1), (1, 0)])  7.49 us
    ppermute x6, starting transfers between devices, shifted(): lax.ppermute(block, axis, [(i, (i + s) % 4) for i in range(4)])  5.4 us
    pallas_call x2, Pallas kernels, place(): pl.pallas_call(place_kernel, out_shape=(whole, whole), in_specs=[pl.Block...  4.73 us
  transfers between devices with their start and end apart: 13, of which 9 were waited for; matrix products, arithmetic and copies ran while one was open for 1% of the time, Pallas kernels for 9%

profile of v5, /device:TPU:1, one launch (start us, length us, event | category | flops | bytes accessed | tf_op | source)
XLA Modules:
  0.0 205.2 jit_solution(8021611253754465995)
XLA Ops:
  0.6 0.0 copy-start.6
  0.6 0.8 convert_bitcast_fusion
  1.5 16.6 %all_to_all.40 = bf16[8,2,8,512]{3,2,1,0:T(8,128)(2,1)S(1)} all-to-all(bf16[8,2,8,512]{3,2,1,0:T(8,128)(2,1)S(1)} %broadcast_in_dim.8), channel_id=1, replica_groups=mesh['z'=8,'y'=4,'c'=2,'x'=4] {'z'}, dimensions={0} | all-to-all | bytes 262144 | tf_op jit(solution)/shard_map/all_to_all | solution.py:18
  18.0 0.1 broadcast_in_dim.10
  18.1 21.5 %all_to_all.41.mine_ref = bf16[16,8,8,512]{3,2,1,0:T(8,128)(2,1)S(1)} all-to-all(bf16[16,8,8,512]{3,2,1,0:T(8,128)(2,1)S(1)} %broadcast_in_dim.10), channel_id=1, replica_groups=mesh['z'=8,'y'=4,'c'=2,'x'=4] {'y','x'}, dimensions={0} | all-to-all | bytes 2097152 | tf_op jit(solution)/shard_map/all_to_all | solution.py:18
  39.6 0.0 copy-start.7
  39.6 3.3 %collective-permute-start = (bf16[16,8,8,512]{3,2,1,0:T(8,128)(2,1)S(1)}, bf16[16,8,8,512]{3,2,1,0:T(8,128)(2,1)}, u32[]{:S(2)}, u32[]{:S(2)}) collective-permute-start(bf16[16,8,8,512]{3,2,1,0:T(8,128)(2,1)S(1)} %all_to_all.41.mine_ref), channel_id=1, source_target_pairs={{0,4},{4,0},{1,5},{5,1},{2,6},{6,2},{3,7},{7,3},{8,12},{12,8},{9,1... | collective-permute-start | bytes 3145736 | tf_op jit(solution)/shard_map/ppermute | solution.py:34
  42.9 0.1 pad_add_fusion.place_ref
  43.0 0.0 copy-done.6
  43.0 3.5 %shard_map.128 = (bf16[16,8,8,512]{3,2,1,0:T(8,128)(2,1)S(1)}, bf16[16,8,8,512]{3,2,1,0:T(8,128)(2,1)S(1)}) custom-call(s32[3]{0:T(128)S(1)} %pad_add_fusion.place_ref, bf16[588,2048]{1,0:T(8,128)(2,1)} %grad_ref.3, bf16[588,512]{1,0:T(8,128)(2,1)S(1)} %copy-done.6), custom_call_target="tpu_custom_call" | custom-call | flops 1233125376 | bytes 5107712 | tf_op jit(solution)/shard_map/pallas_call | solution.py:134
  46.5 0.0 copy-done.7
  46.5 0.4 collective-permute-start.8
  46.9 0.0 collective-permute-done.other_ref
  46.9 6.6 %shard_map.126 = (bf16[588,512]{1,0:T(8,128)(2,1)S(1)}, bf16[16,8,8,512]{3,2,1,0:T(8,128)(2,1)S(1)}, bf16[16,8,8,512]{3,2,1,0:T(8,128)(2,1)S(1)}) custom-call(s32[3]{0:T(128)S(1)} %pad_add_fusion.place_ref, bf16[588,512]{1,0:T(8,128)(2,1)S(1)} %copy-done.6, bf16[16,8,8,512]{3,2,1,0:T(8,128)(2,1)} %copy-done.7, ...), custom_call_target="tpu_custom_call" | custom-call | flops 2466250752 | bytes 10215424 | tf_op jit(solution)/shard_map/pallas_call | solution.py:134
  53.5 0.0 copy-start
  53.5 0.8 copy-done
  54.3 0.2 collective-permute-start.9
  54.5 0.0 collective-permute-done.8.got_ref
  54.6 1.2 shard_map.129
  55.8 4.3 %all-to-all-start.2 = ((bf16[16,8,8,512]{3,2,1,0:T(8,128)(2,1)}), bf16[16,8,8,512]{3,2,1,0:T(8,128)(2,1)}, u32[]{:S(2)}, u32[]{:S(2)}) async-start(bf16[16,8,8,512]{3,2,1,0:T(8,128)(2,1)} %shard_map.129), calls=%async_computation.2 | async-start | bytes 2097152 | tf_op jit(solution)/shard_map/all_to_all | solution.py:18
  60.1 0.0 collective-permute-done.9.got_ref
  60.1 1.2 shard_map.130
  61.3 0.0 copy-start.2
  61.3 0.0 copy-start.3
  61.3 0.0 copy-start.4
  61.3 0.0 copy-start.5
  61.3 16.0 %all-to-all-done.2 = bf16[16,8,8,512]{3,2,1,0:T(8,128)(2,1)} async-done(((bf16[16,8,8,512]{3,2,1,0:T(8,128)(2,1)}), bf16[16,8,8,512]{3,2,1,0:T(8,128)(2,1)}, u32[]{:S(2)}, u32[]{:S(2)}) %all-to-all-start.2) | async-done | bytes 1048608 | tf_op jit(solution)/shard_map/all_to_all | solution.py:18
  77.4 3.9 %all-to-all-start.3 = ((bf16[16,8,8,512]{3,2,1,0:T(8,128)(2,1)}), bf16[16,8,8,512]{3,2,1,0:T(8,128)(2,1)S(1)}, u32[]{:S(2)}, u32[]{:S(2)}) async-start(bf16[16,8,8,512]{3,2,1,0:T(8,128)(2,1)} %shard_map.130), calls=%async_computation.3 | async-start | bytes 2097152 | tf_op jit(solution)/shard_map/all_to_all | solution.py:18
  81.3 1.4 reduce_sum.12.expand_ref
  82.7 14.3 %all-to-all-done.3.reduce_ref = bf16[16,8,8,512]{3,2,1,0:T(8,128)(2,1)S(1)} async-done(((bf16[16,8,8,512]{3,2,1,0:T(8,128)(2,1)}), bf16[16,8,8,512]{3,2,1,0:T(8,128)(2,1)S(1)}, u32[]{:S(2)}, u32[]{:S(2)}) %all-to-all-start.3) | async-done | bytes 1048608 | tf_op jit(solution)/shard_map/all_to_all | solution.py:18
  97.0 0.1 shard_map.131
  97.1 10.3 %all_to_all.42.arrived_ref = bf16[8,2,8,512]{3,2,1,0:T(8,128)(2,1)S(1)} all-to-all(bf16[8,2,8,512]{3,2,1,0:T(8,128)(2,1)S(1)} %shard_map.131), channel_id=1, replica_groups=mesh['z'=8,'y'=4,'c'=2,'x'=4] {'z'}, dimensions={0} | all-to-all | bytes 262144 | tf_op jit(solution)/shard_map/all_to_all | solution.py:18
  107.4 0.0 copy-done.2
  107.4 0.0 copy-done.3
  107.4 0.0 copy-done.4
  107.4 0.0 copy-done.5
  107.4 0.1 shard_map.132
  107.6 12.5 %all_to_all.43.ring_ref = bf16[8,5,8,512]{3,2,1,0:T(8,128)(2,1)S(1)} all-to-all(bf16[8,5,8,512]{3,2,1,0:T(8,128)(2,1)S(1)} %get-tuple-element.28), channel_id=1, replica_groups=mesh['z'=8,'y'=4,'c'=2,'x'=4] {'z'}, dimensions={0} | all-to-all | bytes 655360 | tf_op jit(solution)/shard_map/all_to_all | solution.py:18
  120.1 15.9 %all_to_all.44.squares_ref = f32[32,8,128]{2,1,0:T(8,128)S(1)} all-to-all(f32[32,8,128]{2,1,0:T(8,128)S(1)} %shard_map.133), channel_id=1, replica_groups=mesh['z'=8,'y'=4,'c'=2,'x'=4] {'y','c','x'}, dimensions={0} | all-to-all | bytes 262144 | tf_op jit(solution)/shard_map/all_to_all | solution.py:18
  136.0 0.7 shard_map.134
  136.8 0.2 broadcast_in_dim.22
  137.0 30.0 %all_to_all.45.parts_ref = bf16[16,8,2,8,512]{4,3,2,1,0:T(8,128)(2,1)S(1)} all-to-all(bf16[16,8,2,8,512]{4,3,2,1,0:T(8,128)(2,1)S(1)} %broadcast_in_dim.22), channel_id=1, replica_groups=mesh['z'=8,'y'=4,'c'=2,'x'=4] {'y','x'}, dimensions={0} | all-to-all | bytes 4194304 | tf_op jit(solution)/shard_map/all_to_all | solution.py:18
  167.0 2.0 collective-permute-start.10
  169.0 0.2 collective-permute-start.3
  169.2 1.2 collective-permute-start.1
  170.5 0.6 collective-permute-start.2
  171.1 1.6 collective-permute-done.3
  172.7 0.9 collective-permute-done.1
  173.6 1.5 collective-permute-done.2
  175.1 0.8 collective-permute-start.4
  176.0 1.3 collective-permute-start.5
  177.2 1.2 collective-permute-start.6
  178.5 5.0 %collective-permute-done.4 = bf16[4,8,8,512]{3,2,1,0:T(8,128)(2,1)S(1)} collective-permute-done((bf16[4,8,8,512]{3,2,1,0:T(8,128)(2,1)S(1)}, bf16[4,8,8,512]{3,2,1,0:T(8,128)(2,1)S(1)}, u32[]{:S(2)}, u32[]{:S(2)}) %collective-permute-start.4) | collective-permute-done | bytes 262176 | tf_op jit(solution)/shard_map/ppermute | solution.py:29
  183.5 4.2 %collective-permute-done.5 = bf16[4,8,8,512]{3,2,1,0:T(8,128)(2,1)S(1)} collective-permute-done((bf16[4,8,8,512]{3,2,1,0:T(8,128)(2,1)S(1)}, bf16[4,8,8,512]{3,2,1,0:T(8,128)(2,1)S(1)}, u32[]{:S(2)}, u32[]{:S(2)}) %collective-permute-start.5) | collective-permute-done | bytes 262176 | tf_op jit(solution)/shard_map/ppermute | solution.py:29
  187.7 2.3 %collective-permute-done.6 = bf16[4,8,8,512]{3,2,1,0:T(8,128)(2,1)S(1)} collective-permute-done((bf16[4,8,8,512]{3,2,1,0:T(8,128)(2,1)S(1)}, bf16[4,8,8,512]{3,2,1,0:T(8,128)(2,1)S(1)}, u32[]{:S(2)}, u32[]{:S(2)}) %collective-permute-start.6) | collective-permute-done | bytes 262176 | tf_op jit(solution)/shard_map/ppermute | solution.py:29
  190.0 0.1 pad_maximum_fusion
  190.2 1.6 collective-permute-start.7
  191.8 2.4 %collective-permute-done.7.other_ref = bf16[16,8,8,512]{3,2,1,0:T(8,128)(2,1)} collective-permute-done((bf16[16,8,8,512]{3,2,1,0:T(8,128)(2,1)S(1)}, bf16[16,8,8,512]{3,2,1,0:T(8,128)(2,1)}, u32[]{:S(2)}, u32[]{:S(2)}) %collective-permute-start.7) | collective-permute-done | bytes 1048608 | tf_op jit(solution)/shard_map/ppermute | solution.py:34
  194.2 0.0 copy-start.1
  194.2 1.1 copy-done.1
  195.3 5.0 %shard_map.127 = bf16[588,2048]{1,0:T(8,128)(2,1)} custom-call(s32[3]{0:T(128)S(1)} %pad_add_fusion.place_ref, bf16[588,2048]{1,0:T(8,128)(2,1)} %grad_ref.3, bf16[588,512]{1,0:T(8,128)(2,1)S(1)} %copy-done.1, bf16[16,8,8,512]{3,2,1,0:T(8,128)(2,1)S(1)} %bitcast.26, bf16[16,8,8,512]{3,2,1,0:T(8,128)(2,1)} %collective-permute-done.7.other_ref), custom_call_target="tpu_custom_call" | custom-call | flops 1233125376 | bytes 7516160 | tf_op jit(solution)/shard_map/pallas_call | solution.py:134
  200.3 1.6 shard_map.135
  201.9 0.0 collective-permute-done.10.parts_ref
  201.9 3.2 %shard_map.136 = (bf16[8,4,2,4,8,512]{5,4,3,2,1,0:T(8,128)(2,1)}, bf16[8,4,2,4,8,512]{5,4,3,2,1,0:T(8,128)(2,1)}) custom-call(s32[1]{0:T(128)} %bitcast.16.core_ref, bf16[16,8,2,8,512]{4,3,2,1,0:T(8,128)(2,1)} %collective-permute-done.10.parts_ref, ...), custom_call_target="tpu_custom_call", output_to_operand_aliasing={{0}: (2, {}), {1}: (3, {})} | custom-call | flops 1048576 | bytes 4194304 | tf_op jit(solution)/shard_map/pallas_call | solution.py:258
  (5 shorter events, 0.1 us)
Async XLA Ops:
  0.6 42.4 %copy-start.6 = (bf16[588,512]{1,0:T(8,128)(2,1)S(1)}, bf16[588,512]{1,0:T(8,128)(2,1)}, u32[]{:S(2)}) copy-start(bf16[588,512]{1,0:T(8,128)(2,1)} %hidden_ref.1) | copy-start | bytes 1806340
  39.6 6.9 %copy-start.7 = (bf16[16,8,8,512]{3,2,1,0:T(8,128)(2,1)}, bf16[16,8,8,512]{3,2,1,0:T(8,128)(2,1)S(1)}, u32[]{:S(2)}) copy-start(bf16[16,8,8,512]{3,2,1,0:T(8,128)(2,1)S(1)} %all_to_all.41.mine_ref) | copy-start | bytes 3145732
  39.6 7.3 %collective-permute-start = (bf16[16,8,8,512]{3,2,1,0:T(8,128)(2,1)S(1)}, bf16[16,8,8,512]{3,2,1,0:T(8,128)(2,1)}, u32[]{:S(2)}, u32[]{:S(2)}) collective-permute-start(bf16[16,8,8,512]{3,2,1,0:T(8,128)(2,1)S(1)} %all_to_all.41.mine_ref), channel_id=1, source_target_pairs={{0,4},{4,0},{1,5},{5,1},{2,6},{6,2},{3,7},{7,3},{8,12},{12,8},{9,1... | collective-permute-start | bytes 3145736 | tf_op jit(solution)/shard_map/ppermute | solution.py:34
  46.5 8.0 %collective-permute-start.8 = (bf16[16,8,8,512]{3,2,1,0:T(8,128)(2,1)S(1)}, bf16[16,8,8,512]{3,2,1,0:T(8,128)(2,1)S(1)}, u32[]{:S(2)}, u32[]{:S(2)}) collective-permute-start(bf16[16,8,8,512]{3,2,1,0:T(8,128)(2,1)S(1)} %get-tuple-element.25), channel_id=1, source_target_pairs={{0,4},{4,0},{1,5},{5,1},{2,6},{6,2},{3,7},{7,3},{8,12},{12,8},{9,1... | collective-permute-start | bytes 3145736 | tf_op jit(solution)/shard_map/ppermute | solution.py:34
  53.5 0.8 copy-start
  54.3 5.8 %collective-permute-start.9 = (bf16[16,8,8,512]{3,2,1,0:T(8,128)(2,1)S(1)}, bf16[16,8,8,512]{3,2,1,0:T(8,128)(2,1)S(1)}, u32[]{:S(2)}, u32[]{:S(2)}) collective-permute-start(bf16[16,8,8,512]{3,2,1,0:T(8,128)(2,1)S(1)} %get-tuple-element.27), channel_id=1, source_target_pairs={{0,4},{4,0},{1,5},{5,1},{2,6},{6,2},{3,7},{7,3},{8,12},{12,8},{9,1... | collective-permute-start | bytes 3145736 | tf_op jit(solution)/shard_map/ppermute | solution.py:34
  55.8 21.6 %all-to-all-start.2 = ((bf16[16,8,8,512]{3,2,1,0:T(8,128)(2,1)}), bf16[16,8,8,512]{3,2,1,0:T(8,128)(2,1)}, u32[]{:S(2)}, u32[]{:S(2)}) async-start(bf16[16,8,8,512]{3,2,1,0:T(8,128)(2,1)} %shard_map.129), calls=%async_computation.2 | async-start | bytes 2097152 | tf_op jit(solution)/shard_map/all_to_all | solution.py:18
  61.3 46.1 %copy-start.2 = (f32[8,512]{1,0:T(8,128)S(1)}, f32[8,512]{1,0:T(8,128)}, u32[]{:S(2)}) copy-start(f32[8,512]{1,0:T(8,128)} %mr_ref.3) | copy-start | bytes 49156
  61.3 46.1 %copy-start.3 = (f32[8,512]{1,0:T(8,128)S(1)}, f32[8,512]{1,0:T(8,128)}, u32[]{:S(2)}) copy-start(f32[8,512]{1,0:T(8,128)} %me_ref.3) | copy-start | bytes 49156
  61.3 46.1 %copy-start.4 = (f32[8,512]{1,0:T(8,128)S(1)}, f32[8,512]{1,0:T(8,128)}, u32[]{:S(2)}) copy-start(f32[8,512]{1,0:T(8,128)} %ve_ref.3) | copy-start | bytes 49156
  61.3 46.1 %copy-start.5 = (f32[8,512]{1,0:T(8,128)S(1)}, f32[8,512]{1,0:T(8,128)}, u32[]{:S(2)}) copy-start(f32[8,512]{1,0:T(8,128)} %vr_ref.3) | copy-start | bytes 49156
  77.4 19.6 %all-to-all-start.3 = ((bf16[16,8,8,512]{3,2,1,0:T(8,128)(2,1)}), bf16[16,8,8,512]{3,2,1,0:T(8,128)(2,1)S(1)}, u32[]{:S(2)}, u32[]{:S(2)}) async-start(bf16[16,8,8,512]{3,2,1,0:T(8,128)(2,1)} %shard_map.130), calls=%async_computation.3 | async-start | bytes 2097152 | tf_op jit(solution)/shard_map/all_to_all | solution.py:18
  167.0 34.9 %collective-permute-start.10 = (bf16[16,8,2,8,512]{4,3,2,1,0:T(8,128)(2,1)S(1)}, bf16[16,8,2,8,512]{4,3,2,1,0:T(8,128)(2,1)}, u32[]{:S(2)}, u32[]{:S(2)}) collective-permute-start(bf16[16,8,2,8,512]{4,3,2,1,0:T(8,128)(2,1)S(1)} %all_to_all.45.parts_ref), channel_id=1, source_target_pairs={{0,4},{4,0},{1,5},{5,1},{2,6},{6,2},{3,7},{7,3},{8,12},{12,8},{9,1... | collective-permute-start | bytes 6291464 | tf_op jit(solution)/shard_map/ppermute | solution.py:34
  169.0 3.6 %collective-permute-start.3 = (bf16[8,8,512]{2,1,0:T(8,128)(2,1)S(1)}, bf16[8,8,512]{2,1,0:T(8,128)(2,1)S(1)}, u32[]{:S(2)}, u32[]{:S(2)}) collective-permute-start(bf16[8,8,512]{2,1,0:T(8,128)(2,1)S(1)} %get-tuple-element.42), channel_id=1, source_target_pairs={{0,3},{1,0},{2,1},{3,2},{4,7},{5,4},{6,5},{7,6},{8,11},{9,8},{10,9... | collective-permute-start | bytes 196616 | tf_op jit(solution)/shard_map/ppermute | solution.py:29
  169.2 4.3 %collective-permute-start.1 = (bf16[8,8,512]{2,1,0:T(8,128)(2,1)S(1)}, bf16[8,8,512]{2,1,0:T(8,128)(2,1)S(1)}, u32[]{:S(2)}, u32[]{:S(2)}) collective-permute-start(bf16[8,8,512]{2,1,0:T(8,128)(2,1)S(1)} %get-tuple-element.42), channel_id=1, source_target_pairs={{0,1},{1,2},{2,3},{3,0},{4,5},{5,6},{6,7},{7,4},{8,9},{9,10},{10,1... | collective-permute-start | bytes 196616 | tf_op jit(solution)/shard_map/ppermute | solution.py:29
  170.5 4.6 %collective-permute-start.2 = (bf16[8,8,512]{2,1,0:T(8,128)(2,1)S(1)}, bf16[8,8,512]{2,1,0:T(8,128)(2,1)S(1)}, u32[]{:S(2)}, u32[]{:S(2)}) collective-permute-start(bf16[8,8,512]{2,1,0:T(8,128)(2,1)S(1)} %get-tuple-element.42), channel_id=1, source_target_pairs={{0,2},{1,3},{2,0},{3,1},{4,6},{5,7},{6,4},{7,5},{8,10},{9,11},{10,... | collective-permute-start | bytes 196616 | tf_op jit(solution)/shard_map/ppermute | solution.py:29
  175.1 8.3 %collective-permute-start.4 = (bf16[4,8,8,512]{3,2,1,0:T(8,128)(2,1)S(1)}, bf16[4,8,8,512]{3,2,1,0:T(8,128)(2,1)S(1)}, u32[]{:S(2)}, u32[]{:S(2)}) collective-permute-start(bf16[4,8,8,512]{3,2,1,0:T(8,128)(2,1)S(1)} %get-tuple-element.40), channel_id=1, source_target_pairs={{0,8},{8,16},{16,24},{24,0},{1,9},{9,17},{17,25},{25,1},{2,10},{10... | collective-permute-start | bytes 786440 | tf_op jit(solution)/shard_map/ppermute | solution.py:29
  176.0 11.7 %collective-permute-start.5 = (bf16[4,8,8,512]{3,2,1,0:T(8,128)(2,1)S(1)}, bf16[4,8,8,512]{3,2,1,0:T(8,128)(2,1)S(1)}, u32[]{:S(2)}, u32[]{:S(2)}) collective-permute-start(bf16[4,8,8,512]{3,2,1,0:T(8,128)(2,1)S(1)} %get-tuple-element.40), channel_id=1, source_target_pairs={{0,16},{8,24},{16,0},{24,8},{1,17},{9,25},{17,1},{25,9},{2,18},{10... | collective-permute-start | bytes 786440 | tf_op jit(solution)/shard_map/ppermute | solution.py:29
  177.2 12.8 %collective-permute-start.6 = (bf16[4,8,8,512]{3,2,1,0:T(8,128)(2,1)S(1)}, bf16[4,8,8,512]{3,2,1,0:T(8,128)(2,1)S(1)}, u32[]{:S(2)}, u32[]{:S(2)}) collective-permute-start(bf16[4,8,8,512]{3,2,1,0:T(8,128)(2,1)S(1)} %get-tuple-element.40), channel_id=1, source_target_pairs={{0,24},{8,0},{16,8},{24,16},{1,25},{9,1},{17,9},{25,17},{2,26},{10... | collective-permute-start | bytes 786440 | tf_op jit(solution)/shard_map/ppermute | solution.py:29
  190.2 4.1 %collective-permute-start.7 = (bf16[16,8,8,512]{3,2,1,0:T(8,128)(2,1)S(1)}, bf16[16,8,8,512]{3,2,1,0:T(8,128)(2,1)}, u32[]{:S(2)}, u32[]{:S(2)}) collective-permute-start(bf16[16,8,8,512]{3,2,1,0:T(8,128)(2,1)S(1)} %bitcast.25), channel_id=1, source_target_pairs={{0,4},{4,0},{1,5},{5,1},{2,6},{6,2},{3,7},{7,3},{8,12},{12,8},{9,1... | collective-permute-start | bytes 3145736 | tf_op jit(solution)/shard_map/ppermute | solution.py:34
  194.2 1.1 copy-start.1

commit v6 on v5

--- a/solution.py
+++ b/solution.py
@@ -27,7 +27,7 @@
     pieces = [block]
     for s in range(1, 4):
         pieces.append(lax.ppermute(block, axis, [(i, (i + s) % 4) for i in range(4)]))
-    return jnp.stack(pieces)
+    return jnp.concatenate(pieces)
 
 
 def from_other_core(block):
@@ -93,6 +93,13 @@
     terms_to_halves(core, acts_ref, out_ref[...], inv_c, keep_ref, send_ref)
 
 
+def working_kernel(me_ref, mr_ref, out_ref):
+    for layer, m_ref in enumerate((me_ref, mr_ref)):
+        rows = m_ref[...].astype(BF)
+        for z in range(8):
+            out_ref[z, layer] = rows
+
+
 def chip_sum_kernel(keep_ref, got_ref, out_ref):
     out_ref[...] = (keep_ref[...].astype(F32) + got_ref[...].astype(F32)).astype(BF)
 
@@ -231,42 +238,73 @@
     )(*operands)
 
 
-def place_kernel(core_ref, parts_ref, *refs):
-    expand_ref, reduce_ref, sems = refs[-3:]
-    core = core_ref[0]
+def placements(core, y, parts_ref, out_refs, sems):
+    copies = []
+    for x in range(4):
+        for layer, out_ref in enumerate(out_refs):
+            copies.append(
+                pltpu.make_async_copy(
+                    parts_ref.at[y * 4 + x, :, layer],
+                    out_ref.at[:, y, core, x],
+                    sems.at[y * 8 + x * 2 + layer],
+                )
+            )
+    return copies
+
+
+def place_mine_kernel(core_ref, parts_ref, expand_ref, reduce_ref, sems):
     copies = []
     for y in range(4):
-        for x in range(4):
-            for layer, out_ref in enumerate((expand_ref, reduce_ref)):
-                copies.append(
-                    pltpu.make_async_copy(
-                        parts_ref.at[y * 4 + x, :, layer],
-                        out_ref.at[:, y, core, x],
-                        sems.at[len(copies)],
-                    )
-                )
+        copies += placements(core_ref[0], y, parts_ref, (expand_ref, reduce_ref), sems)
     for copy in copies:
         copy.start()
     for copy in copies:
         copy.wait()
 
 
+def place_other_kernel(
+    core_ref, parts_hbm, _expand, _reduce, expand_ref, reduce_ref, parts_ref, sems, in_sems
+):
+    loads = [
+        pltpu.make_async_copy(
+            parts_hbm.at[pl.ds(y * 4, 4)], parts_ref.at[pl.ds(y * 4, 4)], in_sems.at[y]
+        )
+        for y in range(4)
+    ]
+    for load in loads:
+        load.start()
+    copies = []
+    for y in range(4):
+        loads[y].wait()
+        here = placements(core_ref[0], y, parts_ref, (expand_ref, reduce_ref), sems)
+        for copy in here:
+            copy.start()
+        copies += here
+    for copy in copies:
+        copy.wait()
+
+
 def place(core, parts, into):
     _, z, _, r, n = parts.shape
     whole = jax.ShapeDtypeStruct((z, 4, 2, 4, r, n), BF)
     hbm = pl.BlockSpec(memory_space=pl.ANY)
+    scratch = [pltpu.SemaphoreType.DMA((32,))]
+    if into:
+        scratch = [pltpu.VMEM(parts.shape, BF)] + scratch + [pltpu.SemaphoreType.DMA((4,))]
     return pl.pallas_call(
-        place_kernel,
+        place_other_kernel if into else place_mine_kernel,
         out_shape=(whole, whole),
         in_specs=[
             pl.BlockSpec(memory_space=pltpu.SMEM),
-            pl.BlockSpec(memory_space=pltpu.VMEM),
+            hbm if into else pl.BlockSpec(memory_space=pltpu.VMEM),
         ]
         + [hbm] * len(into),
         out_specs=(hbm, hbm),
-        scratch_shapes=[pltpu.SemaphoreType.DMA((32,))],
+        scratch_shapes=scratch,
         input_output_aliases={2 + at: at for at in range(len(into))},
-        compiler_params=pltpu.CompilerParams(vmem_limit_bytes=8 * 1024 * 1024),
+        compiler_params=pltpu.CompilerParams(
+            vmem_limit_bytes=(60 if into else 8) * 1024 * 1024
+        ),
         cost_estimate=pl.CostEstimate(
             flops=parts.size, bytes_accessed=4 * parts.size, transcendentals=0
         ),
@@ -284,8 +322,12 @@
     whole = pltpu.VMEM((channels, middle), BF)
     flops = 2 * grad_out.size * middle
 
-    cur = jnp.stack([master_expand.astype(BF), master_reduce.astype(BF)])
-    along_z = everywhere(cur, "z")
+    (cur,) = small_call(
+        working_kernel,
+        (master_expand, master_reduce),
+        (jax.ShapeDtypeStruct((8, 2, *master_expand.shape), BF),),
+    )
+    along_z = exchange(cur, "z")
     mine = everywhere(along_z[:, 0], ("y", "x"))
     keep_e, send_e = local_call(
         functools.partial(expand_kernel, inv_m), (grad_out, saved_hidden), (half, half), [], flops
@@ -303,7 +345,7 @@
     )
     (sent_r,) = small_call(chip_sum_kernel, (keep_r, from_other_core(send_r)), (half,))
     arrived_r = exchange(sent_r, ("y", "x"))
-    row = shifted(along_z[:, 1], "x")
+    row = lax.optimization_barrier(shifted(along_z[:, 1], "x"))
     plane_e = jnp.sum(arrived_e.astype(F32), axis=0).astype(BF)
     (over_plane,) = small_call(
         plane_sum_kernel,

time: 206 us -> 207 us (level)
  transfers between devices with their start and end apart: 13 -> 13, of which waited for: 9 -> 8; matrix products, arithmetic and copies ran while one was open for 1% -> 1% of each run, Pallas kernels for 9% -> 9%
where the time goes in v6:
time: 207 us; the launch traced here: 206 us
  blocking collectives  107 us (52%)
  waiting for transfers between devices  48 us (23%)
  Pallas kernels  22.8 us (11%)
  starting transfers between devices  21.9 us (11%)
  local copies, waits for them, and re-layouts  3.69 us (2%)
    all_to_all x6, blocking collectives, exchange(): return lax.all_to_all(parts, axes, 0, 0, tiled=True)  107 us
    all_to_all x2, waiting for transfers between devices, exchange(): return lax.all_to_all(parts, axes, 0, 0, tiled=True)  30.3 us
    ppermute x6, waiting for transfers between devices, shifted(): lax.ppermute(block, axis, [(i, (i + s) % 4) for i in range(4)])  15.2 us
    pallas_call x3, Pallas kernels, local_call(): pl.pallas_call(kernel, out_shape=outs, in_specs=[pl.BlockSpec(memory_spac...  15.2 us
    all_to_all x2, starting transfers between devices, exchange(): return lax.all_to_all(parts, axes, 0, 0, tiled=True)  8.25 us
    ppermute x5, starting transfers between devices, from_other_core(): return lax.ppermute(block, 'c', [(0, 1), (1, 0)])  8.07 us
    ppermute x6, starting transfers between devices, shifted(): lax.ppermute(block, axis, [(i, (i + s) % 4) for i in range(4)])  5.61 us
    pallas_call x2, Pallas kernels, place(): pl.pallas_call(place_other_kernel if into else place_mine_kernel, out_sha...  4.21 us
  transfers between devices with their start and end apart: 13, of which 8 were waited for; matrix products, arithmetic and copies ran while one was open for 1% of the time, Pallas kernels for 9%

profile of v6, /device:TPU:1, one launch (start us, length us, event | category | flops | bytes accessed | tf_op | source)
XLA Modules:
  0.0 206.0 jit_solution(13893701546182170968)
XLA Ops:
  0.6 0.0 copy-start.2
  0.6 0.7 copy-done.2
  1.4 0.0 copy-start.4
  1.4 0.7 copy-done.4
  2.1 0.0 copy-start.8
  2.1 16.7 %all_to_all.40 = bf16[8,2,8,512]{3,2,1,0:T(8,128)(2,1)S(1)} all-to-all(bf16[8,2,8,512]{3,2,1,0:T(8,128)(2,1)S(1)} %shard_map.126), channel_id=1, replica_groups=mesh['z'=8,'y'=4,'c'=2,'x'=4] {'z'}, dimensions={0} | all-to-all | bytes 262144 | tf_op jit(solution)/shard_map/all_to_all | solution.py:18
  18.8 0.1 broadcast_in_dim.14
  18.9 21.5 %all_to_all.41.mine_ref = bf16[16,8,8,512]{3,2,1,0:T(8,128)(2,1)S(1)} all-to-all(bf16[16,8,8,512]{3,2,1,0:T(8,128)(2,1)S(1)} %broadcast_in_dim.14), channel_id=1, replica_groups=mesh['z'=8,'y'=4,'c'=2,'x'=4] {'y','x'}, dimensions={0} | all-to-all | bytes 2097152 | tf_op jit(solution)/shard_map/all_to_all | solution.py:18
  40.4 0.0 copy-start.9
  40.4 3.3 %collective-permute-start = (bf16[16,8,8,512]{3,2,1,0:T(8,128)(2,1)S(1)}, bf16[16,8,8,512]{3,2,1,0:T(8,128)(2,1)}, u32[]{:S(2)}, u32[]{:S(2)}) collective-permute-start(bf16[16,8,8,512]{3,2,1,0:T(8,128)(2,1)S(1)} %all_to_all.41.mine_ref), channel_id=1, source_target_pairs={{0,4},{4,0},{1,5},{5,1},{2,6},{6,2},{3,7},{7,3},{8,12},{12,8},{9,1... | collective-permute-start | bytes 3145736 | tf_op jit(solution)/shard_map/ppermute | solution.py:34
  43.7 0.1 pad_add_fusion.place_ref
  43.7 0.0 copy-done.8
  43.7 3.5 %shard_map.129 = (bf16[16,8,8,512]{3,2,1,0:T(8,128)(2,1)S(1)}, bf16[16,8,8,512]{3,2,1,0:T(8,128)(2,1)S(1)}) custom-call(s32[3]{0:T(128)S(1)} %pad_add_fusion.place_ref, bf16[588,2048]{1,0:T(8,128)(2,1)} %grad_ref.3, bf16[588,512]{1,0:T(8,128)(2,1)S(1)} %copy-done.8), custom_call_target="tpu_custom_call" | custom-call | flops 1233125376 | bytes 5107712 | tf_op jit(solution)/shard_map/pallas_call | solution.py:141
  47.3 0.0 copy-done.9
  47.3 0.4 collective-permute-start.8
  47.7 0.0 collective-permute-done.other_ref
  47.7 6.6 %shard_map.127 = (bf16[588,512]{1,0:T(8,128)(2,1)S(1)}, bf16[16,8,8,512]{3,2,1,0:T(8,128)(2,1)S(1)}, bf16[16,8,8,512]{3,2,1,0:T(8,128)(2,1)S(1)}) custom-call(s32[3]{0:T(128)S(1)} %pad_add_fusion.place_ref, bf16[588,512]{1,0:T(8,128)(2,1)S(1)} %copy-done.8, bf16[16,8,8,512]{3,2,1,0:T(8,128)(2,1)} %copy-done.9, ...), custom_call_target="tpu_custom_call" | custom-call | flops 2466250752 | bytes 10215424 | tf_op jit(solution)/shard_map/pallas_call | solution.py:141
  54.3 0.0 copy-start
  54.3 0.8 copy-done
  55.1 0.2 collective-permute-start.9
  55.3 0.0 collective-permute-done.8.got_ref
  55.3 1.2 shard_map.130
  56.5 4.3 %all-to-all-start.2 = ((bf16[16,8,8,512]{3,2,1,0:T(8,128)(2,1)}), bf16[16,8,8,512]{3,2,1,0:T(8,128)(2,1)}, u32[]{:S(2)}, u32[]{:S(2)}) async-start(bf16[16,8,8,512]{3,2,1,0:T(8,128)(2,1)} %shard_map.130), calls=%async_computation.2 | async-start | bytes 2097152 | tf_op jit(solution)/shard_map/all_to_all | solution.py:18
  60.9 0.0 collective-permute-done.9.got_ref
  60.9 1.2 shard_map.131
  62.1 0.0 copy-start.3
  62.1 0.0 copy-start.5
  62.1 16.0 %all-to-all-done.2 = bf16[16,8,8,512]{3,2,1,0:T(8,128)(2,1)} async-done(((bf16[16,8,8,512]{3,2,1,0:T(8,128)(2,1)}), bf16[16,8,8,512]{3,2,1,0:T(8,128)(2,1)}, u32[]{:S(2)}, u32[]{:S(2)}) %all-to-all-start.2) | async-done | bytes 1048608 | tf_op jit(solution)/shard_map/all_to_all | solution.py:18
  78.1 3.9 %all-to-all-start.3 = ((bf16[16,8,8,512]{3,2,1,0:T(8,128)(2,1)}), bf16[16,8,8,512]{3,2,1,0:T(8,128)(2,1)S(1)}, u32[]{:S(2)}, u32[]{:S(2)}) async-start(bf16[16,8,8,512]{3,2,1,0:T(8,128)(2,1)} %shard_map.131), calls=%async_computation.3 | async-start | bytes 2097152 | tf_op jit(solution)/shard_map/all_to_all | solution.py:18
  82.0 1.4 reduce_sum.12.expand_ref
  83.4 14.3 %all-to-all-done.3.reduce_ref = bf16[16,8,8,512]{3,2,1,0:T(8,128)(2,1)S(1)} async-done(((bf16[16,8,8,512]{3,2,1,0:T(8,128)(2,1)}), bf16[16,8,8,512]{3,2,1,0:T(8,128)(2,1)S(1)}, u32[]{:S(2)}, u32[]{:S(2)}) %all-to-all-start.3) | async-done | bytes 1048608 | tf_op jit(solution)/shard_map/all_to_all | solution.py:18
  97.7 0.1 shard_map.132
  97.9 10.3 %all_to_all.42.arrived_ref = bf16[8,2,8,512]{3,2,1,0:T(8,128)(2,1)S(1)} all-to-all(bf16[8,2,8,512]{3,2,1,0:T(8,128)(2,1)S(1)} %shard_map.132), channel_id=1, replica_groups=mesh['z'=8,'y'=4,'c'=2,'x'=4] {'z'}, dimensions={0} | all-to-all | bytes 262144 | tf_op jit(solution)/shard_map/all_to_all | solution.py:18
  108.2 0.0 copy-done.3
  108.2 0.0 copy-done.5
  108.2 0.0 copy-done.6
  108.2 0.0 copy-done.7
  108.2 0.1 shard_map.133
  108.3 12.5 %all_to_all.43.ring_ref = bf16[8,5,8,512]{3,2,1,0:T(8,128)(2,1)S(1)} all-to-all(bf16[8,5,8,512]{3,2,1,0:T(8,128)(2,1)S(1)} %get-tuple-element.28), channel_id=1, replica_groups=mesh['z'=8,'y'=4,'c'=2,'x'=4] {'z'}, dimensions={0} | all-to-all | bytes 655360 | tf_op jit(solution)/shard_map/all_to_all | solution.py:18
  120.9 15.9 %all_to_all.44.squares_ref = f32[32,8,128]{2,1,0:T(8,128)S(1)} all-to-all(f32[32,8,128]{2,1,0:T(8,128)S(1)} %shard_map.134), channel_id=1, replica_groups=mesh['z'=8,'y'=4,'c'=2,'x'=4] {'y','c','x'}, dimensions={0} | all-to-all | bytes 262144 | tf_op jit(solution)/shard_map/all_to_all | solution.py:18
  136.8 0.7 shard_map.135
  137.5 0.2 broadcast_in_dim.15
  137.8 30.0 %all_to_all.45.parts_ref = bf16[16,8,2,8,512]{4,3,2,1,0:T(8,128)(2,1)S(1)} all-to-all(bf16[16,8,2,8,512]{4,3,2,1,0:T(8,128)(2,1)S(1)} %broadcast_in_dim.15), channel_id=1, replica_groups=mesh['z'=8,'y'=4,'c'=2,'x'=4] {'y','x'}, dimensions={0} | all-to-all | bytes 4194304 | tf_op jit(solution)/shard_map/all_to_all | solution.py:18
  167.8 2.0 collective-permute-start.10
  169.8 0.3 collective-permute-start.1
  170.1 1.1 collective-permute-start.2
  171.2 1.3 collective-permute-start.3
  172.5 3.6 %collective-permute-done.1 = bf16[8,8,512]{2,1,0:T(8,128)(2,1)S(1)} collective-permute-done((bf16[8,8,512]{2,1,0:T(8,128)(2,1)S(1)}, bf16[8,8,512]{2,1,0:T(8,128)(2,1)S(1)}, u32[]{:S(2)}, u32[]{:S(2)}) %collective-permute-start.1) | collective-permute-done | bytes 65568 | tf_op jit(solution)/shard_map/ppermute | solution.py:29
  176.0 0.0 collective-permute-done.2
  176.0 0.3 collective-permute-done.3
  176.4 0.3 collective-permute-start.4
  176.6 1.7 collective-permute-start.5
  178.4 0.9 collective-permute-start.6
  179.3 6.2 %collective-permute-done.4 = bf16[32,8,512]{2,1,0:T(8,128)(2,1)S(1)} collective-permute-done((bf16[32,8,512]{2,1,0:T(8,128)(2,1)S(1)}, bf16[32,8,512]{2,1,0:T(8,128)(2,1)S(1)}, u32[]{:S(2)}, u32[]{:S(2)}) %collective-permute-start.4) | collective-permute-done | bytes 262176 | tf_op jit(solution)/shard_map/ppermute | solution.py:29
  185.5 3.8 %collective-permute-done.5 = bf16[32,8,512]{2,1,0:T(8,128)(2,1)S(1)} collective-permute-done((bf16[32,8,512]{2,1,0:T(8,128)(2,1)S(1)}, bf16[32,8,512]{2,1,0:T(8,128)(2,1)S(1)}, u32[]{:S(2)}, u32[]{:S(2)}) %collective-permute-start.5) | collective-permute-done | bytes 262176 | tf_op jit(solution)/shard_map/ppermute | solution.py:29
  189.3 1.4 collective-permute-done.6
  190.7 0.1 pad_maximum_fusion
  190.8 2.2 %collective-permute-start.7 = (bf16[16,8,8,512]{3,2,1,0:T(8,128)(2,1)S(1)}, bf16[16,8,8,512]{3,2,1,0:T(8,128)(2,1)}, u32[]{:S(2)}, u32[]{:S(2)}) collective-permute-start(bf16[16,8,8,512]{3,2,1,0:T(8,128)(2,1)S(1)} %bitcast.11), channel_id=1, source_target_pairs={{0,4},{4,0},{1,5},{5,1},{2,6},{6,2},{3,7},{7,3},{8,12},{12,8},{9,1... | collective-permute-start | bytes 3145736 | tf_op jit(solution)/shard_map/ppermute | solution.py:34
  193.0 2.4 %collective-permute-done.7.other_ref = bf16[16,8,8,512]{3,2,1,0:T(8,128)(2,1)} collective-permute-done((bf16[16,8,8,512]{3,2,1,0:T(8,128)(2,1)S(1)}, bf16[16,8,8,512]{3,2,1,0:T(8,128)(2,1)}, u32[]{:S(2)}, u32[]{:S(2)}) %collective-permute-start.7) | collective-permute-done | bytes 1048608 | tf_op jit(solution)/shard_map/ppermute | solution.py:34
  195.4 1.1 copy-done.1
  196.5 5.0 %shard_map.128 = bf16[588,2048]{1,0:T(8,128)(2,1)} custom-call(s32[3]{0:T(128)S(1)} %pad_add_fusion.place_ref, bf16[588,2048]{1,0:T(8,128)(2,1)} %grad_ref.3, bf16[588,512]{1,0:T(8,128)(2,1)S(1)} %copy-done.1, bf16[16,8,8,512]{3,2,1,0:T(8,128)(2,1)S(1)} %bitcast.12, bf16[16,8,8,512]{3,2,1,0:T(8,128)(2,1)} %collective-permute-done.7.other_ref), custom_call_target="tpu_custom_call" | custom-call | flops 1233125376 | bytes 7516160 | tf_op jit(solution)/shard_map/pallas_call | solution.py:141
  201.6 1.6 shard_map.136
  203.1 0.0 collective-permute-done.10.parts_hbm
  203.2 2.6 %shard_map.137 = (bf16[8,4,2,4,8,512]{5,4,3,2,1,0:T(8,128)(2,1)}, bf16[8,4,2,4,8,512]{5,4,3,2,1,0:T(8,128)(2,1)}) custom-call(s32[1]{0:T(128)} %bitcast.6.core_ref, bf16[16,8,2,8,512]{4,3,2,1,0:T(8,128)(2,1)} %collective-permute-done.10.parts_hbm, ...), custom_call_target="tpu_custom_call", output_to_operand_aliasing={{0}: (2, {}), {1}: (3, {})} | custom-call | flops 1048576 | bytes 4194304 | tf_op jit(solution)/shard_map/pallas_call | solution.py:294
  (7 shorter events, 0.1 us)
Async XLA Ops:
  0.6 0.7 copy-start.2
  1.4 0.7 copy-start.4
  2.1 41.7 %copy-start.8 = (bf16[588,512]{1,0:T(8,128)(2,1)S(1)}, bf16[588,512]{1,0:T(8,128)(2,1)}, u32[]{:S(2)}) copy-start(bf16[588,512]{1,0:T(8,128)(2,1)} %hidden_ref.1) | copy-start | bytes 1806340
  40.4 6.9 %copy-start.9 = (bf16[16,8,8,512]{3,2,1,0:T(8,128)(2,1)}, bf16[16,8,8,512]{3,2,1,0:T(8,128)(2,1)S(1)}, u32[]{:S(2)}) copy-start(bf16[16,8,8,512]{3,2,1,0:T(8,128)(2,1)S(1)} %all_to_all.41.mine_ref) | copy-start | bytes 3145732
  40.4 7.3 %collective-permute-start = (bf16[16,8,8,512]{3,2,1,0:T(8,128)(2,1)S(1)}, bf16[16,8,8,512]{3,2,1,0:T(8,128)(2,1)}, u32[]{:S(2)}, u32[]{:S(2)}) collective-permute-start(bf16[16,8,8,512]{3,2,1,0:T(8,128)(2,1)S(1)} %all_to_all.41.mine_ref), channel_id=1, source_target_pairs={{0,4},{4,0},{1,5},{5,1},{2,6},{6,2},{3,7},{7,3},{8,12},{12,8},{9,1... | collective-permute-start | bytes 3145736 | tf_op jit(solution)/shard_map/ppermute | solution.py:34
  47.3 8.0 %collective-permute-start.8 = (bf16[16,8,8,512]{3,2,1,0:T(8,128)(2,1)S(1)}, bf16[16,8,8,512]{3,2,1,0:T(8,128)(2,1)S(1)}, u32[]{:S(2)}, u32[]{:S(2)}) collective-permute-start(bf16[16,8,8,512]{3,2,1,0:T(8,128)(2,1)S(1)} %get-tuple-element.25), channel_id=1, source_target_pairs={{0,4},{4,0},{1,5},{5,1},{2,6},{6,2},{3,7},{7,3},{8,12},{12,8},{9,1... | collective-permute-start | bytes 3145736 | tf_op jit(solution)/shard_map/ppermute | solution.py:34
  54.3 0.8 copy-start
  55.1 5.8 %collective-permute-start.9 = (bf16[16,8,8,512]{3,2,1,0:T(8,128)(2,1)S(1)}, bf16[16,8,8,512]{3,2,1,0:T(8,128)(2,1)S(1)}, u32[]{:S(2)}, u32[]{:S(2)}) collective-permute-start(bf16[16,8,8,512]{3,2,1,0:T(8,128)(2,1)S(1)} %get-tuple-element.27), channel_id=1, source_target_pairs={{0,4},{4,0},{1,5},{5,1},{2,6},{6,2},{3,7},{7,3},{8,12},{12,8},{9,1... | collective-permute-start | bytes 3145736 | tf_op jit(solution)/shard_map/ppermute | solution.py:34
  56.5 21.6 %all-to-all-start.2 = ((bf16[16,8,8,512]{3,2,1,0:T(8,128)(2,1)}), bf16[16,8,8,512]{3,2,1,0:T(8,128)(2,1)}, u32[]{:S(2)}, u32[]{:S(2)}) async-start(bf16[16,8,8,512]{3,2,1,0:T(8,128)(2,1)} %shard_map.130), calls=%async_computation.2 | async-start | bytes 2097152 | tf_op jit(solution)/shard_map/all_to_all | solution.py:18
  62.1 46.1 %copy-start.3 = (f32[8,512]{1,0:T(8,128)S(1)}, f32[8,512]{1,0:T(8,128)}, u32[]{:S(2)}) copy-start(f32[8,512]{1,0:T(8,128)} %me_ref.5) | copy-start | bytes 49156
  62.1 46.1 %copy-start.5 = (f32[8,512]{1,0:T(8,128)S(1)}, f32[8,512]{1,0:T(8,128)}, u32[]{:S(2)}) copy-start(f32[8,512]{1,0:T(8,128)} %mr_ref.5) | copy-start | bytes 49156
  62.1 46.1 %copy-start.6 = (f32[8,512]{1,0:T(8,128)S(1)}, f32[8,512]{1,0:T(8,128)}, u32[]{:S(2)}) copy-start(f32[8,512]{1,0:T(8,128)} %ve_ref.3) | copy-start | bytes 49156
  62.1 46.1 %copy-start.7 = (f32[8,512]{1,0:T(8,128)S(1)}, f32[8,512]{1,0:T(8,128)}, u32[]{:S(2)}) copy-start(f32[8,512]{1,0:T(8,128)} %vr_ref.3) | copy-start | bytes 49156
  78.1 19.6 %all-to-all-start.3 = ((bf16[16,8,8,512]{3,2,1,0:T(8,128)(2,1)}), bf16[16,8,8,512]{3,2,1,0:T(8,128)(2,1)S(1)}, u32[]{:S(2)}, u32[]{:S(2)}) async-start(bf16[16,8,8,512]{3,2,1,0:T(8,128)(2,1)} %shard_map.131), calls=%async_computation.3 | async-start | bytes 2097152 | tf_op jit(solution)/shard_map/all_to_all | solution.py:18
  167.8 35.3 %collective-permute-start.10 = (bf16[16,8,2,8,512]{4,3,2,1,0:T(8,128)(2,1)S(1)}, bf16[16,8,2,8,512]{4,3,2,1,0:T(8,128)(2,1)}, u32[]{:S(2)}, u32[]{:S(2)}) collective-permute-start(bf16[16,8,2,8,512]{4,3,2,1,0:T(8,128)(2,1)S(1)} %all_to_all.45.parts_ref), channel_id=1, source_target_pairs={{0,4},{4,0},{1,5},{5,1},{2,6},{6,2},{3,7},{7,3},{8,12},{12,8},{9,1... | collective-permute-start | bytes 6291464 | tf_op jit(solution)/shard_map/ppermute | solution.py:34
  169.8 6.3 %collective-permute-start.1 = (bf16[8,8,512]{2,1,0:T(8,128)(2,1)S(1)}, bf16[8,8,512]{2,1,0:T(8,128)(2,1)S(1)}, u32[]{:S(2)}, u32[]{:S(2)}) collective-permute-start(bf16[8,8,512]{2,1,0:T(8,128)(2,1)S(1)} %get-tuple-element.39), channel_id=1, source_target_pairs={{0,1},{1,2},{2,3},{3,0},{4,5},{5,6},{6,7},{7,4},{8,9},{9,10},{10,1... | collective-permute-start | bytes 196616 | tf_op jit(solution)/shard_map/ppermute | solution.py:29
  170.1 6.0 %collective-permute-start.2 = (bf16[8,8,512]{2,1,0:T(8,128)(2,1)S(1)}, bf16[8,8,512]{2,1,0:T(8,128)(2,1)S(1)}, u32[]{:S(2)}, u32[]{:S(2)}) collective-permute-start(bf16[8,8,512]{2,1,0:T(8,128)(2,1)S(1)} %get-tuple-element.39), channel_id=1, source_target_pairs={{0,2},{1,3},{2,0},{3,1},{4,6},{5,7},{6,4},{7,5},{8,10},{9,11},{10,... | collective-permute-start | bytes 196616 | tf_op jit(solution)/shard_map/ppermute | solution.py:29
  171.2 5.2 %collective-permute-start.3 = (bf16[8,8,512]{2,1,0:T(8,128)(2,1)S(1)}, bf16[8,8,512]{2,1,0:T(8,128)(2,1)S(1)}, u32[]{:S(2)}, u32[]{:S(2)}) collective-permute-start(bf16[8,8,512]{2,1,0:T(8,128)(2,1)S(1)} %get-tuple-element.39), channel_id=1, source_target_pairs={{0,3},{1,0},{2,1},{3,2},{4,7},{5,4},{6,5},{7,6},{8,11},{9,8},{10,9... | collective-permute-start | bytes 196616 | tf_op jit(solution)/shard_map/ppermute | solution.py:29
  176.4 9.1 %collective-permute-start.4 = (bf16[32,8,512]{2,1,0:T(8,128)(2,1)S(1)}, bf16[32,8,512]{2,1,0:T(8,128)(2,1)S(1)}, u32[]{:S(2)}, u32[]{:S(2)}) collective-permute-start(bf16[32,8,512]{2,1,0:T(8,128)(2,1)S(1)} %pad_maximum_fusion.1), channel_id=1, source_target_pairs={{0,8},{8,16},{16,24},{24,0},{1,9},{9,17},{17,25},{25,1},{2,10},{10... | collective-permute-start | bytes 786440 | tf_op jit(solution)/shard_map/ppermute | solution.py:29
  176.6 12.6 %collective-permute-start.5 = (bf16[32,8,512]{2,1,0:T(8,128)(2,1)S(1)}, bf16[32,8,512]{2,1,0:T(8,128)(2,1)S(1)}, u32[]{:S(2)}, u32[]{:S(2)}) collective-permute-start(bf16[32,8,512]{2,1,0:T(8,128)(2,1)S(1)} %pad_maximum_fusion.1), channel_id=1, source_target_pairs={{0,16},{8,24},{16,0},{24,8},{1,17},{9,25},{17,1},{25,9},{2,18},{10... | collective-permute-start | bytes 786440 | tf_op jit(solution)/shard_map/ppermute | solution.py:29
  178.4 12.3 %collective-permute-start.6 = (bf16[32,8,512]{2,1,0:T(8,128)(2,1)S(1)}, bf16[32,8,512]{2,1,0:T(8,128)(2,1)S(1)}, u32[]{:S(2)}, u32[]{:S(2)}) collective-permute-start(bf16[32,8,512]{2,1,0:T(8,128)(2,1)S(1)} %pad_maximum_fusion.1), channel_id=1, source_target_pairs={{0,24},{8,0},{16,8},{24,16},{1,25},{9,1},{17,9},{25,17},{2,26},{10... | collective-permute-start | bytes 786440 | tf_op jit(solution)/shard_map/ppermute | solution.py:29
  190.8 4.6 %collective-permute-start.7 = (bf16[16,8,8,512]{3,2,1,0:T(8,128)(2,1)S(1)}, bf16[16,8,8,512]{3,2,1,0:T(8,128)(2,1)}, u32[]{:S(2)}, u32[]{:S(2)}) collective-permute-start(bf16[16,8,8,512]{3,2,1,0:T(8,128)(2,1)S(1)} %bitcast.11), channel_id=1, source_target_pairs={{0,4},{4,0},{1,5},{5,1},{2,6},{6,2},{3,7},{7,3},{8,12},{12,8},{9,1... | collective-permute-start | bytes 3145736 | tf_op jit(solution)/shard_map/ppermute | solution.py:34
  195.4 1.1 copy-start.1

commit v7 on v6

--- a/solution.py
+++ b/solution.py
@@ -23,11 +23,15 @@
     return exchange(jnp.broadcast_to(block[None], (peers, *block.shape)), axes)
 
 
-def shifted(block, axis):
+def shifts(block, axis):
     pieces = [block]
     for s in range(1, 4):
         pieces.append(lax.ppermute(block, axis, [(i, (i + s) % 4) for i in range(4)]))
-    return jnp.concatenate(pieces)
+    return pieces
+
+
+def shifted(block, axis):
+    return jnp.concatenate(shifts(block, axis))
 
 
 def from_other_core(block):
@@ -182,28 +186,27 @@
             out_ref[z, at] = tile
 
 
-def ring_squares_kernel(ring_ref, out_ref):
+def ring_squares_kernel(ring_ref, out_ref, low_ref, high_ref):
     total = jnp.zeros((8, 128), F32)
     for z in range(8):
         packed = ring_ref[z, 4].astype(F32)
         total = total + ((packed[:, :128] + packed[:, 128:256]) + packed[:, 256:384])
+        half_ref = low_ref if z < 4 else high_ref
+        half_ref[z % 4] = ring_ref[z, :4]
     out_ref[...] = jnp.broadcast_to(total[None], out_ref.shape)
 
 
 def update_kernel(
     squares_ref,
-    ring_ref,
     grads_ref,
     me_ref,
     mr_ref,
     ve_ref,
     vr_ref,
-    new_me_ref,
-    new_mr_ref,
-    new_ve_ref,
-    new_vr_ref,
-    work_ref,
+    *refs,
 ):
+    low_refs, high_refs = refs[:4], refs[4:8]
+    new_me_ref, new_mr_ref, new_ve_ref, new_vr_ref, low_work_ref, high_work_ref = refs[8:]
     squares = squares_ref[0]
     for peer in range(1, squares_ref.shape[0]):
         squares = squares + squares_ref[peer]
@@ -220,12 +223,14 @@
         new_velocity = 0.9 * v_ref[...] + trust * (grads_ref[layer] + 5e-05 * master)
         new_v_ref[...] = new_velocity
         new_m_ref[...] = master - 0.1 * new_velocity
-        for z in range(8):
-            step = 0.1 * (trust * ring_ref[z, layer].astype(F32))
-            work_ref[z, layer] = (ring_ref[z, 2 + layer].astype(F32) - step).astype(BF)
-
-
-def small_call(kernel, operands, outs):
+        for half_refs, work_ref in ((low_refs, low_work_ref), (high_refs, high_work_ref)):
+            for s, half_ref in enumerate(half_refs):
+                for z in range(4):
+                    step = 0.1 * (trust * half_ref[z, layer].astype(F32))
+                    work_ref[s, z, layer] = (half_ref[z, 2 + layer].astype(F32) - step).astype(BF)
+
+
+def small_call(kernel, operands, outs, limit=16):
     whole = pl.BlockSpec(memory_space=pltpu.VMEM)
     moved = sum(x.size * x.dtype.itemsize for x in (*operands, *outs))
     return pl.pallas_call(
@@ -233,82 +238,61 @@
         out_shape=outs,
         in_specs=[whole] * len(operands),
         out_specs=[whole] * len(outs),
-        compiler_params=pltpu.CompilerParams(vmem_limit_bytes=16 * 1024 * 1024),
+        compiler_params=pltpu.CompilerParams(vmem_limit_bytes=limit * 1024 * 1024),
         cost_estimate=pl.CostEstimate(flops=moved, bytes_accessed=moved, transcendentals=0),
     )(*operands)
 
 
-def placements(core, y, parts_ref, out_refs, sems):
+def placements(at_ref, core, half, i, parts_ref, out_refs, sems):
     copies = []
-    for x in range(4):
+    for j in range(4):
+        x = lax.rem(at_ref[2] - (i if half else j) + 4, 4)
+        y = lax.rem(at_ref[1] - j + 4, 4) if half else i
         for layer, out_ref in enumerate(out_refs):
             copies.append(
                 pltpu.make_async_copy(
-                    parts_ref.at[y * 4 + x, :, layer],
-                    out_ref.at[:, y, core, x],
-                    sems.at[y * 8 + x * 2 + layer],
+                    parts_ref.at[i, j, :, layer],
+                    out_ref.at[pl.ds(half * 4, 4), y, core, x],
+                    sems.at[half * 32 + i * 8 + j * 2 + layer],
                 )
             )
     return copies
 
 
-def place_mine_kernel(core_ref, parts_ref, expand_ref, reduce_ref, sems):
+def place_kernel(other, at_ref, low_ref, high_ref, *refs):
+    expand_ref, reduce_ref, sems = refs[-3:]
+    core = 1 - at_ref[0] if other else at_ref[0]
     copies = []
-    for y in range(4):
-        copies += placements(core_ref[0], y, parts_ref, (expand_ref, reduce_ref), sems)
+    for half, parts_ref in enumerate((low_ref, high_ref)):
+        for i in range(4):
+            copies += placements(at_ref, core, half, i, parts_ref, (expand_ref, reduce_ref), sems)
     for copy in copies:
         copy.start()
     for copy in copies:
         copy.wait()
 
 
-def place_other_kernel(
-    core_ref, parts_hbm, _expand, _reduce, expand_ref, reduce_ref, parts_ref, sems, in_sems
-):
-    loads = [
-        pltpu.make_async_copy(
-            parts_hbm.at[pl.ds(y * 4, 4)], parts_ref.at[pl.ds(y * 4, 4)], in_sems.at[y]
-        )
-        for y in range(4)
-    ]
-    for load in loads:
-        load.start()
-    copies = []
-    for y in range(4):
-        loads[y].wait()
-        here = placements(core_ref[0], y, parts_ref, (expand_ref, reduce_ref), sems)
-        for copy in here:
-            copy.start()
-        copies += here
-    for copy in copies:
-        copy.wait()
-
-
-def place(core, parts, into):
-    _, z, _, r, n = parts.shape
-    whole = jax.ShapeDtypeStruct((z, 4, 2, 4, r, n), BF)
+def place(halves, into):
+    _, _, z, _, r, n = halves[0].shape
+    whole = jax.ShapeDtypeStruct((2 * z, 4, 2, 4, r, n), BF)
     hbm = pl.BlockSpec(memory_space=pl.ANY)
-    scratch = [pltpu.SemaphoreType.DMA((32,))]
-    if into:
-        scratch = [pltpu.VMEM(parts.shape, BF)] + scratch + [pltpu.SemaphoreType.DMA((4,))]
+    at = jnp.stack([lax.axis_index(axis).astype(jnp.int32) for axis in ("c", "y", "x")])
     return pl.pallas_call(
-        place_other_kernel if into else place_mine_kernel,
+        functools.partial(place_kernel, bool(into)),
         out_shape=(whole, whole),
-        in_specs=[
-            pl.BlockSpec(memory_space=pltpu.SMEM),
-            hbm if into else pl.BlockSpec(memory_space=pltpu.VMEM),
-        ]
+        in_specs=[pl.BlockSpec(memory_space=pltpu.SMEM)]
+        + [pl.BlockSpec(memory_space=pltpu.VMEM)] * 2
         + [hbm] * len(into),
         out_specs=(hbm, hbm),
-        scratch_shapes=scratch,
-        input_output_aliases={2 + at: at for at in range(len(into))},
+        scratch_shapes=[pltpu.SemaphoreType.DMA((64,))],
+        input_output_aliases={3 + at: at for at in range(len(into))},
         compiler_params=pltpu.CompilerParams(
-            vmem_limit_bytes=(60 if into else 8) * 1024 * 1024
+            vmem_limit_bytes=8 * 1024 * 1024
         ),
         cost_estimate=pl.CostEstimate(
-            flops=parts.size, bytes_accessed=4 * parts.size, transcendentals=0
+            flops=halves[0].size, bytes_accessed=8 * halves[0].size, transcendentals=0
         ),
-    )(core.astype(jnp.int32).reshape(1), parts, *into)
+    )(at, *halves, *into)
 
 
 def step(
@@ -326,6 +310,7 @@
         working_kernel,
         (master_expand, master_reduce),
         (jax.ShapeDtypeStruct((8, 2, *master_expand.shape), BF),),
+        60,
     )
     along_z = exchange(cur, "z")
     mine = everywhere(along_z[:, 0], ("y", "x"))
@@ -374,20 +359,27 @@
         ),
     )
     ring = exchange(rows, "z")
-    (squares,) = small_call(
-        ring_squares_kernel, (ring,), (jax.ShapeDtypeStruct((32, 8, 128), F32),)
+    quarter = jax.ShapeDtypeStruct((4, 4, *own.shape), BF)
+    squares, low, high = small_call(
+        ring_squares_kernel,
+        (ring,),
+        (jax.ShapeDtypeStruct((32, 8, 128), F32), quarter, quarter),
     )
     squares = exchange(squares, ("y", "c", "x"))
-    new_me, new_mr, new_ve, new_vr, work = small_call(
+    lows = shifts(low, "x")
+    highs = shifts(high, "y")
+    four = jax.ShapeDtypeStruct((4, 4, 2, *own.shape), BF)
+    new_me, new_mr, new_ve, new_vr, low_work, high_work = small_call(
         update_kernel,
-        (squares, ring, grads, *state),
-        (own, own, own, own, jax.ShapeDtypeStruct((8, 2, *own.shape), BF)),
-    )
-    mine = everywhere(work, ("y", "x"))
-    core = lax.axis_index("c")
-    other = from_other_core(mine)
-    placed = place(core, mine, ())
-    placed = place(1 - core, other, placed)
+        (squares, grads, *state, *lows, *highs),
+        (own, own, own, own, four, four),
+    )
+    low_mine = everywhere(low_work, "y")
+    high_mine = jnp.stack(shifts(high_work, "x"))
+    low_other = from_other_core(low_mine)
+    high_other = from_other_core(high_mine)
+    placed = place((low_mine, high_mine), ())
+    placed = place((low_other, high_other), placed)
     work_expand, work_reduce = (p.reshape(channels, middle) for p in placed)
     return (grad_in, new_mr, new_me, new_vr, new_ve, work_reduce, work_expand)
 

time: 207 us -> 196 us (0.947)
  blocking collectives: 107 us -> 61.1 us
  starting transfers between devices: 21.9 us -> 49.2 us
  waiting for transfers between devices: 48 us -> 52.7 us
  Pallas kernels: 22.8 us -> 26.3 us
    all_to_all x6 -> x4, blocking collectives: 107 us -> 61.1 us  [exchange(): return lax.all_to_all(parts, axes, 0, 0, tiled=True)]
    all_to_all x2 -> x4, starting transfers between devices: 8.25 us -> 22.8 us  [exchange(): return lax.all_to_all(parts, axes, 0, 0, tiled=True)]
    ppermute x6 -> x15, starting transfers between devices: 5.61 us -> 19.8 us  [shifts(): lax.ppermute(block, axis, [(i, (i + s) % 4) for i in range(4)])]
    ppermute x6 -> x15, waiting for transfers between devices: 15.2 us -> 18.6 us  [shifts(): lax.ppermute(block, axis, [(i, (i + s) % 4) for i in range(4)])]
    all_to_all x2 -> x4, waiting for transfers between devices: 30.3 us -> 33.3 us  [exchange(): return lax.all_to_all(parts, axes, 0, 0, tiled=True)]
    pallas_call x7, Pallas kernels: 3.45 us -> 5.64 us  [small_call(): pl.pallas_call(kernel, out_shape=outs, in_specs=[whole] * len(operands),...]
    ppermute x5 -> x6, starting transfers between devices: 8.07 us -> 6.68 us  [from_other_core(): return lax.ppermute(block, 'c', [(0, 1), (1, 0)])]
  transfers between devices with their start and end apart: 13 -> 25, of which waited for: 8 -> 7; matrix products, arithmetic and copies ran while one was open for 1% -> 1% of each run, Pallas kernels for 9% -> 11%
where the time goes in v7:
time: 196 us; the launch traced here: 195 us
  blocking collectives  61.1 us (31%)
  waiting for transfers between devices  52.7 us (27%)
  starting transfers between devices  49.2 us (25%)
  Pallas kernels  26.3 us (13%)
  local copies, waits for them, and re-layouts  3.11 us (2%)
    all_to_all x4, blocking collectives, exchange(): return lax.all_to_all(parts, axes, 0, 0, tiled=True)  61.1 us
    all_to_all x4, waiting for transfers between devices, exchange(): return lax.all_to_all(parts, axes, 0, 0, tiled=True)  33.3 us
    all_to_all x4, starting transfers between devices, exchange(): return lax.all_to_all(parts, axes, 0, 0, tiled=True)  22.8 us
    ppermute x15, starting transfers between devices, shifts(): lax.ppermute(block, axis, [(i, (i + s) % 4) for i in range(4)])  19.8 us
    ppermute x15, waiting for transfers between devices, shifts(): lax.ppermute(block, axis, [(i, (i + s) % 4) for i in range(4)])  18.6 us
    pallas_call x3, Pallas kernels, local_call(): pl.pallas_call(kernel, out_shape=outs, in_specs=[pl.BlockSpec(memory_spac...  15.2 us
    ppermute x6, starting transfers between devices, from_other_core(): return lax.ppermute(block, 'c', [(0, 1), (1, 0)])  6.68 us
    pallas_call x7, Pallas kernels, small_call(): pl.pallas_call(kernel, out_shape=outs, in_specs=[whole] * len(operands),...  5.64 us
  transfers between devices with their start and end apart: 25, of which 7 were waited for; matrix products, arithmetic and copies ran while one was open for 1% of the time, Pallas kernels for 11%

profile of v7, /device:TPU:1, one launch (start us, length us, event | category | flops | bytes accessed | tf_op | source)
XLA Modules:
  0.0 195.1 jit_solution(479265208340316087)
XLA Ops:
  0.6 1.5 shard_map.126
  2.1 16.8 %all_to_all.40 = bf16[8,2,8,512]{3,2,1,0:T(8,128)(2,1)S(1)} all-to-all(bf16[8,2,8,512]{3,2,1,0:T(8,128)(2,1)} %shard_map.126), channel_id=1, replica_groups=mesh['z'=8,'y'=4,'c'=2,'x'=4] {'z'}, dimensions={0} | all-to-all | bytes 262144 | tf_op jit(solution)/shard_map/all_to_all | solution.py:18
  18.9 0.1 broadcast_in_dim.14
  19.0 21.5 %all_to_all.41.mine_ref = bf16[16,8,8,512]{3,2,1,0:T(8,128)(2,1)S(1)} all-to-all(bf16[16,8,8,512]{3,2,1,0:T(8,128)(2,1)S(1)} %broadcast_in_dim.14), channel_id=1, replica_groups=mesh['z'=8,'y'=4,'c'=2,'x'=4] {'y','x'}, dimensions={0} | all-to-all | bytes 2097152 | tf_op jit(solution)/shard_map/all_to_all | solution.py:18
  40.5 3.3 %collective-permute-start = (bf16[16,8,8,512]{3,2,1,0:T(8,128)(2,1)S(1)}, bf16[16,8,8,512]{3,2,1,0:T(8,128)(2,1)}, u32[]{:S(2)}, u32[]{:S(2)}) collective-permute-start(bf16[16,8,8,512]{3,2,1,0:T(8,128)(2,1)S(1)} %all_to_all.41.mine_ref), channel_id=1, source_target_pairs={{0,4},{4,0},{1,5},{5,1},{2,6},{6,2},{3,7},{7,3},{8,12},{12,8},{9,1... | collective-permute-start | bytes 3145736 | tf_op jit(solution)/shard_map/ppermute | solution.py:38
  43.8 0.1 pad_add_fusion.place_ref.at_ref
  43.8 3.5 %shard_map.129 = (bf16[16,8,8,512]{3,2,1,0:T(8,128)(2,1)S(1)}, bf16[16,8,8,512]{3,2,1,0:T(8,128)(2,1)S(1)}) custom-call(s32[3]{0:T(128)S(1)} %pad_add_fusion.place_ref.at_ref, bf16[588,2048]{1,0:T(8,128)(2,1)} %grad_ref.3, bf16[588,512]{1,0:T(8,128)(2,1)S(1)} %copy-done.6), custom_call_target="tpu_custom_call" | custom-call | flops 1233125376 | bytes 5107712 | tf_op jit(solution)/shard_map/pallas_call | solution.py:145
  47.4 0.4 collective-permute-start.8
  47.8 6.6 %shard_map.127 = (bf16[588,512]{1,0:T(8,128)(2,1)S(1)}, bf16[16,8,8,512]{3,2,1,0:T(8,128)(2,1)S(1)}, bf16[16,8,8,512]{3,2,1,0:T(8,128)(2,1)S(1)}) custom-call(s32[3]{0:T(128)S(1)} %pad_add_fusion.place_ref.at_ref, bf16[588,512]{1,0:T(8,128)(2,1)S(1)} %copy-done.6, bf16[16,8,8,512]{3,2,1,0:T(8,128)(2,1)} %copy-done.7, ...), custom_call_target="tpu_custom_call" | custom-call | flops 2466250752 | bytes 10215424 | tf_op jit(solution)/shard_map/pallas_call | solution.py:145
  54.4 0.0 copy-start
  54.4 0.8 copy-done
  55.2 0.2 collective-permute-start.9
  55.4 1.2 shard_map.130
  56.6 4.3 %all-to-all-start.2 = ((bf16[16,8,8,512]{3,2,1,0:T(8,128)(2,1)}), bf16[16,8,8,512]{3,2,1,0:T(8,128)(2,1)}, u32[]{:S(2)}, u32[]{:S(2)}) async-start(bf16[16,8,8,512]{3,2,1,0:T(8,128)(2,1)} %shard_map.130), calls=%async_computation.2 | async-start | bytes 2097152 | tf_op jit(solution)/shard_map/all_to_all | solution.py:18
  60.9 0.0 collective-permute-done.9.got_ref
  61.0 1.2 shard_map.131
  62.2 16.0 %all-to-all-done.2 = bf16[16,8,8,512]{3,2,1,0:T(8,128)(2,1)} async-done(((bf16[16,8,8,512]{3,2,1,0:T(8,128)(2,1)}), bf16[16,8,8,512]{3,2,1,0:T(8,128)(2,1)}, u32[]{:S(2)}, u32[]{:S(2)}) %all-to-all-start.2) | async-done | bytes 1048608 | tf_op jit(solution)/shard_map/all_to_all | solution.py:18
  78.2 3.9 %all-to-all-start.3 = ((bf16[16,8,8,512]{3,2,1,0:T(8,128)(2,1)}), bf16[16,8,8,512]{3,2,1,0:T(8,128)(2,1)S(1)}, u32[]{:S(2)}, u32[]{:S(2)}) async-start(bf16[16,8,8,512]{3,2,1,0:T(8,128)(2,1)} %shard_map.131), calls=%async_computation.3 | async-start | bytes 2097152 | tf_op jit(solution)/shard_map/all_to_all | solution.py:18
  82.1 1.4 reduce_sum.12.expand_ref
  83.5 14.3 %all-to-all-done.3.reduce_ref = bf16[16,8,8,512]{3,2,1,0:T(8,128)(2,1)S(1)} async-done(((bf16[16,8,8,512]{3,2,1,0:T(8,128)(2,1)}), bf16[16,8,8,512]{3,2,1,0:T(8,128)(2,1)S(1)}, u32[]{:S(2)}, u32[]{:S(2)}) %all-to-all-start.3) | async-done | bytes 1048608 | tf_op jit(solution)/shard_map/all_to_all | solution.py:18
  97.8 0.1 shard_map.132
  98.0 10.3 %all_to_all.42.arrived_ref = bf16[8,2,8,512]{3,2,1,0:T(8,128)(2,1)S(1)} all-to-all(bf16[8,2,8,512]{3,2,1,0:T(8,128)(2,1)S(1)} %shard_map.132), channel_id=1, replica_groups=mesh['z'=8,'y'=4,'c'=2,'x'=4] {'z'}, dimensions={0} | all-to-all | bytes 262144 | tf_op jit(solution)/shard_map/all_to_all | solution.py:18
  108.3 0.1 shard_map.133
  108.4 12.5 %all_to_all.43.ring_ref = bf16[8,5,8,512]{3,2,1,0:T(8,128)(2,1)S(1)} all-to-all(bf16[8,5,8,512]{3,2,1,0:T(8,128)(2,1)S(1)} %get-tuple-element.32), channel_id=1, replica_groups=mesh['z'=8,'y'=4,'c'=2,'x'=4] {'z'}, dimensions={0} | all-to-all | bytes 655360 | tf_op jit(solution)/shard_map/all_to_all | solution.py:18
  120.9 0.7 shard_map.134
  121.6 0.3 collective-permute-start.10
  121.9 2.2 %collective-permute-start.11 = (bf16[4,4,8,512]{3,2,1,0:T(8,128)(2,1)S(1)}, bf16[4,4,8,512]{3,2,1,0:T(8,128)(2,1)S(1)}, u32[]{:S(2)}, u32[]{:S(2)}) collective-permute-start(bf16[4,4,8,512]{3,2,1,0:T(8,128)(2,1)S(1)} %get-tuple-element.35.refs_0_), channel_id=1, source_target_pairs={{0,2},{1,3},{2,0},{3,1},{4,6},{5,7},{6,4},{7,5},{8,10},{9,11},{10,... | collective-permute-start | bytes 393224 | tf_op jit(solution)/shard_map/ppermute | solution.py:29
  124.1 2.1 %collective-permute-start.12 = (bf16[4,4,8,512]{3,2,1,0:T(8,128)(2,1)S(1)}, bf16[4,4,8,512]{3,2,1,0:T(8,128)(2,1)S(1)}, u32[]{:S(2)}, u32[]{:S(2)}) collective-permute-start(bf16[4,4,8,512]{3,2,1,0:T(8,128)(2,1)S(1)} %get-tuple-element.35.refs_0_), channel_id=1, source_target_pairs={{0,3},{1,0},{2,1},{3,2},{4,7},{5,4},{6,5},{7,6},{8,11},{9,8},{10,9... | collective-permute-start | bytes 393224 | tf_op jit(solution)/shard_map/ppermute | solution.py:29
  126.2 0.0 collective-permute-start.13
  126.2 1.6 collective-permute-start.14
  127.8 0.3 collective-permute-done.10.refs_1_
  128.1 0.9 collective-permute-start.15
  128.9 11.0 %all-to-all-start.6 = ((f32[32,8,128]{2,1,0:T(8,128)}), f32[32,8,128]{2,1,0:T(8,128)S(1)}, u32[]{:S(2)}, u32[]{:S(2)}) async-start(f32[32,8,128]{2,1,0:T(8,128)} %get-tuple-element.33), calls=%async_computation.6 | async-start | bytes 262144 | tf_op jit(solution)/shard_map/all_to_all | solution.py:18
  139.9 1.4 collective-permute-start.1
  141.4 2.4 %collective-permute-start.2 = (bf16[8,8,512]{2,1,0:T(8,128)(2,1)S(1)}, bf16[8,8,512]{2,1,0:T(8,128)(2,1)S(1)}, u32[]{:S(2)}, u32[]{:S(2)}) collective-permute-start(bf16[8,8,512]{2,1,0:T(8,128)(2,1)S(1)} %get-tuple-element.47), channel_id=1, source_target_pairs={{0,2},{1,3},{2,0},{3,1},{4,6},{5,7},{6,4},{7,5},{8,10},{9,11},{10,... | collective-permute-start | bytes 196616 | tf_op jit(solution)/shard_map/ppermute | solution.py:29
  143.8 1.2 collective-permute-start.3
  144.9 3.0 %all-to-all-done.6.squares_ref = f32[32,8,128]{2,1,0:T(8,128)S(1)} async-done(((f32[32,8,128]{2,1,0:T(8,128)}), f32[32,8,128]{2,1,0:T(8,128)S(1)}, u32[]{:S(2)}, u32[]{:S(2)}) %all-to-all-start.6) | async-done | bytes 131104 | tf_op jit(solution)/shard_map/all_to_all | solution.py:18
  147.9 0.0 collective-permute-done.14.refs_6_
  147.9 0.0 collective-permute-done.15.refs_7_
  147.9 0.8 shard_map.135
  148.7 1.1 broadcast_in_dim.15
  149.8 3.5 %all-to-all-start.7 = ((bf16[4,4,4,2,8,512]{5,4,3,2,1,0:T(8,128)(2,1)}), bf16[4,4,4,2,8,512]{5,4,3,2,1,0:T(8,128)(2,1)S(1)}, u32[]{:S(2)}, u32[]{:S(2)}) async-start(bf16[4,4,4,2,8,512]{5,4,3,2,1,0:T(8,128)(2,1)} %broadcast_in_dim.15), calls=%async_computation.7 | async-start | bytes 2097152 | tf_op jit(solution)/shard_map/all_to_all | solution.py:18
  153.4 0.0 collective-permute-done.1
  153.4 0.0 collective-permute-done.2
  153.4 1.5 collective-permute-start.4
  154.9 2.4 %collective-permute-start.5 = (bf16[32,8,512]{2,1,0:T(8,128)(2,1)S(1)}, bf16[32,8,512]{2,1,0:T(8,128)(2,1)S(1)}, u32[]{:S(2)}, u32[]{:S(2)}) collective-permute-start(bf16[32,8,512]{2,1,0:T(8,128)(2,1)S(1)} %pad_maximum_fusion.2), channel_id=1, source_target_pairs={{0,16},{8,24},{16,0},{24,8},{1,17},{9,25},{17,1},{25,9},{2,18},{10... | collective-permute-start | bytes 786440 | tf_op jit(solution)/shard_map/ppermute | solution.py:29
  157.3 1.2 collective-permute-start.6
  158.5 2.0 %collective-permute-start.18 = (bf16[4,4,2,8,512]{4,3,2,1,0:T(8,128)(2,1)S(1)}, bf16[4,4,2,8,512]{4,3,2,1,0:T(8,128)(2,1)S(1)}, u32[]{:S(2)}, u32[]{:S(2)}) collective-permute-start(bf16[4,4,2,8,512]{4,3,2,1,0:T(8,128)(2,1)S(1)} %get-tuple-element.42), channel_id=1, source_target_pairs={{0,2},{1,3},{2,0},{3,1},{4,6},{5,7},{6,4},{7,5},{8,10},{9,11},{10,... | collective-permute-start | bytes 786440 | tf_op jit(solution)/shard_map/ppermute | solution.py:29
  160.5 13.1 %collective-permute-done.4 = bf16[32,8,512]{2,1,0:T(8,128)(2,1)S(1)} collective-permute-done((bf16[32,8,512]{2,1,0:T(8,128)(2,1)S(1)}, bf16[32,8,512]{2,1,0:T(8,128)(2,1)S(1)}, u32[]{:S(2)}, u32[]{:S(2)}) %collective-permute-start.4) | collective-permute-done | bytes 262176 | tf_op jit(solution)/shard_map/ppermute | solution.py:29
  173.5 0.7 collective-permute-start.19
  174.2 5.3 %collective-permute-done.5 = bf16[32,8,512]{2,1,0:T(8,128)(2,1)S(1)} collective-permute-done((bf16[32,8,512]{2,1,0:T(8,128)(2,1)S(1)}, bf16[32,8,512]{2,1,0:T(8,128)(2,1)S(1)}, u32[]{:S(2)}, u32[]{:S(2)}) %collective-permute-start.5) | collective-permute-done | bytes 262176 | tf_op jit(solution)/shard_map/ppermute | solution.py:29
  179.5 0.0 collective-permute-done.6
  179.5 0.1 pad_maximum_fusion
  179.6 1.3 collective-permute-start.7
  180.9 0.1 pad_maximum_fusion.1.high_ref
  181.0 1.4 collective-permute-start.20
  182.5 0.0 all-to-all-done.7.low_ref
  182.5 0.1 collective-permute-start.16
  182.6 0.7 collective-permute-done.7.other_ref
  183.3 1.1 copy-done.1
  184.4 5.0 %shard_map.128 = bf16[588,2048]{1,0:T(8,128)(2,1)} custom-call(s32[3]{0:T(128)S(1)} %pad_add_fusion.place_ref.at_ref, bf16[588,2048]{1,0:T(8,128)(2,1)} %grad_ref.3, bf16[588,512]{1,0:T(8,128)(2,1)S(1)} %copy-done.1, bf16[16,8,8,512]{3,2,1,0:T(8,128)(2,1)S(1)} %bitcast.15, bf16[16,8,8,512]{3,2,1,0:T(8,128)(2,1)} %collective-permute-done.7.other_ref), custom_call_target="tpu_custom_call" | custom-call | flops 1233125376 | bytes 7516160 | tf_op jit(solution)/shard_map/pallas_call | solution.py:145
  189.4 2.4 %shard_map.136 = (bf16[8,4,2,4,8,512]{5,4,3,2,1,0:T(8,128)(2,1)}, bf16[8,4,2,4,8,512]{5,4,3,2,1,0:T(8,128)(2,1)}) custom-call(s32[3]{0:T(128)S(1)} %pad_add_fusion.place_ref.at_ref, bf16[4,4,4,2,8,512]{5,4,3,2,1,0:T(8,128)(2,1)S(1)} %all-to-all-done.7.low_ref, bf16[4,4,4,2,8,512]{5,4,3,2,1,0:T(8,128)(2,1)S(1)} %pad_maximum_fusion.1.high_ref), custom_call_target="tpu_custom_call" | custom-call | flops 524288 | bytes 4194304 | tf_op jit(solution)/shard_map/pallas_call | solution.py:280
  191.8 0.0 collective-permute-done.16.low_ref
  191.8 3.1 %shard_map.137 = (bf16[8,4,2,4,8,512]{5,4,3,2,1,0:T(8,128)(2,1)}, bf16[8,4,2,4,8,512]{5,4,3,2,1,0:T(8,128)(2,1)}) custom-call(s32[3]{0:T(128)S(1)} %pad_add_fusion.place_ref.at_ref, bf16[4,4,4,2,8,512]{5,4,3,2,1,0:T(8,128)(2,1)S(1)} %collective-permute-done.16.low_ref, ...), custom_call_target="tpu_custom_call", output_to_operand_aliasing={{0}: (3, {}), {1}: (4, {})} | custom-call | flops 524288 | bytes 4194304 | tf_op jit(solution)/shard_map/pallas_call | solution.py:280
  (26 shorter events, 0.1 us)
Async XLA Ops:
  0.6 43.2 %copy-start.6 = (bf16[588,512]{1,0:T(8,128)(2,1)S(1)}, bf16[588,512]{1,0:T(8,128)(2,1)}, u32[]{:S(2)}) copy-start(bf16[588,512]{1,0:T(8,128)(2,1)} %hidden_ref.1) | copy-start | bytes 1806340
  40.5 6.9 %copy-start.7 = (bf16[16,8,8,512]{3,2,1,0:T(8,128)(2,1)}, bf16[16,8,8,512]{3,2,1,0:T(8,128)(2,1)S(1)}, u32[]{:S(2)}) copy-start(bf16[16,8,8,512]{3,2,1,0:T(8,128)(2,1)S(1)} %all_to_all.41.mine_ref) | copy-start | bytes 3145732
  40.5 7.3 %collective-permute-start = (bf16[16,8,8,512]{3,2,1,0:T(8,128)(2,1)S(1)}, bf16[16,8,8,512]{3,2,1,0:T(8,128)(2,1)}, u32[]{:S(2)}, u32[]{:S(2)}) collective-permute-start(bf16[16,8,8,512]{3,2,1,0:T(8,128)(2,1)S(1)} %all_to_all.41.mine_ref), channel_id=1, source_target_pairs={{0,4},{4,0},{1,5},{5,1},{2,6},{6,2},{3,7},{7,3},{8,12},{12,8},{9,1... | collective-permute-start | bytes 3145736 | tf_op jit(solution)/shard_map/ppermute | solution.py:38
  47.4 8.0 %collective-permute-start.8 = (bf16[16,8,8,512]{3,2,1,0:T(8,128)(2,1)S(1)}, bf16[16,8,8,512]{3,2,1,0:T(8,128)(2,1)S(1)}, u32[]{:S(2)}, u32[]{:S(2)}) collective-permute-start(bf16[16,8,8,512]{3,2,1,0:T(8,128)(2,1)S(1)} %get-tuple-element.29), channel_id=1, source_target_pairs={{0,4},{4,0},{1,5},{5,1},{2,6},{6,2},{3,7},{7,3},{8,12},{12,8},{9,1... | collective-permute-start | bytes 3145736 | tf_op jit(solution)/shard_map/ppermute | solution.py:38
  54.4 0.8 copy-start
  55.2 5.8 %collective-permute-start.9 = (bf16[16,8,8,512]{3,2,1,0:T(8,128)(2,1)S(1)}, bf16[16,8,8,512]{3,2,1,0:T(8,128)(2,1)S(1)}, u32[]{:S(2)}, u32[]{:S(2)}) collective-permute-start(bf16[16,8,8,512]{3,2,1,0:T(8,128)(2,1)S(1)} %get-tuple-element.31), channel_id=1, source_target_pairs={{0,4},{4,0},{1,5},{5,1},{2,6},{6,2},{3,7},{7,3},{8,12},{12,8},{9,1... | collective-permute-start | bytes 3145736 | tf_op jit(solution)/shard_map/ppermute | solution.py:38
  56.6 21.6 %all-to-all-start.2 = ((bf16[16,8,8,512]{3,2,1,0:T(8,128)(2,1)}), bf16[16,8,8,512]{3,2,1,0:T(8,128)(2,1)}, u32[]{:S(2)}, u32[]{:S(2)}) async-start(bf16[16,8,8,512]{3,2,1,0:T(8,128)(2,1)} %shard_map.130), calls=%async_computation.2 | async-start | bytes 2097152 | tf_op jit(solution)/shard_map/all_to_all | solution.py:18
  62.2 46.1 %copy-start.2 = (f32[8,512]{1,0:T(8,128)S(1)}, f32[8,512]{1,0:T(8,128)}, u32[]{:S(2)}) copy-start(f32[8,512]{1,0:T(8,128)} %me_ref.5) | copy-start | bytes 49156
  62.2 46.1 %copy-start.3 = (f32[8,512]{1,0:T(8,128)S(1)}, f32[8,512]{1,0:T(8,128)}, u32[]{:S(2)}) copy-start(f32[8,512]{1,0:T(8,128)} %mr_ref.5) | copy-start | bytes 49156
  62.2 46.1 %copy-start.4 = (f32[8,512]{1,0:T(8,128)S(1)}, f32[8,512]{1,0:T(8,128)}, u32[]{:S(2)}) copy-start(f32[8,512]{1,0:T(8,128)} %ve_ref.3) | copy-start | bytes 49156
  62.2 46.1 %copy-start.5 = (f32[8,512]{1,0:T(8,128)S(1)}, f32[8,512]{1,0:T(8,128)}, u32[]{:S(2)}) copy-start(f32[8,512]{1,0:T(8,128)} %vr_ref.3) | copy-start | bytes 49156
  78.2 19.6 %all-to-all-start.3 = ((bf16[16,8,8,512]{3,2,1,0:T(8,128)(2,1)}), bf16[16,8,8,512]{3,2,1,0:T(8,128)(2,1)S(1)}, u32[]{:S(2)}, u32[]{:S(2)}) async-start(bf16[16,8,8,512]{3,2,1,0:T(8,128)(2,1)} %shard_map.131), calls=%async_computation.3 | async-start | bytes 2097152 | tf_op jit(solution)/shard_map/all_to_all | solution.py:18
  121.6 6.4 %collective-permute-start.10 = (bf16[4,4,8,512]{3,2,1,0:T(8,128)(2,1)S(1)}, bf16[4,4,8,512]{3,2,1,0:T(8,128)(2,1)S(1)}, u32[]{:S(2)}, u32[]{:S(2)}) collective-permute-start(bf16[4,4,8,512]{3,2,1,0:T(8,128)(2,1)S(1)} %get-tuple-element.35.refs_0_), channel_id=1, source_target_pairs={{0,1},{1,2},{2,3},{3,0},{4,5},{5,6},{6,7},{7,4},{8,9},{9,10},{10,1... | collective-permute-start | bytes 393224 | tf_op jit(solution)/shard_map/ppermute | solution.py:29
  121.9 18.0 %collective-permute-start.11 = (bf16[4,4,8,512]{3,2,1,0:T(8,128)(2,1)S(1)}, bf16[4,4,8,512]{3,2,1,0:T(8,128)(2,1)S(1)}, u32[]{:S(2)}, u32[]{:S(2)}) collective-permute-start(bf16[4,4,8,512]{3,2,1,0:T(8,128)(2,1)S(1)} %get-tuple-element.35.refs_0_), channel_id=1, source_target_pairs={{0,2},{1,3},{2,0},{3,1},{4,6},{5,7},{6,4},{7,5},{8,10},{9,11},{10,... | collective-permute-start | bytes 393224 | tf_op jit(solution)/shard_map/ppermute | solution.py:29
  124.1 17.3 %collective-permute-start.12 = (bf16[4,4,8,512]{3,2,1,0:T(8,128)(2,1)S(1)}, bf16[4,4,8,512]{3,2,1,0:T(8,128)(2,1)S(1)}, u32[]{:S(2)}, u32[]{:S(2)}) collective-permute-start(bf16[4,4,8,512]{3,2,1,0:T(8,128)(2,1)S(1)} %get-tuple-element.35.refs_0_), channel_id=1, source_target_pairs={{0,3},{1,0},{2,1},{3,2},{4,7},{5,4},{6,5},{7,6},{8,11},{9,8},{10,9... | collective-permute-start | bytes 393224 | tf_op jit(solution)/shard_map/ppermute | solution.py:29
  126.2 17.6 %collective-permute-start.13 = (bf16[4,4,8,512]{3,2,1,0:T(8,128)(2,1)S(1)}, bf16[4,4,8,512]{3,2,1,0:T(8,128)(2,1)S(1)}, u32[]{:S(2)}, u32[]{:S(2)}) collective-permute-start(bf16[4,4,8,512]{3,2,1,0:T(8,128)(2,1)S(1)} %get-tuple-element.36.refs_4_), channel_id=1, source_target_pairs={{0,8},{8,16},{16,24},{24,0},{1,9},{9,17},{17,25},{25,1},{2,10},{10... | collective-permute-start | bytes 393224 | tf_op jit(solution)/shard_map/ppermute | solution.py:29
  126.2 21.8 %collective-permute-start.14 = (bf16[4,4,8,512]{3,2,1,0:T(8,128)(2,1)S(1)}, bf16[4,4,8,512]{3,2,1,0:T(8,128)(2,1)S(1)}, u32[]{:S(2)}, u32[]{:S(2)}) collective-permute-start(bf16[4,4,8,512]{3,2,1,0:T(8,128)(2,1)S(1)} %get-tuple-element.36.refs_4_), channel_id=1, source_target_pairs={{0,16},{8,24},{16,0},{24,8},{1,17},{9,25},{17,1},{25,9},{2,18},{10... | collective-permute-start | bytes 393224 | tf_op jit(solution)/shard_map/ppermute | solution.py:29
  128.1 19.9 %collective-permute-start.15 = (bf16[4,4,8,512]{3,2,1,0:T(8,128)(2,1)S(1)}, bf16[4,4,8,512]{3,2,1,0:T(8,128)(2,1)S(1)}, u32[]{:S(2)}, u32[]{:S(2)}) collective-permute-start(bf16[4,4,8,512]{3,2,1,0:T(8,128)(2,1)S(1)} %get-tuple-element.36.refs_4_), channel_id=1, source_target_pairs={{0,24},{8,0},{16,8},{24,16},{1,25},{9,1},{17,9},{25,17},{2,26},{10... | collective-permute-start | bytes 393224 | tf_op jit(solution)/shard_map/ppermute | solution.py:29
  128.9 19.0 %all-to-all-start.6 = ((f32[32,8,128]{2,1,0:T(8,128)}), f32[32,8,128]{2,1,0:T(8,128)S(1)}, u32[]{:S(2)}, u32[]{:S(2)}) async-start(f32[32,8,128]{2,1,0:T(8,128)} %get-tuple-element.33), calls=%async_computation.6 | async-start | bytes 262144 | tf_op jit(solution)/shard_map/all_to_all | solution.py:18
  139.9 13.4 %collective-permute-start.1 = (bf16[8,8,512]{2,1,0:T(8,128)(2,1)S(1)}, bf16[8,8,512]{2,1,0:T(8,128)(2,1)S(1)}, u32[]{:S(2)}, u32[]{:S(2)}) collective-permute-start(bf16[8,8,512]{2,1,0:T(8,128)(2,1)S(1)} %get-tuple-element.47), channel_id=1, source_target_pairs={{0,1},{1,2},{2,3},{3,0},{4,5},{5,6},{6,7},{7,4},{8,9},{9,10},{10,1... | collective-permute-start | bytes 196616 | tf_op jit(solution)/shard_map/ppermute | solution.py:29
  141.4 12.0 %collective-permute-start.2 = (bf16[8,8,512]{2,1,0:T(8,128)(2,1)S(1)}, bf16[8,8,512]{2,1,0:T(8,128)(2,1)S(1)}, u32[]{:S(2)}, u32[]{:S(2)}) collective-permute-start(bf16[8,8,512]{2,1,0:T(8,128)(2,1)S(1)} %get-tuple-element.47), channel_id=1, source_target_pairs={{0,2},{1,3},{2,0},{3,1},{4,6},{5,7},{6,4},{7,5},{8,10},{9,11},{10,... | collective-permute-start | bytes 196616 | tf_op jit(solution)/shard_map/ppermute | solution.py:29
  143.8 9.6 %collective-permute-start.3 = (bf16[8,8,512]{2,1,0:T(8,128)(2,1)S(1)}, bf16[8,8,512]{2,1,0:T(8,128)(2,1)S(1)}, u32[]{:S(2)}, u32[]{:S(2)}) collective-permute-start(bf16[8,8,512]{2,1,0:T(8,128)(2,1)S(1)} %get-tuple-element.47), channel_id=1, source_target_pairs={{0,3},{1,0},{2,1},{3,2},{4,7},{5,4},{6,5},{7,6},{8,11},{9,8},{10,9... | collective-permute-start | bytes 196616 | tf_op jit(solution)/shard_map/ppermute | solution.py:29
  149.8 32.6 %all-to-all-start.7 = ((bf16[4,4,4,2,8,512]{5,4,3,2,1,0:T(8,128)(2,1)}), bf16[4,4,4,2,8,512]{5,4,3,2,1,0:T(8,128)(2,1)S(1)}, u32[]{:S(2)}, u32[]{:S(2)}) async-start(bf16[4,4,4,2,8,512]{5,4,3,2,1,0:T(8,128)(2,1)} %broadcast_in_dim.15), calls=%async_computation.7 | async-start | bytes 2097152 | tf_op jit(solution)/shard_map/all_to_all | solution.py:18
  153.4 20.1 %collective-permute-start.4 = (bf16[32,8,512]{2,1,0:T(8,128)(2,1)S(1)}, bf16[32,8,512]{2,1,0:T(8,128)(2,1)S(1)}, u32[]{:S(2)}, u32[]{:S(2)}) collective-permute-start(bf16[32,8,512]{2,1,0:T(8,128)(2,1)S(1)} %pad_maximum_fusion.2), channel_id=1, source_target_pairs={{0,8},{8,16},{16,24},{24,0},{1,9},{9,17},{17,25},{25,1},{2,10},{10... | collective-permute-start | bytes 786440 | tf_op jit(solution)/shard_map/ppermute | solution.py:29
  154.9 24.6 %collective-permute-start.5 = (bf16[32,8,512]{2,1,0:T(8,128)(2,1)S(1)}, bf16[32,8,512]{2,1,0:T(8,128)(2,1)S(1)}, u32[]{:S(2)}, u32[]{:S(2)}) collective-permute-start(bf16[32,8,512]{2,1,0:T(8,128)(2,1)S(1)} %pad_maximum_fusion.2), channel_id=1, source_target_pairs={{0,16},{8,24},{16,0},{24,8},{1,17},{9,25},{17,1},{25,9},{2,18},{10... | collective-permute-start | bytes 786440 | tf_op jit(solution)/shard_map/ppermute | solution.py:29
  157.3 22.2 %collective-permute-start.6 = (bf16[32,8,512]{2,1,0:T(8,128)(2,1)S(1)}, bf16[32,8,512]{2,1,0:T(8,128)(2,1)S(1)}, u32[]{:S(2)}, u32[]{:S(2)}) collective-permute-start(bf16[32,8,512]{2,1,0:T(8,128)(2,1)S(1)} %pad_maximum_fusion.2), channel_id=1, source_target_pairs={{0,24},{8,0},{16,8},{24,16},{1,25},{9,1},{17,9},{25,17},{2,26},{10... | collective-permute-start | bytes 786440 | tf_op jit(solution)/shard_map/ppermute | solution.py:29
  158.5 22.4 %collective-permute-start.17 = (bf16[4,4,2,8,512]{4,3,2,1,0:T(8,128)(2,1)S(1)}, bf16[4,4,2,8,512]{4,3,2,1,0:T(8,128)(2,1)S(1)}, u32[]{:S(2)}, u32[]{:S(2)}) collective-permute-start(bf16[4,4,2,8,512]{4,3,2,1,0:T(8,128)(2,1)S(1)} %get-tuple-element.42), channel_id=1, source_target_pairs={{0,1},{1,2},{2,3},{3,0},{4,5},{5,6},{6,7},{7,4},{8,9},{9,10},{10,1... | collective-permute-start | bytes 786440 | tf_op jit(solution)/shard_map/ppermute | solution.py:29
  158.5 22.4 %collective-permute-start.18 = (bf16[4,4,2,8,512]{4,3,2,1,0:T(8,128)(2,1)S(1)}, bf16[4,4,2,8,512]{4,3,2,1,0:T(8,128)(2,1)S(1)}, u32[]{:S(2)}, u32[]{:S(2)}) collective-permute-start(bf16[4,4,2,8,512]{4,3,2,1,0:T(8,128)(2,1)S(1)} %get-tuple-element.42), channel_id=1, source_target_pairs={{0,2},{1,3},{2,0},{3,1},{4,6},{5,7},{6,4},{7,5},{8,10},{9,11},{10,... | collective-permute-start | bytes 786440 | tf_op jit(solution)/shard_map/ppermute | solution.py:29
  173.5 7.4 %collective-permute-start.19 = (bf16[4,4,2,8,512]{4,3,2,1,0:T(8,128)(2,1)S(1)}, bf16[4,4,2,8,512]{4,3,2,1,0:T(8,128)(2,1)S(1)}, u32[]{:S(2)}, u32[]{:S(2)}) collective-permute-start(bf16[4,4,2,8,512]{4,3,2,1,0:T(8,128)(2,1)S(1)} %get-tuple-element.42), channel_id=1, source_target_pairs={{0,3},{1,0},{2,1},{3,2},{4,7},{5,4},{6,5},{7,6},{8,11},{9,8},{10,9... | collective-permute-start | bytes 786440 | tf_op jit(solution)/shard_map/ppermute | solution.py:29
  179.6 3.7 %collective-permute-start.7 = (bf16[16,8,8,512]{3,2,1,0:T(8,128)(2,1)S(1)}, bf16[16,8,8,512]{3,2,1,0:T(8,128)(2,1)}, u32[]{:S(2)}, u32[]{:S(2)}) collective-permute-start(bf16[16,8,8,512]{3,2,1,0:T(8,128)(2,1)S(1)} %bitcast.14), channel_id=1, source_target_pairs={{0,4},{4,0},{1,5},{5,1},{2,6},{6,2},{3,7},{7,3},{8,12},{12,8},{9,1... | collective-permute-start | bytes 3145736 | tf_op jit(solution)/shard_map/ppermute | solution.py:38
  181.0 10.8 %collective-permute-start.20 = (bf16[4,4,4,2,8,512]{5,4,3,2,1,0:T(8,128)(2,1)S(1)}, bf16[4,4,4,2,8,512]{5,4,3,2,1,0:T(8,128)(2,1)}, u32[]{:S(2)}, u32[]{:S(2)}) collective-permute-start(bf16[4,4,4,2,8,512]{5,4,3,2,1,0:T(8,128)(2,1)S(1)} %pad_maximum_fusion.1.high_ref), channel_id=1, source_target_pairs={{0,4},{4,0},{1,5},{5,1},{2,6},{6,2},{3,7},{7,3},{8,12},{12,8},{9,1... | collective-permute-start | bytes 3145736 | tf_op jit(solution)/shard_map/ppermute | solution.py:38
  182.5 9.4 %collective-permute-start.16 = (bf16[4,4,4,2,8,512]{5,4,3,2,1,0:T(8,128)(2,1)S(1)}, bf16[4,4,4,2,8,512]{5,4,3,2,1,0:T(8,128)(2,1)S(1)}, u32[]{:S(2)}, u32[]{:S(2)}) collective-permute-start(bf16[4,4,4,2,8,512]{5,4,3,2,1,0:T(8,128)(2,1)S(1)} %all-to-all-done.7.low_ref), channel_id=1, source_target_pairs={{0,4},{4,0},{1,5},{5,1},{2,6},{6,2},{3,7},{7,3},{8,12},{12,8},{9,1... | collective-permute-start | bytes 3145736 | tf_op jit(solution)/shard_map/ppermute | solution.py:38
  183.3 1.1 copy-start.1

commit v8 on v7

--- a/solution.py
+++ b/solution.py
@@ -135,7 +135,7 @@
         out_ref[:, columns] = (grad_ref[:, columns].astype(F32) + back * inv_c).astype(BF)
 
 
-def local_call(kernel, operands, outs, scratch, flops, streamed=()):
+def local_call(kernel, operands, outs, scratch, flops, streamed=(), limit=50):
     whole = pl.BlockSpec(memory_space=pltpu.VMEM)
     at = jnp.stack([lax.axis_index(axis).astype(jnp.int32) for axis in ("c", "y", "x")])
     moved = sum(x.size * x.dtype.itemsize for x in (*operands, *streamed, *outs))
@@ -149,7 +149,7 @@
         + [pl.BlockSpec(memory_space=pltpu.HBM)] * len(streamed),
         out_specs=[whole] * len(outs),
         scratch_shapes=scratch,
-        compiler_params=pltpu.CompilerParams(vmem_limit_bytes=50 * 1024 * 1024),
+        compiler_params=pltpu.CompilerParams(vmem_limit_bytes=limit * 1024 * 1024),
         cost_estimate=pl.CostEstimate(flops=flops, bytes_accessed=moved, transcendentals=0),
     )(at, *operands, *streamed)
 
@@ -259,11 +259,11 @@
     return copies
 
 
-def place_kernel(other, at_ref, low_ref, high_ref, *refs):
+def place_kernel(other, halves, at_ref, *refs):
     expand_ref, reduce_ref, sems = refs[-3:]
     core = 1 - at_ref[0] if other else at_ref[0]
     copies = []
-    for half, parts_ref in enumerate((low_ref, high_ref)):
+    for half, parts_ref in zip(halves, refs):
         for i in range(4):
             copies += placements(at_ref, core, half, i, parts_ref, (expand_ref, reduce_ref), sems)
     for copy in copies:
@@ -272,27 +272,26 @@
         copy.wait()
 
 
-def place(halves, into):
-    _, _, z, _, r, n = halves[0].shape
+def place(other, halves, parts, into):
+    _, _, z, _, r, n = parts[0].shape
     whole = jax.ShapeDtypeStruct((2 * z, 4, 2, 4, r, n), BF)
     hbm = pl.BlockSpec(memory_space=pl.ANY)
     at = jnp.stack([lax.axis_index(axis).astype(jnp.int32) for axis in ("c", "y", "x")])
+    first = 1 + len(parts)
     return pl.pallas_call(
-        functools.partial(place_kernel, bool(into)),
+        functools.partial(place_kernel, other, halves),
         out_shape=(whole, whole),
         in_specs=[pl.BlockSpec(memory_space=pltpu.SMEM)]
-        + [pl.BlockSpec(memory_space=pltpu.VMEM)] * 2
+        + [pl.BlockSpec(memory_space=pltpu.VMEM)] * len(parts)
         + [hbm] * len(into),
         out_specs=(hbm, hbm),
         scratch_shapes=[pltpu.SemaphoreType.DMA((64,))],
-        input_output_aliases={3 + at: at for at in range(len(into))},
-        compiler_params=pltpu.CompilerParams(
-            vmem_limit_bytes=8 * 1024 * 1024
+        input_output_aliases={first + at: at for at in range(len(into))},
+        compiler_params=pltpu.CompilerParams(vmem_limit_bytes=8 * 1024 * 1024),
+        cost_estimate=pl.CostEstimate(
+            flops=parts[0].size, bytes_accessed=4 * len(parts) * parts[0].size, transcendentals=0
         ),
-        cost_estimate=pl.CostEstimate(
-            flops=halves[0].size, bytes_accessed=8 * halves[0].size, transcendentals=0
-        ),
-    )(at, *halves, *into)
+    )(at, *parts, *into)
 
 
 def step(
@@ -346,6 +345,7 @@
         (jax.ShapeDtypeStruct(grad_out.shape, BF),),
         [whole],
         flops,
+        limit=62,
     )
 
     state = (master_expand, master_reduce, velocity_expand, velocity_reduce)
@@ -378,8 +378,9 @@
     high_mine = jnp.stack(shifts(high_work, "x"))
     low_other = from_other_core(low_mine)
     high_other = from_other_core(high_mine)
-    placed = place((low_mine, high_mine), ())
-    placed = place((low_other, high_other), placed)
+    placed = place(False, (0, 1), (low_mine, high_mine), ())
+    placed = place(True, (1,), (high_other,), placed)
+    placed = place(True, (0,), (low_other,), placed)
     work_expand, work_reduce = (p.reshape(channels, middle) for p in placed)
     return (grad_in, new_mr, new_me, new_vr, new_ve, work_reduce, work_expand)
 

time: 196 us -> 200 us (1.020)
  Pallas kernels: 26.3 us -> 30.8 us
    pallas_call x2 -> x3, Pallas kernels: 5.49 us -> 8.61 us  [place(): pl.pallas_call(functools.partial(place_kernel, other, halves), out_shape=...]
  transfers between devices with their start and end apart: 25 -> 25, of which waited for: 7 -> 6; matrix products, arithmetic and copies ran while one was open for 1% -> 1% of each run, Pallas kernels for 11% -> 13%
where the time goes in v8:
time: 200 us; the launch traced here: 198 us
  blocking collectives  61.1 us (31%)
  waiting for transfers between devices  53.1 us (27%)
  starting transfers between devices  48.3 us (24%)
  Pallas kernels  30.8 us (15%)
  local copies, waits for them, and re-layouts  2.06 us (1%)
    all_to_all x4, blocking collectives, exchange(): return lax.all_to_all(parts, axes, 0, 0, tiled=True)  61.1 us
    all_to_all x4, waiting for transfers between devices, exchange(): return lax.all_to_all(parts, axes, 0, 0, tiled=True)  34.5 us
    all_to_all x4, starting transfers between devices, exchange(): return lax.all_to_all(parts, axes, 0, 0, tiled=True)  22 us
    ppermute x15, starting transfers between devices, shifts(): lax.ppermute(block, axis, [(i, (i + s) % 4) for i in range(4)])  19.8 us
    ppermute x15, waiting for transfers between devices, shifts(): lax.ppermute(block, axis, [(i, (i + s) % 4) for i in range(4)])  18.6 us
    pallas_call x3, Pallas kernels, local_call(): pl.pallas_call(kernel, out_shape=outs, in_specs=[pl.BlockSpec(memory_spac...  16.6 us
    pallas_call x3, Pallas kernels, place(): pl.pallas_call(functools.partial(place_kernel, other, halves), out_shape=...  8.61 us
    ppermute x6, starting transfers between devices, from_other_core(): return lax.ppermute(block, 'c', [(0, 1), (1, 0)])  6.48 us
  transfers between devices with their start and end apart: 25, of which 6 were waited for; matrix products, arithmetic and copies ran while one was open for 1% of the time, Pallas kernels for 13%

profile of v8, /device:TPU:1, one launch (start us, length us, event | category | flops | bytes accessed | tf_op | source)
XLA Modules:
  0.0 198.0 jit_solution(8165527627136149650)
XLA Ops:
  0.6 1.5 shard_map.126
  2.1 16.8 %all_to_all.40 = bf16[8,2,8,512]{3,2,1,0:T(8,128)(2,1)S(1)} all-to-all(bf16[8,2,8,512]{3,2,1,0:T(8,128)(2,1)} %shard_map.126), channel_id=1, replica_groups=mesh['z'=8,'y'=4,'c'=2,'x'=4] {'z'}, dimensions={0} | all-to-all | bytes 262144 | tf_op jit(solution)/shard_map/all_to_all | solution.py:18
  18.9 0.1 broadcast_in_dim.14
  19.0 21.5 %all_to_all.41.mine_ref = bf16[16,8,8,512]{3,2,1,0:T(8,128)(2,1)S(1)} all-to-all(bf16[16,8,8,512]{3,2,1,0:T(8,128)(2,1)S(1)} %broadcast_in_dim.14), channel_id=1, replica_groups=mesh['z'=8,'y'=4,'c'=2,'x'=4] {'y','x'}, dimensions={0} | all-to-all | bytes 2097152 | tf_op jit(solution)/shard_map/all_to_all | solution.py:18
  40.5 3.3 %collective-permute-start = (bf16[16,8,8,512]{3,2,1,0:T(8,128)(2,1)S(1)}, bf16[16,8,8,512]{3,2,1,0:T(8,128)(2,1)}, u32[]{:S(2)}, u32[]{:S(2)}) collective-permute-start(bf16[16,8,8,512]{3,2,1,0:T(8,128)(2,1)S(1)} %all_to_all.41.mine_ref), channel_id=1, source_target_pairs={{0,4},{4,0},{1,5},{5,1},{2,6},{6,2},{3,7},{7,3},{8,12},{12,8},{9,1... | collective-permute-start | bytes 3145736 | tf_op jit(solution)/shard_map/ppermute | solution.py:38
  43.8 0.1 pad_add_fusion.place_ref.at_ref
  43.8 3.5 %shard_map.129 = (bf16[16,8,8,512]{3,2,1,0:T(8,128)(2,1)S(1)}, bf16[16,8,8,512]{3,2,1,0:T(8,128)(2,1)S(1)}) custom-call(s32[3]{0:T(128)S(1)} %pad_add_fusion.place_ref.at_ref, bf16[588,2048]{1,0:T(8,128)(2,1)} %grad_ref.3, bf16[588,512]{1,0:T(8,128)(2,1)S(1)} %copy-done.7), custom_call_target="tpu_custom_call" | custom-call | flops 1233125376 | bytes 5107712 | tf_op jit(solution)/shard_map/pallas_call | solution.py:145
  47.4 0.4 collective-permute-start.8
  47.8 0.0 collective-permute-done.other_ref
  47.8 7.5 %shard_map.127 = (bf16[588,512]{1,0:T(8,128)(2,1)S(1)}, bf16[16,8,8,512]{3,2,1,0:T(8,128)(2,1)S(1)}, bf16[16,8,8,512]{3,2,1,0:T(8,128)(2,1)}) custom-call(s32[3]{0:T(128)S(1)} %pad_add_fusion.place_ref.at_ref, bf16[588,512]{1,0:T(8,128)(2,1)S(1)} %copy-done.7, bf16[16,8,8,512]{3,2,1,0:T(8,128)(2,1)} %copy-done.9, ...), custom_call_target="tpu_custom_call" | custom-call | flops 2466250752 | bytes 10215424 | tf_op jit(solution)/shard_map/pallas_call | solution.py:145
  55.3 0.8 copy-done
  56.2 0.2 collective-permute-start.9
  56.4 0.0 collective-permute-done.8.got_ref
  56.4 1.2 shard_map.130
  57.6 3.7 %all-to-all-start.2 = ((bf16[16,8,8,512]{3,2,1,0:T(8,128)(2,1)}), bf16[16,8,8,512]{3,2,1,0:T(8,128)(2,1)S(1)}, u32[]{:S(2)}, u32[]{:S(2)}) async-start(bf16[16,8,8,512]{3,2,1,0:T(8,128)(2,1)} %shard_map.130), calls=%async_computation.2 | async-start | bytes 2097152 | tf_op jit(solution)/shard_map/all_to_all | solution.py:18
  61.2 0.0 collective-permute-done.9.got_ref
  61.3 1.2 shard_map.131
  62.5 16.0 %all-to-all-done.2 = bf16[16,8,8,512]{3,2,1,0:T(8,128)(2,1)S(1)} async-done(((bf16[16,8,8,512]{3,2,1,0:T(8,128)(2,1)}), bf16[16,8,8,512]{3,2,1,0:T(8,128)(2,1)S(1)}, u32[]{:S(2)}, u32[]{:S(2)}) %all-to-all-start.2) | async-done | bytes 1048608 | tf_op jit(solution)/shard_map/all_to_all | solution.py:18
  78.5 3.9 %all-to-all-start.3 = ((bf16[16,8,8,512]{3,2,1,0:T(8,128)(2,1)}), bf16[16,8,8,512]{3,2,1,0:T(8,128)(2,1)S(1)}, u32[]{:S(2)}, u32[]{:S(2)}) async-start(bf16[16,8,8,512]{3,2,1,0:T(8,128)(2,1)} %shard_map.131), calls=%async_computation.3 | async-start | bytes 2097152 | tf_op jit(solution)/shard_map/all_to_all | solution.py:18
  82.4 0.2 reduce_sum.12.expand_ref
  82.5 15.5 %all-to-all-done.3.reduce_ref = bf16[16,8,8,512]{3,2,1,0:T(8,128)(2,1)S(1)} async-done(((bf16[16,8,8,512]{3,2,1,0:T(8,128)(2,1)}), bf16[16,8,8,512]{3,2,1,0:T(8,128)(2,1)S(1)}, u32[]{:S(2)}, u32[]{:S(2)}) %all-to-all-start.3) | async-done | bytes 1048608 | tf_op jit(solution)/shard_map/all_to_all | solution.py:18
  98.1 0.1 shard_map.132
  98.2 10.3 %all_to_all.42.arrived_ref = bf16[8,2,8,512]{3,2,1,0:T(8,128)(2,1)S(1)} all-to-all(bf16[8,2,8,512]{3,2,1,0:T(8,128)(2,1)S(1)} %shard_map.132), channel_id=1, replica_groups=mesh['z'=8,'y'=4,'c'=2,'x'=4] {'z'}, dimensions={0} | all-to-all | bytes 262144 | tf_op jit(solution)/shard_map/all_to_all | solution.py:18
  108.5 0.1 shard_map.133
  108.7 12.5 %all_to_all.43.ring_ref = bf16[8,5,8,512]{3,2,1,0:T(8,128)(2,1)S(1)} all-to-all(bf16[8,5,8,512]{3,2,1,0:T(8,128)(2,1)S(1)} %get-tuple-element.34), channel_id=1, replica_groups=mesh['z'=8,'y'=4,'c'=2,'x'=4] {'z'}, dimensions={0} | all-to-all | bytes 655360 | tf_op jit(solution)/shard_map/all_to_all | solution.py:18
  121.2 0.7 shard_map.134
  121.9 0.3 collective-permute-start.10
  122.1 2.1 %collective-permute-start.11 = (bf16[4,4,8,512]{3,2,1,0:T(8,128)(2,1)S(1)}, bf16[4,4,8,512]{3,2,1,0:T(8,128)(2,1)S(1)}, u32[]{:S(2)}, u32[]{:S(2)}) collective-permute-start(bf16[4,4,8,512]{3,2,1,0:T(8,128)(2,1)S(1)} %get-tuple-element.37.refs_0_), channel_id=1, source_target_pairs={{0,2},{1,3},{2,0},{3,1},{4,6},{5,7},{6,4},{7,5},{8,10},{9,11},{10,... | collective-permute-start | bytes 393224 | tf_op jit(solution)/shard_map/ppermute | solution.py:29
  124.2 1.7 collective-permute-start.12
  125.9 0.3 collective-permute-start.13
  126.2 1.8 collective-permute-start.14
  128.1 0.2 collective-permute-done.10.refs_1_
  128.3 0.9 collective-permute-start.15
  129.2 11.0 %all-to-all-start.6 = ((f32[32,8,128]{2,1,0:T(8,128)}), f32[32,8,128]{2,1,0:T(8,128)S(1)}, u32[]{:S(2)}, u32[]{:S(2)}) async-start(f32[32,8,128]{2,1,0:T(8,128)} %get-tuple-element.35), calls=%async_computation.6 | async-start | bytes 262144 | tf_op jit(solution)/shard_map/all_to_all | solution.py:18
  140.2 1.4 collective-permute-start.1
  141.6 2.4 %collective-permute-start.2 = (bf16[8,8,512]{2,1,0:T(8,128)(2,1)S(1)}, bf16[8,8,512]{2,1,0:T(8,128)(2,1)S(1)}, u32[]{:S(2)}, u32[]{:S(2)}) collective-permute-start(bf16[8,8,512]{2,1,0:T(8,128)(2,1)S(1)} %get-tuple-element.51), channel_id=1, source_target_pairs={{0,2},{1,3},{2,0},{3,1},{4,6},{5,7},{6,4},{7,5},{8,10},{9,11},{10,... | collective-permute-start | bytes 196616 | tf_op jit(solution)/shard_map/ppermute | solution.py:29
  144.0 1.2 collective-permute-start.3
  145.2 3.0 %all-to-all-done.6.squares_ref = f32[32,8,128]{2,1,0:T(8,128)S(1)} async-done(((f32[32,8,128]{2,1,0:T(8,128)}), f32[32,8,128]{2,1,0:T(8,128)S(1)}, u32[]{:S(2)}, u32[]{:S(2)}) %all-to-all-start.6) | async-done | bytes 131104 | tf_op jit(solution)/shard_map/all_to_all | solution.py:18
  148.2 0.8 shard_map.135
  149.0 1.1 broadcast_in_dim.15
  150.1 3.5 %all-to-all-start.7 = ((bf16[4,4,4,2,8,512]{5,4,3,2,1,0:T(8,128)(2,1)}), bf16[4,4,4,2,8,512]{5,4,3,2,1,0:T(8,128)(2,1)S(1)}, u32[]{:S(2)}, u32[]{:S(2)}) async-start(bf16[4,4,4,2,8,512]{5,4,3,2,1,0:T(8,128)(2,1)} %broadcast_in_dim.15), calls=%async_computation.7 | async-start | bytes 2097152 | tf_op jit(solution)/shard_map/all_to_all | solution.py:18
  153.6 0.0 collective-permute-done.1
  153.6 0.0 collective-permute-done.2
  153.7 1.5 collective-permute-start.4
  155.2 2.4 %collective-permute-start.5 = (bf16[32,8,512]{2,1,0:T(8,128)(2,1)S(1)}, bf16[32,8,512]{2,1,0:T(8,128)(2,1)S(1)}, u32[]{:S(2)}, u32[]{:S(2)}) collective-permute-start(bf16[32,8,512]{2,1,0:T(8,128)(2,1)S(1)} %pad_maximum_fusion.2), channel_id=1, source_target_pairs={{0,16},{8,24},{16,0},{24,8},{1,17},{9,25},{17,1},{25,9},{2,18},{10... | collective-permute-start | bytes 786440 | tf_op jit(solution)/shard_map/ppermute | solution.py:29
  157.6 1.2 collective-permute-start.6
  158.7 2.0 collective-permute-start.18
  160.7 13.1 %collective-permute-done.4 = bf16[32,8,512]{2,1,0:T(8,128)(2,1)S(1)} collective-permute-done((bf16[32,8,512]{2,1,0:T(8,128)(2,1)S(1)}, bf16[32,8,512]{2,1,0:T(8,128)(2,1)S(1)}, u32[]{:S(2)}, u32[]{:S(2)}) %collective-permute-start.4) | collective-permute-done | bytes 262176 | tf_op jit(solution)/shard_map/ppermute | solution.py:29
  173.8 0.7 collective-permute-start.19
  174.5 5.3 %collective-permute-done.5 = bf16[32,8,512]{2,1,0:T(8,128)(2,1)S(1)} collective-permute-done((bf16[32,8,512]{2,1,0:T(8,128)(2,1)S(1)}, bf16[32,8,512]{2,1,0:T(8,128)(2,1)S(1)}, u32[]{:S(2)}, u32[]{:S(2)}) %collective-permute-start.5) | collective-permute-done | bytes 262176 | tf_op jit(solution)/shard_map/ppermute | solution.py:29
  179.7 0.0 collective-permute-done.6
  179.7 0.1 pad_maximum_fusion
  179.9 0.0 copy-start.8
  179.9 1.3 collective-permute-start.7
  181.1 0.0 collective-permute-done.17
  181.2 1.1 pad_maximum_fusion.1.refs_1_
  182.3 1.3 collective-permute-start.20
  183.6 0.0 all-to-all-done.7.refs_0_
  183.6 0.0 collective-permute-start.16
  183.6 5.5 %shard_map.128 = bf16[588,2048]{1,0:T(8,128)(2,1)} custom-call(s32[3]{0:T(128)} %copy-done.5, bf16[588,2048]{1,0:T(8,128)(2,1)} %grad_ref.3, bf16[588,512]{1,0:T(8,128)(2,1)} %copy-done, bf16[16,8,8,512]{3,2,1,0:T(8,128)(2,1)} %bitcast.18, bf16[16,8,8,512]{3,2,1,0:T(8,128)(2,1)} %collective-permute-done.7.other_ref), custom_call_target="tpu_custom_call" | custom-call | flops 1233125376 | bytes 7516160 | tf_op jit(solution)/shard_map/pallas_call | solution.py:145
  189.2 3.1 %shard_map.136 = (bf16[8,4,2,4,8,512]{5,4,3,2,1,0:T(8,128)(2,1)}, bf16[8,4,2,4,8,512]{5,4,3,2,1,0:T(8,128)(2,1)}) custom-call(s32[3]{0:T(128)S(1)} %copy-done.6, bf16[4,4,4,2,8,512]{5,4,3,2,1,0:T(8,128)(2,1)S(1)} %all-to-all-done.7.refs_0_, bf16[4,4,4,2,8,512]{5,4,3,2,1,0:T(8,128)(2,1)} %pad_maximum_fusion.1.refs_1_), custom_call_target="tpu_custom_call" | custom-call | flops 524288 | bytes 4194304 | tf_op jit(solution)/shard_map/pallas_call | solution.py:281
  192.3 0.0 collective-permute-done.20.refs_0_
  192.3 2.8 %shard_map.137 = (bf16[8,4,2,4,8,512]{5,4,3,2,1,0:T(8,128)(2,1)}, bf16[8,4,2,4,8,512]{5,4,3,2,1,0:T(8,128)(2,1)}) custom-call(s32[3]{0:T(128)S(1)} %copy-done.6, bf16[4,4,4,2,8,512]{5,4,3,2,1,0:T(8,128)(2,1)} %collective-permute-done.20.refs_0_, ...), custom_call_target="tpu_custom_call", output_to_operand_aliasing={{0}: (2, {}), {1}: (3, {})} | custom-call | flops 524288 | bytes 2097152 | tf_op jit(solution)/shard_map/pallas_call | solution.py:281
  195.0 2.8 %shard_map.138 = (bf16[8,4,2,4,8,512]{5,4,3,2,1,0:T(8,128)(2,1)}, bf16[8,4,2,4,8,512]{5,4,3,2,1,0:T(8,128)(2,1)}) custom-call(s32[3]{0:T(128)S(1)} %copy-done.6, bf16[4,4,4,2,8,512]{5,4,3,2,1,0:T(8,128)(2,1)} %collective-permute-done.16.refs_0_, ...), custom_call_target="tpu_custom_call", output_to_operand_aliasing={{0}: (2, {}), {1}: (3, {})} | custom-call | flops 524288 | bytes 2097152 | tf_op jit(solution)/shard_map/pallas_call | solution.py:281
  (31 shorter events, 0.1 us)
Async XLA Ops:
  0.6 43.2 %copy-start.7 = (bf16[588,512]{1,0:T(8,128)(2,1)S(1)}, bf16[588,512]{1,0:T(8,128)(2,1)}, u32[]{:S(2)}) copy-start(bf16[588,512]{1,0:T(8,128)(2,1)} %hidden_ref.1) | copy-start | bytes 1806340
  40.5 6.9 %copy-start.9 = (bf16[16,8,8,512]{3,2,1,0:T(8,128)(2,1)}, bf16[16,8,8,512]{3,2,1,0:T(8,128)(2,1)S(1)}, u32[]{:S(2)}) copy-start(bf16[16,8,8,512]{3,2,1,0:T(8,128)(2,1)S(1)} %all_to_all.41.mine_ref) | copy-start | bytes 3145732
  40.5 7.3 %collective-permute-start = (bf16[16,8,8,512]{3,2,1,0:T(8,128)(2,1)S(1)}, bf16[16,8,8,512]{3,2,1,0:T(8,128)(2,1)}, u32[]{:S(2)}, u32[]{:S(2)}) collective-permute-start(bf16[16,8,8,512]{3,2,1,0:T(8,128)(2,1)S(1)} %all_to_all.41.mine_ref), channel_id=1, source_target_pairs={{0,4},{4,0},{1,5},{5,1},{2,6},{6,2},{3,7},{7,3},{8,12},{12,8},{9,1... | collective-permute-start | bytes 3145736 | tf_op jit(solution)/shard_map/ppermute | solution.py:38
  43.8 3.9 %copy-start.5 = (s32[3]{0:T(128)}, s32[3]{0:T(128)S(1)}, u32[]{:S(2)}) copy-start(s32[3]{0:T(128)S(1)} %pad_add_fusion.place_ref.at_ref) | copy-start | bytes 40
  47.4 9.0 %collective-permute-start.8 = (bf16[16,8,8,512]{3,2,1,0:T(8,128)(2,1)S(1)}, bf16[16,8,8,512]{3,2,1,0:T(8,128)(2,1)S(1)}, u32[]{:S(2)}, u32[]{:S(2)}) collective-permute-start(bf16[16,8,8,512]{3,2,1,0:T(8,128)(2,1)S(1)} %get-tuple-element.31), channel_id=1, source_target_pairs={{0,4},{4,0},{1,5},{5,1},{2,6},{6,2},{3,7},{7,3},{8,12},{12,8},{9,1... | collective-permute-start | bytes 3145736 | tf_op jit(solution)/shard_map/ppermute | solution.py:38
  55.3 0.8 copy-start
  56.2 5.1 %collective-permute-start.9 = (bf16[16,8,8,512]{3,2,1,0:T(8,128)(2,1)}, bf16[16,8,8,512]{3,2,1,0:T(8,128)(2,1)S(1)}, u32[]{:S(2)}, u32[]{:S(2)}) collective-permute-start(bf16[16,8,8,512]{3,2,1,0:T(8,128)(2,1)} %get-tuple-element.33), channel_id=1, source_target_pairs={{0,4},{4,0},{1,5},{5,1},{2,6},{6,2},{3,7},{7,3},{8,12},{12,8},{9,1... | collective-permute-start | bytes 3145736 | tf_op jit(solution)/shard_map/ppermute | solution.py:38
  57.6 20.9 %all-to-all-start.2 = ((bf16[16,8,8,512]{3,2,1,0:T(8,128)(2,1)}), bf16[16,8,8,512]{3,2,1,0:T(8,128)(2,1)S(1)}, u32[]{:S(2)}, u32[]{:S(2)}) async-start(bf16[16,8,8,512]{3,2,1,0:T(8,128)(2,1)} %shard_map.130), calls=%async_computation.2 | async-start | bytes 2097152 | tf_op jit(solution)/shard_map/all_to_all | solution.py:18
  62.5 46.1 %copy-start.1 = (f32[8,512]{1,0:T(8,128)S(1)}, f32[8,512]{1,0:T(8,128)}, u32[]{:S(2)}) copy-start(f32[8,512]{1,0:T(8,128)} %me_ref.5) | copy-start | bytes 49156
  62.5 46.1 %copy-start.2 = (f32[8,512]{1,0:T(8,128)S(1)}, f32[8,512]{1,0:T(8,128)}, u32[]{:S(2)}) copy-start(f32[8,512]{1,0:T(8,128)} %mr_ref.5) | copy-start | bytes 49156
  62.5 46.1 %copy-start.3 = (f32[8,512]{1,0:T(8,128)S(1)}, f32[8,512]{1,0:T(8,128)}, u32[]{:S(2)}) copy-start(f32[8,512]{1,0:T(8,128)} %ve_ref.3) | copy-start | bytes 49156
  62.5 46.1 %copy-start.4 = (f32[8,512]{1,0:T(8,128)S(1)}, f32[8,512]{1,0:T(8,128)}, u32[]{:S(2)}) copy-start(f32[8,512]{1,0:T(8,128)} %vr_ref.3) | copy-start | bytes 49156
  78.5 19.6 %all-to-all-start.3 = ((bf16[16,8,8,512]{3,2,1,0:T(8,128)(2,1)}), bf16[16,8,8,512]{3,2,1,0:T(8,128)(2,1)S(1)}, u32[]{:S(2)}, u32[]{:S(2)}) async-start(bf16[16,8,8,512]{3,2,1,0:T(8,128)(2,1)} %shard_map.131), calls=%async_computation.3 | async-start | bytes 2097152 | tf_op jit(solution)/shard_map/all_to_all | solution.py:18
  121.9 6.4 %collective-permute-start.10 = (bf16[4,4,8,512]{3,2,1,0:T(8,128)(2,1)S(1)}, bf16[4,4,8,512]{3,2,1,0:T(8,128)(2,1)S(1)}, u32[]{:S(2)}, u32[]{:S(2)}) collective-permute-start(bf16[4,4,8,512]{3,2,1,0:T(8,128)(2,1)S(1)} %get-tuple-element.37.refs_0_), channel_id=1, source_target_pairs={{0,1},{1,2},{2,3},{3,0},{4,5},{5,6},{6,7},{7,4},{8,9},{9,10},{10,1... | collective-permute-start | bytes 393224 | tf_op jit(solution)/shard_map/ppermute | solution.py:29
  122.1 18.0 %collective-permute-start.11 = (bf16[4,4,8,512]{3,2,1,0:T(8,128)(2,1)S(1)}, bf16[4,4,8,512]{3,2,1,0:T(8,128)(2,1)S(1)}, u32[]{:S(2)}, u32[]{:S(2)}) collective-permute-start(bf16[4,4,8,512]{3,2,1,0:T(8,128)(2,1)S(1)} %get-tuple-element.37.refs_0_), channel_id=1, source_target_pairs={{0,2},{1,3},{2,0},{3,1},{4,6},{5,7},{6,4},{7,5},{8,10},{9,11},{10,... | collective-permute-start | bytes 393224 | tf_op jit(solution)/shard_map/ppermute | solution.py:29
  124.2 17.4 %collective-permute-start.12 = (bf16[4,4,8,512]{3,2,1,0:T(8,128)(2,1)S(1)}, bf16[4,4,8,512]{3,2,1,0:T(8,128)(2,1)S(1)}, u32[]{:S(2)}, u32[]{:S(2)}) collective-permute-start(bf16[4,4,8,512]{3,2,1,0:T(8,128)(2,1)S(1)} %get-tuple-element.37.refs_0_), channel_id=1, source_target_pairs={{0,3},{1,0},{2,1},{3,2},{4,7},{5,4},{6,5},{7,6},{8,11},{9,8},{10,9... | collective-permute-start | bytes 393224 | tf_op jit(solution)/shard_map/ppermute | solution.py:29
  125.9 18.1 %collective-permute-start.13 = (bf16[4,4,8,512]{3,2,1,0:T(8,128)(2,1)S(1)}, bf16[4,4,8,512]{3,2,1,0:T(8,128)(2,1)S(1)}, u32[]{:S(2)}, u32[]{:S(2)}) collective-permute-start(bf16[4,4,8,512]{3,2,1,0:T(8,128)(2,1)S(1)} %get-tuple-element.38.refs_4_), channel_id=1, source_target_pairs={{0,8},{8,16},{16,24},{24,0},{1,9},{9,17},{17,25},{25,1},{2,10},{10... | collective-permute-start | bytes 393224 | tf_op jit(solution)/shard_map/ppermute | solution.py:29
  126.2 21.9 %collective-permute-start.14 = (bf16[4,4,8,512]{3,2,1,0:T(8,128)(2,1)S(1)}, bf16[4,4,8,512]{3,2,1,0:T(8,128)(2,1)S(1)}, u32[]{:S(2)}, u32[]{:S(2)}) collective-permute-start(bf16[4,4,8,512]{3,2,1,0:T(8,128)(2,1)S(1)} %get-tuple-element.38.refs_4_), channel_id=1, source_target_pairs={{0,16},{8,24},{16,0},{24,8},{1,17},{9,25},{17,1},{25,9},{2,18},{10... | collective-permute-start | bytes 393224 | tf_op jit(solution)/shard_map/ppermute | solution.py:29
  128.3 19.9 %collective-permute-start.15 = (bf16[4,4,8,512]{3,2,1,0:T(8,128)(2,1)S(1)}, bf16[4,4,8,512]{3,2,1,0:T(8,128)(2,1)S(1)}, u32[]{:S(2)}, u32[]{:S(2)}) collective-permute-start(bf16[4,4,8,512]{3,2,1,0:T(8,128)(2,1)S(1)} %get-tuple-element.38.refs_4_), channel_id=1, source_target_pairs={{0,24},{8,0},{16,8},{24,16},{1,25},{9,1},{17,9},{25,17},{2,26},{10... | collective-permute-start | bytes 393224 | tf_op jit(solution)/shard_map/ppermute | solution.py:29
  129.2 19.0 %all-to-all-start.6 = ((f32[32,8,128]{2,1,0:T(8,128)}), f32[32,8,128]{2,1,0:T(8,128)S(1)}, u32[]{:S(2)}, u32[]{:S(2)}) async-start(f32[32,8,128]{2,1,0:T(8,128)} %get-tuple-element.35), calls=%async_computation.6 | async-start | bytes 262144 | tf_op jit(solution)/shard_map/all_to_all | solution.py:18
  140.2 13.4 %collective-permute-start.1 = (bf16[8,8,512]{2,1,0:T(8,128)(2,1)S(1)}, bf16[8,8,512]{2,1,0:T(8,128)(2,1)S(1)}, u32[]{:S(2)}, u32[]{:S(2)}) collective-permute-start(bf16[8,8,512]{2,1,0:T(8,128)(2,1)S(1)} %get-tuple-element.51), channel_id=1, source_target_pairs={{0,1},{1,2},{2,3},{3,0},{4,5},{5,6},{6,7},{7,4},{8,9},{9,10},{10,1... | collective-permute-start | bytes 196616 | tf_op jit(solution)/shard_map/ppermute | solution.py:29
  141.6 12.0 %collective-permute-start.2 = (bf16[8,8,512]{2,1,0:T(8,128)(2,1)S(1)}, bf16[8,8,512]{2,1,0:T(8,128)(2,1)S(1)}, u32[]{:S(2)}, u32[]{:S(2)}) collective-permute-start(bf16[8,8,512]{2,1,0:T(8,128)(2,1)S(1)} %get-tuple-element.51), channel_id=1, source_target_pairs={{0,2},{1,3},{2,0},{3,1},{4,6},{5,7},{6,4},{7,5},{8,10},{9,11},{10,... | collective-permute-start | bytes 196616 | tf_op jit(solution)/shard_map/ppermute | solution.py:29
  144.0 9.6 %collective-permute-start.3 = (bf16[8,8,512]{2,1,0:T(8,128)(2,1)S(1)}, bf16[8,8,512]{2,1,0:T(8,128)(2,1)S(1)}, u32[]{:S(2)}, u32[]{:S(2)}) collective-permute-start(bf16[8,8,512]{2,1,0:T(8,128)(2,1)S(1)} %get-tuple-element.51), channel_id=1, source_target_pairs={{0,3},{1,0},{2,1},{3,2},{4,7},{5,4},{6,5},{7,6},{8,11},{9,8},{10,9... | collective-permute-start | bytes 196616 | tf_op jit(solution)/shard_map/ppermute | solution.py:29
  150.1 33.5 %all-to-all-start.7 = ((bf16[4,4,4,2,8,512]{5,4,3,2,1,0:T(8,128)(2,1)}), bf16[4,4,4,2,8,512]{5,4,3,2,1,0:T(8,128)(2,1)S(1)}, u32[]{:S(2)}, u32[]{:S(2)}) async-start(bf16[4,4,4,2,8,512]{5,4,3,2,1,0:T(8,128)(2,1)} %broadcast_in_dim.15), calls=%async_computation.7 | async-start | bytes 2097152 | tf_op jit(solution)/shard_map/all_to_all | solution.py:18
  153.7 20.1 %collective-permute-start.4 = (bf16[32,8,512]{2,1,0:T(8,128)(2,1)S(1)}, bf16[32,8,512]{2,1,0:T(8,128)(2,1)S(1)}, u32[]{:S(2)}, u32[]{:S(2)}) collective-permute-start(bf16[32,8,512]{2,1,0:T(8,128)(2,1)S(1)} %pad_maximum_fusion.2), channel_id=1, source_target_pairs={{0,8},{8,16},{16,24},{24,0},{1,9},{9,17},{17,25},{25,1},{2,10},{10... | collective-permute-start | bytes 786440 | tf_op jit(solution)/shard_map/ppermute | solution.py:29
  155.2 24.6 %collective-permute-start.5 = (bf16[32,8,512]{2,1,0:T(8,128)(2,1)S(1)}, bf16[32,8,512]{2,1,0:T(8,128)(2,1)S(1)}, u32[]{:S(2)}, u32[]{:S(2)}) collective-permute-start(bf16[32,8,512]{2,1,0:T(8,128)(2,1)S(1)} %pad_maximum_fusion.2), channel_id=1, source_target_pairs={{0,16},{8,24},{16,0},{24,8},{1,17},{9,25},{17,1},{25,9},{2,18},{10... | collective-permute-start | bytes 786440 | tf_op jit(solution)/shard_map/ppermute | solution.py:29
  157.6 22.2 %collective-permute-start.6 = (bf16[32,8,512]{2,1,0:T(8,128)(2,1)S(1)}, bf16[32,8,512]{2,1,0:T(8,128)(2,1)S(1)}, u32[]{:S(2)}, u32[]{:S(2)}) collective-permute-start(bf16[32,8,512]{2,1,0:T(8,128)(2,1)S(1)} %pad_maximum_fusion.2), channel_id=1, source_target_pairs={{0,24},{8,0},{16,8},{24,16},{1,25},{9,1},{17,9},{25,17},{2,26},{10... | collective-permute-start | bytes 786440 | tf_op jit(solution)/shard_map/ppermute | solution.py:29
  158.7 22.4 %collective-permute-start.17 = (bf16[4,4,2,8,512]{4,3,2,1,0:T(8,128)(2,1)S(1)}, bf16[4,4,2,8,512]{4,3,2,1,0:T(8,128)(2,1)S(1)}, u32[]{:S(2)}, u32[]{:S(2)}) collective-permute-start(bf16[4,4,2,8,512]{4,3,2,1,0:T(8,128)(2,1)S(1)} %get-tuple-element.44), channel_id=1, source_target_pairs={{0,1},{1,2},{2,3},{3,0},{4,5},{5,6},{6,7},{7,4},{8,9},{9,10},{10,1... | collective-permute-start | bytes 786440 | tf_op jit(solution)/shard_map/ppermute | solution.py:29
  158.7 22.4 %collective-permute-start.18 = (bf16[4,4,2,8,512]{4,3,2,1,0:T(8,128)(2,1)S(1)}, bf16[4,4,2,8,512]{4,3,2,1,0:T(8,128)(2,1)S(1)}, u32[]{:S(2)}, u32[]{:S(2)}) collective-permute-start(bf16[4,4,2,8,512]{4,3,2,1,0:T(8,128)(2,1)S(1)} %get-tuple-element.44), channel_id=1, source_target_pairs={{0,2},{1,3},{2,0},{3,1},{4,6},{5,7},{6,4},{7,5},{8,10},{9,11},{10,... | collective-permute-start | bytes 786440 | tf_op jit(solution)/shard_map/ppermute | solution.py:29
  173.8 7.4 %collective-permute-start.19 = (bf16[4,4,2,8,512]{4,3,2,1,0:T(8,128)(2,1)S(1)}, bf16[4,4,2,8,512]{4,3,2,1,0:T(8,128)(2,1)S(1)}, u32[]{:S(2)}, u32[]{:S(2)}) collective-permute-start(bf16[4,4,2,8,512]{4,3,2,1,0:T(8,128)(2,1)S(1)} %get-tuple-element.44), channel_id=1, source_target_pairs={{0,3},{1,0},{2,1},{3,2},{4,7},{5,4},{6,5},{7,6},{8,11},{9,8},{10,9... | collective-permute-start | bytes 786440 | tf_op jit(solution)/shard_map/ppermute | solution.py:29
  179.9 3.8 %copy-start.8 = (bf16[128,8,512]{2,1,0:T(8,128)(2,1)}, bf16[128,8,512]{2,1,0:T(8,128)(2,1)S(1)}, u32[]{:S(2)}) copy-start(bf16[128,8,512]{2,1,0:T(8,128)(2,1)S(1)} %pad_maximum_fusion) | copy-start | bytes 3145732
  179.9 3.7 %collective-permute-start.7 = (bf16[16,8,8,512]{3,2,1,0:T(8,128)(2,1)S(1)}, bf16[16,8,8,512]{3,2,1,0:T(8,128)(2,1)}, u32[]{:S(2)}, u32[]{:S(2)}) collective-permute-start(bf16[16,8,8,512]{3,2,1,0:T(8,128)(2,1)S(1)} %bitcast.17), channel_id=1, source_target_pairs={{0,4},{4,0},{1,5},{5,1},{2,6},{6,2},{3,7},{7,3},{8,12},{12,8},{9,1... | collective-permute-start | bytes 3145736 | tf_op jit(solution)/shard_map/ppermute | solution.py:38
  182.3 10.0 %collective-permute-start.20 = (bf16[4,4,4,2,8,512]{5,4,3,2,1,0:T(8,128)(2,1)}, bf16[4,4,4,2,8,512]{5,4,3,2,1,0:T(8,128)(2,1)}, u32[]{:S(2)}, u32[]{:S(2)}) collective-permute-start(bf16[4,4,4,2,8,512]{5,4,3,2,1,0:T(8,128)(2,1)} %pad_maximum_fusion.1.refs_1_), channel_id=1, source_target_pairs={{0,4},{4,0},{1,5},{5,1},{2,6},{6,2},{3,7},{7,3},{8,12},{12,8},{9,1... | collective-permute-start | bytes 3145736 | tf_op jit(solution)/shard_map/ppermute | solution.py:38
  183.6 11.4 %collective-permute-start.16 = (bf16[4,4,4,2,8,512]{5,4,3,2,1,0:T(8,128)(2,1)S(1)}, bf16[4,4,4,2,8,512]{5,4,3,2,1,0:T(8,128)(2,1)}, u32[]{:S(2)}, u32[]{:S(2)}) collective-permute-start(bf16[4,4,4,2,8,512]{5,4,3,2,1,0:T(8,128)(2,1)S(1)} %all-to-all-done.7.refs_0_), channel_id=1, source_target_pairs={{0,4},{4,0},{1,5},{5,1},{2,6},{6,2},{3,7},{7,3},{8,12},{12,8},{9,1... | collective-permute-start | bytes 3145736 | tf_op jit(solution)/shard_map/ppermute | solution.py:38
  183.6 5.5 %copy-start.6 = (s32[3]{0:T(128)S(1)}, s32[3]{0:T(128)}, u32[]{:S(2)}) copy-start(s32[3]{0:T(128)} %copy-done.5) | copy-start | bytes 40

commit v9 on v8

--- a/solution.py
+++ b/solution.py
@@ -345,7 +345,7 @@
         (jax.ShapeDtypeStruct(grad_out.shape, BF),),
         [whole],
         flops,
-        limit=62,
+        limit=56,
     )
 
     state = (master_expand, master_reduce, velocity_expand, velocity_reduce)
@@ -379,8 +379,7 @@
     low_other = from_other_core(low_mine)
     high_other = from_other_core(high_mine)
     placed = place(False, (0, 1), (low_mine, high_mine), ())
-    placed = place(True, (1,), (high_other,), placed)
-    placed = place(True, (0,), (low_other,), placed)
+    placed = place(True, (0, 1), (low_other, high_other), placed)
     work_expand, work_reduce = (p.reshape(channels, middle) for p in placed)
     return (grad_in, new_mr, new_me, new_vr, new_ve, work_reduce, work_expand)
 

time: 200 us -> 196 us (0.980)
  Pallas kernels: 30.8 us -> 26.1 us
    pallas_call x3 -> x2, Pallas kernels: 8.61 us -> 4.8 us  [place(): pl.pallas_call(functools.partial(place_kernel, other, halves), out_shape=...]
  transfers between devices with their start and end apart: 25 -> 25, of which waited for: 6 -> 7; matrix products, arithmetic and copies ran while one was open for 1% -> 2% of each run, Pallas kernels for 13% -> 11%
where the time goes in v9:
time: 196 us; the launch traced here: 195 us
  blocking collectives  61.1 us (31%)
  waiting for transfers between devices  53.8 us (27%)
  starting transfers between devices  48.2 us (25%)
  Pallas kernels  26.1 us (13%)
  other arithmetic  2.73 us (1%)
  local copies, waits for them, and re-layouts  2.08 us (1%)
    all_to_all x4, blocking collectives, exchange(): return lax.all_to_all(parts, axes, 0, 0, tiled=True)  61.1 us
    all_to_all x4, waiting for transfers between devices, exchange(): return lax.all_to_all(parts, axes, 0, 0, tiled=True)  33.3 us
    all_to_all x4, starting transfers between devices, exchange(): return lax.all_to_all(parts, axes, 0, 0, tiled=True)  22.7 us
    ppermute x15, starting transfers between devices, shifts(): lax.ppermute(block, axis, [(i, (i + s) % 4) for i in range(4)])  19.8 us
    ppermute x15, waiting for transfers between devices, shifts(): lax.ppermute(block, axis, [(i, (i + s) % 4) for i in range(4)])  18.6 us
    pallas_call x3, Pallas kernels, local_call(): pl.pallas_call(kernel, out_shape=outs, in_specs=[pl.BlockSpec(memory_spac...  15.6 us
    ppermute x6, starting transfers between devices, from_other_core(): return lax.ppermute(block, 'c', [(0, 1), (1, 0)])  5.71 us
    pallas_call x7, Pallas kernels, small_call(): pl.pallas_call(kernel, out_shape=outs, in_specs=[whole] * len(operands),...  5.64 us
  transfers between devices with their start and end apart: 25, of which 7 were waited for; matrix products, arithmetic and copies ran while one was open for 2% of the time, Pallas kernels for 11%

profile of v9, /device:TPU:1, one launch (start us, length us, event | category | flops | bytes accessed | tf_op | source)
XLA Modules:
  0.0 194.9 jit_solution(9746479695041108537)
XLA Ops:
  0.6 1.5 shard_map.126
  2.1 16.8 %all_to_all.40 = bf16[8,2,8,512]{3,2,1,0:T(8,128)(2,1)S(1)} all-to-all(bf16[8,2,8,512]{3,2,1,0:T(8,128)(2,1)} %shard_map.126), channel_id=1, replica_groups=mesh['z'=8,'y'=4,'c'=2,'x'=4] {'z'}, dimensions={0} | all-to-all | bytes 262144 | tf_op jit(solution)/shard_map/all_to_all | solution.py:18
  18.9 0.1 broadcast_in_dim.14
  19.0 21.5 %all_to_all.41.mine_ref = bf16[16,8,8,512]{3,2,1,0:T(8,128)(2,1)S(1)} all-to-all(bf16[16,8,8,512]{3,2,1,0:T(8,128)(2,1)S(1)} %broadcast_in_dim.14), channel_id=1, replica_groups=mesh['z'=8,'y'=4,'c'=2,'x'=4] {'y','x'}, dimensions={0} | all-to-all | bytes 2097152 | tf_op jit(solution)/shard_map/all_to_all | solution.py:18
  40.5 3.3 %collective-permute-start = (bf16[16,8,8,512]{3,2,1,0:T(8,128)(2,1)S(1)}, bf16[16,8,8,512]{3,2,1,0:T(8,128)(2,1)}, u32[]{:S(2)}, u32[]{:S(2)}) collective-permute-start(bf16[16,8,8,512]{3,2,1,0:T(8,128)(2,1)S(1)} %all_to_all.41.mine_ref), channel_id=1, source_target_pairs={{0,4},{4,0},{1,5},{5,1},{2,6},{6,2},{3,7},{7,3},{8,12},{12,8},{9,1... | collective-permute-start | bytes 3145736 | tf_op jit(solution)/shard_map/ppermute | solution.py:38
  43.8 0.1 pad_add_fusion.place_ref.at_ref
  43.8 3.5 %shard_map.129 = (bf16[16,8,8,512]{3,2,1,0:T(8,128)(2,1)S(1)}, bf16[16,8,8,512]{3,2,1,0:T(8,128)(2,1)S(1)}) custom-call(s32[3]{0:T(128)S(1)} %pad_add_fusion.place_ref.at_ref, bf16[588,2048]{1,0:T(8,128)(2,1)} %grad_ref.3, bf16[588,512]{1,0:T(8,128)(2,1)S(1)} %copy-done.7), custom_call_target="tpu_custom_call" | custom-call | flops 1233125376 | bytes 5107712 | tf_op jit(solution)/shard_map/pallas_call | solution.py:145
  47.4 0.4 collective-permute-start.8
  47.8 0.0 collective-permute-done.other_ref
  47.8 6.6 %shard_map.127 = (bf16[588,512]{1,0:T(8,128)(2,1)S(1)}, bf16[16,8,8,512]{3,2,1,0:T(8,128)(2,1)S(1)}, bf16[16,8,8,512]{3,2,1,0:T(8,128)(2,1)S(1)}) custom-call(s32[3]{0:T(128)S(1)} %pad_add_fusion.place_ref.at_ref, bf16[588,512]{1,0:T(8,128)(2,1)S(1)} %copy-done.7, bf16[16,8,8,512]{3,2,1,0:T(8,128)(2,1)} %copy-done.8, ...), custom_call_target="tpu_custom_call" | custom-call | flops 2466250752 | bytes 10215424 | tf_op jit(solution)/shard_map/pallas_call | solution.py:145
  54.4 0.8 copy-done
  55.2 0.2 collective-permute-start.9
  55.4 1.2 shard_map.130
  56.6 4.3 %all-to-all-start.2 = ((bf16[16,8,8,512]{3,2,1,0:T(8,128)(2,1)}), bf16[16,8,8,512]{3,2,1,0:T(8,128)(2,1)}, u32[]{:S(2)}, u32[]{:S(2)}) async-start(bf16[16,8,8,512]{3,2,1,0:T(8,128)(2,1)} %shard_map.130), calls=%async_computation.2 | async-start | bytes 2097152 | tf_op jit(solution)/shard_map/all_to_all | solution.py:18
  61.0 0.0 collective-permute-done.9.got_ref
  61.0 1.2 shard_map.131
  62.2 16.1 %all-to-all-done.2 = bf16[16,8,8,512]{3,2,1,0:T(8,128)(2,1)} async-done(((bf16[16,8,8,512]{3,2,1,0:T(8,128)(2,1)}), bf16[16,8,8,512]{3,2,1,0:T(8,128)(2,1)}, u32[]{:S(2)}, u32[]{:S(2)}) %all-to-all-start.2) | async-done | bytes 1048608 | tf_op jit(solution)/shard_map/all_to_all | solution.py:18
  78.3 3.9 %all-to-all-start.3 = ((bf16[16,8,8,512]{3,2,1,0:T(8,128)(2,1)}), bf16[16,8,8,512]{3,2,1,0:T(8,128)(2,1)S(1)}, u32[]{:S(2)}, u32[]{:S(2)}) async-start(bf16[16,8,8,512]{3,2,1,0:T(8,128)(2,1)} %shard_map.131), calls=%async_computation.3 | async-start | bytes 2097152 | tf_op jit(solution)/shard_map/all_to_all | solution.py:18
  82.2 1.4 reduce_sum.12.expand_ref
  83.5 14.3 %all-to-all-done.3.reduce_ref = bf16[16,8,8,512]{3,2,1,0:T(8,128)(2,1)S(1)} async-done(((bf16[16,8,8,512]{3,2,1,0:T(8,128)(2,1)}), bf16[16,8,8,512]{3,2,1,0:T(8,128)(2,1)S(1)}, u32[]{:S(2)}, u32[]{:S(2)}) %all-to-all-start.3) | async-done | bytes 1048608 | tf_op jit(solution)/shard_map/all_to_all | solution.py:18
  97.9 0.1 shard_map.132
  98.0 10.3 %all_to_all.42.arrived_ref = bf16[8,2,8,512]{3,2,1,0:T(8,128)(2,1)S(1)} all-to-all(bf16[8,2,8,512]{3,2,1,0:T(8,128)(2,1)S(1)} %shard_map.132), channel_id=1, replica_groups=mesh['z'=8,'y'=4,'c'=2,'x'=4] {'z'}, dimensions={0} | all-to-all | bytes 262144 | tf_op jit(solution)/shard_map/all_to_all | solution.py:18
  108.3 0.1 shard_map.133
  108.4 12.5 %all_to_all.43.ring_ref = bf16[8,5,8,512]{3,2,1,0:T(8,128)(2,1)S(1)} all-to-all(bf16[8,5,8,512]{3,2,1,0:T(8,128)(2,1)S(1)} %get-tuple-element.32), channel_id=1, replica_groups=mesh['z'=8,'y'=4,'c'=2,'x'=4] {'z'}, dimensions={0} | all-to-all | bytes 655360 | tf_op jit(solution)/shard_map/all_to_all | solution.py:18
  121.0 0.7 shard_map.134
  121.6 0.3 collective-permute-start.10
  121.9 2.1 %collective-permute-start.11 = (bf16[4,4,8,512]{3,2,1,0:T(8,128)(2,1)S(1)}, bf16[4,4,8,512]{3,2,1,0:T(8,128)(2,1)S(1)}, u32[]{:S(2)}, u32[]{:S(2)}) collective-permute-start(bf16[4,4,8,512]{3,2,1,0:T(8,128)(2,1)S(1)} %get-tuple-element.35.refs_0_), channel_id=1, source_target_pairs={{0,2},{1,3},{2,0},{3,1},{4,6},{5,7},{6,4},{7,5},{8,10},{9,11},{10,... | collective-permute-start | bytes 393224 | tf_op jit(solution)/shard_map/ppermute | solution.py:29
  124.0 1.7 collective-permute-start.12
  125.7 0.3 collective-permute-start.13
  126.0 1.8 collective-permute-start.14
  127.8 0.2 collective-permute-done.10.refs_1_
  128.1 0.9 collective-permute-start.15
  129.0 11.0 %all-to-all-start.6 = ((f32[32,8,128]{2,1,0:T(8,128)}), f32[32,8,128]{2,1,0:T(8,128)S(1)}, u32[]{:S(2)}, u32[]{:S(2)}) async-start(f32[32,8,128]{2,1,0:T(8,128)} %get-tuple-element.33), calls=%async_computation.6 | async-start | bytes 262144 | tf_op jit(solution)/shard_map/all_to_all | solution.py:18
  139.9 0.0 collective-permute-done.11.refs_2_
  140.0 1.4 collective-permute-start.1
  141.4 0.0 collective-permute-done.12.refs_3_
  141.4 2.4 %collective-permute-start.2 = (bf16[8,8,512]{2,1,0:T(8,128)(2,1)S(1)}, bf16[8,8,512]{2,1,0:T(8,128)(2,1)S(1)}, u32[]{:S(2)}, u32[]{:S(2)}) collective-permute-start(bf16[8,8,512]{2,1,0:T(8,128)(2,1)S(1)} %get-tuple-element.47), channel_id=1, source_target_pairs={{0,2},{1,3},{2,0},{3,1},{4,6},{5,7},{6,4},{7,5},{8,10},{9,11},{10,... | collective-permute-start | bytes 196616 | tf_op jit(solution)/shard_map/ppermute | solution.py:29
  143.8 0.0 collective-permute-done.13.refs_5_
  143.8 1.2 collective-permute-start.3
  145.0 3.0 %all-to-all-done.6.squares_ref = f32[32,8,128]{2,1,0:T(8,128)S(1)} async-done(((f32[32,8,128]{2,1,0:T(8,128)}), f32[32,8,128]{2,1,0:T(8,128)S(1)}, u32[]{:S(2)}, u32[]{:S(2)}) %all-to-all-start.6) | async-done | bytes 131104 | tf_op jit(solution)/shard_map/all_to_all | solution.py:18
  147.9 0.8 shard_map.135
  148.8 1.1 broadcast_in_dim.15
  149.9 3.5 %all-to-all-start.7 = ((bf16[4,4,4,2,8,512]{5,4,3,2,1,0:T(8,128)(2,1)}), bf16[4,4,4,2,8,512]{5,4,3,2,1,0:T(8,128)(2,1)S(1)}, u32[]{:S(2)}, u32[]{:S(2)}) async-start(bf16[4,4,4,2,8,512]{5,4,3,2,1,0:T(8,128)(2,1)} %broadcast_in_dim.15), calls=%async_computation.7 | async-start | bytes 2097152 | tf_op jit(solution)/shard_map/all_to_all | solution.py:18
  153.4 0.0 collective-permute-done.2
  153.4 0.0 collective-permute-done.3
  153.5 1.5 collective-permute-start.4
  154.9 2.4 %collective-permute-start.5 = (bf16[32,8,512]{2,1,0:T(8,128)(2,1)S(1)}, bf16[32,8,512]{2,1,0:T(8,128)(2,1)S(1)}, u32[]{:S(2)}, u32[]{:S(2)}) collective-permute-start(bf16[32,8,512]{2,1,0:T(8,128)(2,1)S(1)} %pad_maximum_fusion.2), channel_id=1, source_target_pairs={{0,16},{8,24},{16,0},{24,8},{1,17},{9,25},{17,1},{25,9},{2,18},{10... | collective-permute-start | bytes 786440 | tf_op jit(solution)/shard_map/ppermute | solution.py:29
  157.3 1.2 collective-permute-start.6
  158.5 0.0 collective-permute-start.17
  158.5 2.0 %collective-permute-start.18 = (bf16[4,4,2,8,512]{4,3,2,1,0:T(8,128)(2,1)S(1)}, bf16[4,4,2,8,512]{4,3,2,1,0:T(8,128)(2,1)S(1)}, u32[]{:S(2)}, u32[]{:S(2)}) collective-permute-start(bf16[4,4,2,8,512]{4,3,2,1,0:T(8,128)(2,1)S(1)} %get-tuple-element.42), channel_id=1, source_target_pairs={{0,2},{1,3},{2,0},{3,1},{4,6},{5,7},{6,4},{7,5},{8,10},{9,11},{10,... | collective-permute-start | bytes 786440 | tf_op jit(solution)/shard_map/ppermute | solution.py:29
  160.5 13.1 %collective-permute-done.4 = bf16[32,8,512]{2,1,0:T(8,128)(2,1)S(1)} collective-permute-done((bf16[32,8,512]{2,1,0:T(8,128)(2,1)S(1)}, bf16[32,8,512]{2,1,0:T(8,128)(2,1)S(1)}, u32[]{:S(2)}, u32[]{:S(2)}) %collective-permute-start.4) | collective-permute-done | bytes 262176 | tf_op jit(solution)/shard_map/ppermute | solution.py:29
  173.6 0.7 collective-permute-start.19
  174.2 5.3 %collective-permute-done.5 = bf16[32,8,512]{2,1,0:T(8,128)(2,1)S(1)} collective-permute-done((bf16[32,8,512]{2,1,0:T(8,128)(2,1)S(1)}, bf16[32,8,512]{2,1,0:T(8,128)(2,1)S(1)}, u32[]{:S(2)}, u32[]{:S(2)}) %collective-permute-start.5) | collective-permute-done | bytes 262176 | tf_op jit(solution)/shard_map/ppermute | solution.py:29
  179.5 1.1 pad_maximum_fusion
  180.6 1.2 collective-permute-start.7
  181.8 0.0 collective-permute-done.17
  181.8 0.0 collective-permute-done.18
  181.8 0.1 pad_maximum_fusion.1.refs_1_
  181.9 0.6 collective-permute-start.20
  182.5 0.1 collective-permute-start.16
  182.6 1.8 collective-permute-done.7.other_ref
  184.4 5.5 %shard_map.128 = bf16[588,2048]{1,0:T(8,128)(2,1)} custom-call(s32[3]{0:T(128)} %copy-done.5, bf16[588,2048]{1,0:T(8,128)(2,1)} %grad_ref.3, bf16[588,512]{1,0:T(8,128)(2,1)} %copy-done, bf16[16,8,8,512]{3,2,1,0:T(8,128)(2,1)} %bitcast.5.mine_ref, bf16[16,8,8,512]{3,2,1,0:T(8,128)(2,1)} %collective-permute-done.7.other_ref), custom_call_target="tpu_custom_call" | custom-call | flops 1233125376 | bytes 7516160 | tf_op jit(solution)/shard_map/pallas_call | solution.py:145
  189.9 2.4 %shard_map.136 = (bf16[8,4,2,4,8,512]{5,4,3,2,1,0:T(8,128)(2,1)}, bf16[8,4,2,4,8,512]{5,4,3,2,1,0:T(8,128)(2,1)}) custom-call(s32[3]{0:T(128)S(1)} %copy-done.6, bf16[4,4,4,2,8,512]{5,4,3,2,1,0:T(8,128)(2,1)S(1)} %all-to-all-done.7.refs_0_, bf16[4,4,4,2,8,512]{5,4,3,2,1,0:T(8,128)(2,1)S(1)} %pad_maximum_fusion.1.refs_1_), custom_call_target="tpu_custom_call" | custom-call | flops 524288 | bytes 4194304 | tf_op jit(solution)/shard_map/pallas_call | solution.py:281
  192.4 2.4 %shard_map.137 = (bf16[8,4,2,4,8,512]{5,4,3,2,1,0:T(8,128)(2,1)}, bf16[8,4,2,4,8,512]{5,4,3,2,1,0:T(8,128)(2,1)}) custom-call(s32[3]{0:T(128)S(1)} %copy-done.6, bf16[4,4,4,2,8,512]{5,4,3,2,1,0:T(8,128)(2,1)S(1)} %collective-permute-done.16.refs_0_, ...), custom_call_target="tpu_custom_call", output_to_operand_aliasing={{0}: (3, {}), {1}: (4, {})} | custom-call | flops 524288 | bytes 4194304 | tf_op jit(solution)/shard_map/pallas_call | solution.py:281
  (28 shorter events, 0.1 us)
Async XLA Ops:
  0.6 43.2 %copy-start.7 = (bf16[588,512]{1,0:T(8,128)(2,1)S(1)}, bf16[588,512]{1,0:T(8,128)(2,1)}, u32[]{:S(2)}) copy-start(bf16[588,512]{1,0:T(8,128)(2,1)} %hidden_ref.1) | copy-start | bytes 1806340
  40.5 6.9 %copy-start.8 = (bf16[16,8,8,512]{3,2,1,0:T(8,128)(2,1)}, bf16[16,8,8,512]{3,2,1,0:T(8,128)(2,1)S(1)}, u32[]{:S(2)}) copy-start(bf16[16,8,8,512]{3,2,1,0:T(8,128)(2,1)S(1)} %all_to_all.41.mine_ref) | copy-start | bytes 3145732
  40.5 7.3 %collective-permute-start = (bf16[16,8,8,512]{3,2,1,0:T(8,128)(2,1)S(1)}, bf16[16,8,8,512]{3,2,1,0:T(8,128)(2,1)}, u32[]{:S(2)}, u32[]{:S(2)}) collective-permute-start(bf16[16,8,8,512]{3,2,1,0:T(8,128)(2,1)S(1)} %all_to_all.41.mine_ref), channel_id=1, source_target_pairs={{0,4},{4,0},{1,5},{5,1},{2,6},{6,2},{3,7},{7,3},{8,12},{12,8},{9,1... | collective-permute-start | bytes 3145736 | tf_op jit(solution)/shard_map/ppermute | solution.py:38
  43.8 3.9 %copy-start.5 = (s32[3]{0:T(128)}, s32[3]{0:T(128)S(1)}, u32[]{:S(2)}) copy-start(s32[3]{0:T(128)S(1)} %pad_add_fusion.place_ref.at_ref) | copy-start | bytes 40
  47.4 8.0 %collective-permute-start.8 = (bf16[16,8,8,512]{3,2,1,0:T(8,128)(2,1)S(1)}, bf16[16,8,8,512]{3,2,1,0:T(8,128)(2,1)S(1)}, u32[]{:S(2)}, u32[]{:S(2)}) collective-permute-start(bf16[16,8,8,512]{3,2,1,0:T(8,128)(2,1)S(1)} %get-tuple-element.29), channel_id=1, source_target_pairs={{0,4},{4,0},{1,5},{5,1},{2,6},{6,2},{3,7},{7,3},{8,12},{12,8},{9,1... | collective-permute-start | bytes 3145736 | tf_op jit(solution)/shard_map/ppermute | solution.py:38
  54.4 0.8 copy-start
  55.2 5.8 %collective-permute-start.9 = (bf16[16,8,8,512]{3,2,1,0:T(8,128)(2,1)S(1)}, bf16[16,8,8,512]{3,2,1,0:T(8,128)(2,1)S(1)}, u32[]{:S(2)}, u32[]{:S(2)}) collective-permute-start(bf16[16,8,8,512]{3,2,1,0:T(8,128)(2,1)S(1)} %get-tuple-element.31), channel_id=1, source_target_pairs={{0,4},{4,0},{1,5},{5,1},{2,6},{6,2},{3,7},{7,3},{8,12},{12,8},{9,1... | collective-permute-start | bytes 3145736 | tf_op jit(solution)/shard_map/ppermute | solution.py:38
  56.6 21.6 %all-to-all-start.2 = ((bf16[16,8,8,512]{3,2,1,0:T(8,128)(2,1)}), bf16[16,8,8,512]{3,2,1,0:T(8,128)(2,1)}, u32[]{:S(2)}, u32[]{:S(2)}) async-start(bf16[16,8,8,512]{3,2,1,0:T(8,128)(2,1)} %shard_map.130), calls=%async_computation.2 | async-start | bytes 2097152 | tf_op jit(solution)/shard_map/all_to_all | solution.py:18
  62.2 46.1 %copy-start.1 = (f32[8,512]{1,0:T(8,128)S(1)}, f32[8,512]{1,0:T(8,128)}, u32[]{:S(2)}) copy-start(f32[8,512]{1,0:T(8,128)} %me_ref.5) | copy-start | bytes 49156
  62.2 46.1 %copy-start.2 = (f32[8,512]{1,0:T(8,128)S(1)}, f32[8,512]{1,0:T(8,128)}, u32[]{:S(2)}) copy-start(f32[8,512]{1,0:T(8,128)} %mr_ref.5) | copy-start | bytes 49156
  62.2 46.1 %copy-start.3 = (f32[8,512]{1,0:T(8,128)S(1)}, f32[8,512]{1,0:T(8,128)}, u32[]{:S(2)}) copy-start(f32[8,512]{1,0:T(8,128)} %ve_ref.3) | copy-start | bytes 49156
  62.2 46.1 %copy-start.4 = (f32[8,512]{1,0:T(8,128)S(1)}, f32[8,512]{1,0:T(8,128)}, u32[]{:S(2)}) copy-start(f32[8,512]{1,0:T(8,128)} %vr_ref.3) | copy-start | bytes 49156
  78.3 19.6 %all-to-all-start.3 = ((bf16[16,8,8,512]{3,2,1,0:T(8,128)(2,1)}), bf16[16,8,8,512]{3,2,1,0:T(8,128)(2,1)S(1)}, u32[]{:S(2)}, u32[]{:S(2)}) async-start(bf16[16,8,8,512]{3,2,1,0:T(8,128)(2,1)} %shard_map.131), calls=%async_computation.3 | async-start | bytes 2097152 | tf_op jit(solution)/shard_map/all_to_all | solution.py:18
  121.6 6.4 %collective-permute-start.10 = (bf16[4,4,8,512]{3,2,1,0:T(8,128)(2,1)S(1)}, bf16[4,4,8,512]{3,2,1,0:T(8,128)(2,1)S(1)}, u32[]{:S(2)}, u32[]{:S(2)}) collective-permute-start(bf16[4,4,8,512]{3,2,1,0:T(8,128)(2,1)S(1)} %get-tuple-element.35.refs_0_), channel_id=1, source_target_pairs={{0,1},{1,2},{2,3},{3,0},{4,5},{5,6},{6,7},{7,4},{8,9},{9,10},{10,1... | collective-permute-start | bytes 393224 | tf_op jit(solution)/shard_map/ppermute | solution.py:29
  121.9 18.0 %collective-permute-start.11 = (bf16[4,4,8,512]{3,2,1,0:T(8,128)(2,1)S(1)}, bf16[4,4,8,512]{3,2,1,0:T(8,128)(2,1)S(1)}, u32[]{:S(2)}, u32[]{:S(2)}) collective-permute-start(bf16[4,4,8,512]{3,2,1,0:T(8,128)(2,1)S(1)} %get-tuple-element.35.refs_0_), channel_id=1, source_target_pairs={{0,2},{1,3},{2,0},{3,1},{4,6},{5,7},{6,4},{7,5},{8,10},{9,11},{10,... | collective-permute-start | bytes 393224 | tf_op jit(solution)/shard_map/ppermute | solution.py:29
  124.0 17.4 %collective-permute-start.12 = (bf16[4,4,8,512]{3,2,1,0:T(8,128)(2,1)S(1)}, bf16[4,4,8,512]{3,2,1,0:T(8,128)(2,1)S(1)}, u32[]{:S(2)}, u32[]{:S(2)}) collective-permute-start(bf16[4,4,8,512]{3,2,1,0:T(8,128)(2,1)S(1)} %get-tuple-element.35.refs_0_), channel_id=1, source_target_pairs={{0,3},{1,0},{2,1},{3,2},{4,7},{5,4},{6,5},{7,6},{8,11},{9,8},{10,9... | collective-permute-start | bytes 393224 | tf_op jit(solution)/shard_map/ppermute | solution.py:29
  125.7 18.1 %collective-permute-start.13 = (bf16[4,4,8,512]{3,2,1,0:T(8,128)(2,1)S(1)}, bf16[4,4,8,512]{3,2,1,0:T(8,128)(2,1)S(1)}, u32[]{:S(2)}, u32[]{:S(2)}) collective-permute-start(bf16[4,4,8,512]{3,2,1,0:T(8,128)(2,1)S(1)} %get-tuple-element.36.refs_4_), channel_id=1, source_target_pairs={{0,8},{8,16},{16,24},{24,0},{1,9},{9,17},{17,25},{25,1},{2,10},{10... | collective-permute-start | bytes 393224 | tf_op jit(solution)/shard_map/ppermute | solution.py:29
  126.0 21.9 %collective-permute-start.14 = (bf16[4,4,8,512]{3,2,1,0:T(8,128)(2,1)S(1)}, bf16[4,4,8,512]{3,2,1,0:T(8,128)(2,1)S(1)}, u32[]{:S(2)}, u32[]{:S(2)}) collective-permute-start(bf16[4,4,8,512]{3,2,1,0:T(8,128)(2,1)S(1)} %get-tuple-element.36.refs_4_), channel_id=1, source_target_pairs={{0,16},{8,24},{16,0},{24,8},{1,17},{9,25},{17,1},{25,9},{2,18},{10... | collective-permute-start | bytes 393224 | tf_op jit(solution)/shard_map/ppermute | solution.py:29
  128.1 19.9 %collective-permute-start.15 = (bf16[4,4,8,512]{3,2,1,0:T(8,128)(2,1)S(1)}, bf16[4,4,8,512]{3,2,1,0:T(8,128)(2,1)S(1)}, u32[]{:S(2)}, u32[]{:S(2)}) collective-permute-start(bf16[4,4,8,512]{3,2,1,0:T(8,128)(2,1)S(1)} %get-tuple-element.36.refs_4_), channel_id=1, source_target_pairs={{0,24},{8,0},{16,8},{24,16},{1,25},{9,1},{17,9},{25,17},{2,26},{10... | collective-permute-start | bytes 393224 | tf_op jit(solution)/shard_map/ppermute | solution.py:29
  129.0 19.0 %all-to-all-start.6 = ((f32[32,8,128]{2,1,0:T(8,128)}), f32[32,8,128]{2,1,0:T(8,128)S(1)}, u32[]{:S(2)}, u32[]{:S(2)}) async-start(f32[32,8,128]{2,1,0:T(8,128)} %get-tuple-element.33), calls=%async_computation.6 | async-start | bytes 262144 | tf_op jit(solution)/shard_map/all_to_all | solution.py:18
  140.0 13.4 %collective-permute-start.1 = (bf16[8,8,512]{2,1,0:T(8,128)(2,1)S(1)}, bf16[8,8,512]{2,1,0:T(8,128)(2,1)S(1)}, u32[]{:S(2)}, u32[]{:S(2)}) collective-permute-start(bf16[8,8,512]{2,1,0:T(8,128)(2,1)S(1)} %get-tuple-element.47), channel_id=1, source_target_pairs={{0,1},{1,2},{2,3},{3,0},{4,5},{5,6},{6,7},{7,4},{8,9},{9,10},{10,1... | collective-permute-start | bytes 196616 | tf_op jit(solution)/shard_map/ppermute | solution.py:29
  141.4 12.0 %collective-permute-start.2 = (bf16[8,8,512]{2,1,0:T(8,128)(2,1)S(1)}, bf16[8,8,512]{2,1,0:T(8,128)(2,1)S(1)}, u32[]{:S(2)}, u32[]{:S(2)}) collective-permute-start(bf16[8,8,512]{2,1,0:T(8,128)(2,1)S(1)} %get-tuple-element.47), channel_id=1, source_target_pairs={{0,2},{1,3},{2,0},{3,1},{4,6},{5,7},{6,4},{7,5},{8,10},{9,11},{10,... | collective-permute-start | bytes 196616 | tf_op jit(solution)/shard_map/ppermute | solution.py:29
  143.8 9.6 %collective-permute-start.3 = (bf16[8,8,512]{2,1,0:T(8,128)(2,1)S(1)}, bf16[8,8,512]{2,1,0:T(8,128)(2,1)S(1)}, u32[]{:S(2)}, u32[]{:S(2)}) collective-permute-start(bf16[8,8,512]{2,1,0:T(8,128)(2,1)S(1)} %get-tuple-element.47), channel_id=1, source_target_pairs={{0,3},{1,0},{2,1},{3,2},{4,7},{5,4},{6,5},{7,6},{8,11},{9,8},{10,9... | collective-permute-start | bytes 196616 | tf_op jit(solution)/shard_map/ppermute | solution.py:29
  149.9 32.6 %all-to-all-start.7 = ((bf16[4,4,4,2,8,512]{5,4,3,2,1,0:T(8,128)(2,1)}), bf16[4,4,4,2,8,512]{5,4,3,2,1,0:T(8,128)(2,1)S(1)}, u32[]{:S(2)}, u32[]{:S(2)}) async-start(bf16[4,4,4,2,8,512]{5,4,3,2,1,0:T(8,128)(2,1)} %broadcast_in_dim.15), calls=%async_computation.7 | async-start | bytes 2097152 | tf_op jit(solution)/shard_map/all_to_all | solution.py:18
  153.5 20.1 %collective-permute-start.4 = (bf16[32,8,512]{2,1,0:T(8,128)(2,1)S(1)}, bf16[32,8,512]{2,1,0:T(8,128)(2,1)S(1)}, u32[]{:S(2)}, u32[]{:S(2)}) collective-permute-start(bf16[32,8,512]{2,1,0:T(8,128)(2,1)S(1)} %pad_maximum_fusion.2), channel_id=1, source_target_pairs={{0,8},{8,16},{16,24},{24,0},{1,9},{9,17},{17,25},{25,1},{2,10},{10... | collective-permute-start | bytes 786440 | tf_op jit(solution)/shard_map/ppermute | solution.py:29
  154.9 24.6 %collective-permute-start.5 = (bf16[32,8,512]{2,1,0:T(8,128)(2,1)S(1)}, bf16[32,8,512]{2,1,0:T(8,128)(2,1)S(1)}, u32[]{:S(2)}, u32[]{:S(2)}) collective-permute-start(bf16[32,8,512]{2,1,0:T(8,128)(2,1)S(1)} %pad_maximum_fusion.2), channel_id=1, source_target_pairs={{0,16},{8,24},{16,0},{24,8},{1,17},{9,25},{17,1},{25,9},{2,18},{10... | collective-permute-start | bytes 786440 | tf_op jit(solution)/shard_map/ppermute | solution.py:29
  157.3 22.2 %collective-permute-start.6 = (bf16[32,8,512]{2,1,0:T(8,128)(2,1)S(1)}, bf16[32,8,512]{2,1,0:T(8,128)(2,1)S(1)}, u32[]{:S(2)}, u32[]{:S(2)}) collective-permute-start(bf16[32,8,512]{2,1,0:T(8,128)(2,1)S(1)} %pad_maximum_fusion.2), channel_id=1, source_target_pairs={{0,24},{8,0},{16,8},{24,16},{1,25},{9,1},{17,9},{25,17},{2,26},{10... | collective-permute-start | bytes 786440 | tf_op jit(solution)/shard_map/ppermute | solution.py:29
  158.5 23.3 %collective-permute-start.17 = (bf16[4,4,2,8,512]{4,3,2,1,0:T(8,128)(2,1)S(1)}, bf16[4,4,2,8,512]{4,3,2,1,0:T(8,128)(2,1)S(1)}, u32[]{:S(2)}, u32[]{:S(2)}) collective-permute-start(bf16[4,4,2,8,512]{4,3,2,1,0:T(8,128)(2,1)S(1)} %get-tuple-element.42), channel_id=1, source_target_pairs={{0,1},{1,2},{2,3},{3,0},{4,5},{5,6},{6,7},{7,4},{8,9},{9,10},{10,1... | collective-permute-start | bytes 786440 | tf_op jit(solution)/shard_map/ppermute | solution.py:29
  158.5 23.3 %collective-permute-start.18 = (bf16[4,4,2,8,512]{4,3,2,1,0:T(8,128)(2,1)S(1)}, bf16[4,4,2,8,512]{4,3,2,1,0:T(8,128)(2,1)S(1)}, u32[]{:S(2)}, u32[]{:S(2)}) collective-permute-start(bf16[4,4,2,8,512]{4,3,2,1,0:T(8,128)(2,1)S(1)} %get-tuple-element.42), channel_id=1, source_target_pairs={{0,2},{1,3},{2,0},{3,1},{4,6},{5,7},{6,4},{7,5},{8,10},{9,11},{10,... | collective-permute-start | bytes 786440 | tf_op jit(solution)/shard_map/ppermute | solution.py:29
  173.6 8.2 %collective-permute-start.19 = (bf16[4,4,2,8,512]{4,3,2,1,0:T(8,128)(2,1)S(1)}, bf16[4,4,2,8,512]{4,3,2,1,0:T(8,128)(2,1)S(1)}, u32[]{:S(2)}, u32[]{:S(2)}) collective-permute-start(bf16[4,4,2,8,512]{4,3,2,1,0:T(8,128)(2,1)S(1)} %get-tuple-element.42), channel_id=1, source_target_pairs={{0,3},{1,0},{2,1},{3,2},{4,7},{5,4},{6,5},{7,6},{8,11},{9,8},{10,9... | collective-permute-start | bytes 786440 | tf_op jit(solution)/shard_map/ppermute | solution.py:29
  180.6 3.8 %collective-permute-start.7 = (bf16[16,8,8,512]{3,2,1,0:T(8,128)(2,1)}, bf16[16,8,8,512]{3,2,1,0:T(8,128)(2,1)}, u32[]{:S(2)}, u32[]{:S(2)}) collective-permute-start(bf16[16,8,8,512]{3,2,1,0:T(8,128)(2,1)} %bitcast.5.mine_ref), channel_id=1, source_target_pairs={{0,4},{4,0},{1,5},{5,1},{2,6},{6,2},{3,7},{7,3},{8,12},{12,8},{9,1... | collective-permute-start | bytes 3145736 | tf_op jit(solution)/shard_map/ppermute | solution.py:38
  181.9 10.4 %collective-permute-start.20 = (bf16[4,4,4,2,8,512]{5,4,3,2,1,0:T(8,128)(2,1)S(1)}, bf16[4,4,4,2,8,512]{5,4,3,2,1,0:T(8,128)(2,1)S(1)}, u32[]{:S(2)}, u32[]{:S(2)}) collective-permute-start(bf16[4,4,4,2,8,512]{5,4,3,2,1,0:T(8,128)(2,1)S(1)} %pad_maximum_fusion.1.refs_1_), channel_id=1, source_target_pairs={{0,4},{4,0},{1,5},{5,1},{2,6},{6,2},{3,7},{7,3},{8,12},{12,8},{9,1... | collective-permute-start | bytes 3145736 | tf_op jit(solution)/shard_map/ppermute | solution.py:38
  182.5 9.8 %collective-permute-start.16 = (bf16[4,4,4,2,8,512]{5,4,3,2,1,0:T(8,128)(2,1)S(1)}, bf16[4,4,4,2,8,512]{5,4,3,2,1,0:T(8,128)(2,1)S(1)}, u32[]{:S(2)}, u32[]{:S(2)}) collective-permute-start(bf16[4,4,4,2,8,512]{5,4,3,2,1,0:T(8,128)(2,1)S(1)} %all-to-all-done.7.refs_0_), channel_id=1, source_target_pairs={{0,4},{4,0},{1,5},{5,1},{2,6},{6,2},{3,7},{7,3},{8,12},{12,8},{9,1... | collective-permute-start | bytes 3145736 | tf_op jit(solution)/shard_map/ppermute | solution.py:38
  184.4 5.5 %copy-start.6 = (s32[3]{0:T(128)S(1)}, s32[3]{0:T(128)}, u32[]{:S(2)}) copy-start(s32[3]{0:T(128)} %copy-done.5) | copy-start | bytes 40
